TPU v7x, 16 devices: a 4x2x1 block of a 4x4x8 slice. The times are simulated.
16 devices in a mesh: dp: 2 (over y, z), w: 8 (over x, core).
Axes of the slice: x: 4, y: 2, z: 1, core: 2. Of those that a mesh axis runs over, the one named last changes fastest.
The devices are a block of a 4x4x8 slice.
Arguments:
- hidden: bfloat16 [2048, 1152], P(('dp', 'w')), parts along dimension 0
- positions: int32 [2048], P(('dp', 'w')), parts along dimension 0
- k_cache: bfloat16 [2, 2048, 1, 128, 256], P(None, ('dp', 'w')), parts along dimension 1
- v_cache: bfloat16 [2, 2048, 1, 128, 256], P(None, ('dp', 'w')), parts along dimension 1
- attn_norm: float32 [2, 1152], P(None, 'w')
- w_query: bfloat16 [2, 1152, 1024], P(None, 'w')
- w_key: bfloat16 [2, 1152, 256], P(None, 'w')
- w_value: bfloat16 [2, 1152, 256], P(None, 'w')
- w_out: bfloat16 [2, 1024, 1152], P(None, 'w')
- mlp_norm: float32 [2, 1152], P(None, 'w')
- w_gate: bfloat16 [2, 1152, 6912], P(None, 'w')
- w_up: bfloat16 [2, 1152, 6912], P(None, 'w')
- w_down: bfloat16 [2, 6912, 1152], P(None, 'w')
Outputs:
- output 1: bfloat16 [2048, 1152], P(('dp', 'w')), parts along dimension 0
- output 2: bfloat16 [2, 2048, 1, 128, 256], P(None, ('dp', 'w')), parts along dimension 1
- output 3: bfloat16 [2, 2048, 1, 128, 256], P(None, ('dp', 'w')), parts along dimension 1
There are 2 independent parts. A program takes and returns all parts, laid end to end along the dimension named above; an argument that names none is the same for every part.
All inputs are finite; a program needn't handle non-finite values.
Results may differ from a plain program's by a relative error of at most 0.0169962.
Values are sent between devices in bfloat16 or wider.
A program may use at most 768 MiB of HBM per device.

v0:
```python
import jax
import jax.numpy as jnp
from jax import lax
from jax.sharding import PartitionSpec as P

EPS = 1e-6
ROPE_BASE = 10000.0


def rms_norm(hidden, gain):
    hid_f32 = hidden.astype(jnp.float32)
    mean_sq = jnp.mean(hid_f32 * hid_f32, axis=-1, keepdims=True)
    return (hid_f32 * lax.rsqrt(mean_sq + EPS) * (1.0 + gain)).astype(jnp.bfloat16)


def rope_tables(positions, head_dim):
    half_dim = head_dim // 2
    inv_freq = ROPE_BASE ** (-2.0 * jnp.arange(half_dim, dtype=jnp.float32) / head_dim)
    angles = positions.astype(jnp.float32)[:, None] * inv_freq[None, :]
    return jnp.cos(angles), jnp.sin(angles)


def apply_rope(vectors, cos_tab, sin_tab):
    half_dim = vectors.shape[-1] // 2
    lead_half = vectors[..., :half_dim]
    tail_half = vectors[..., half_dim:]
    cos_b = cos_tab[:, None, :]
    sin_b = sin_tab[:, None, :]
    return jnp.concatenate([lead_half * cos_b - tail_half * sin_b, tail_half * cos_b + lead_half * sin_b], axis=-1)


def attention_core(q_proj, k_proj, v_proj, positions, cos_tab, sin_tab, k_layer, v_layer):
    batch_rows, kv_heads, cache_len, head_dim = k_layer.shape
    num_heads = q_proj.shape[-1] // head_dim
    q_rot = apply_rope(q_proj.reshape(batch_rows, num_heads, head_dim), cos_tab, sin_tab)
    q_rot = (q_rot * head_dim ** -0.5).astype(jnp.bfloat16).reshape(batch_rows, kv_heads, num_heads // kv_heads, head_dim)
    k_rot = apply_rope(k_proj.reshape(batch_rows, kv_heads, head_dim), cos_tab, sin_tab).astype(jnp.bfloat16)
    v_new = v_proj.reshape(batch_rows, kv_heads, head_dim).astype(jnp.bfloat16)
    cache_steps = jnp.arange(cache_len)
    write_mask = (cache_steps[None, :] == positions[:, None])[:, None, :, None]
    k_layer = jnp.where(write_mask, k_rot[:, :, None, :], k_layer)
    v_layer = jnp.where(write_mask, v_new[:, :, None, :], v_layer)
    scores = jnp.einsum("bkge,bkse->bkgs", q_rot, k_layer, preferred_element_type=jnp.float32)
    is_valid = cache_steps[None, None, None, :] <= positions[:, None, None, None]
    scores = jnp.where(is_valid, scores, -1e30)
    row_max = jnp.max(scores, axis=-1, keepdims=True)
    attn_prob = jnp.exp(scores - row_max)
    row_sum = jnp.sum(attn_prob, axis=-1, keepdims=True)
    attn_vals = jnp.einsum("bkgs,bkse->bkge", attn_prob.astype(jnp.bfloat16), v_layer, preferred_element_type=jnp.float32)
    attn_vals = (attn_vals / row_sum).astype(jnp.bfloat16).reshape(batch_rows, num_heads * head_dim)
    return attn_vals, k_layer, v_layer


def gather_rows(row_shard):
    return lax.all_gather(row_shard, "w", axis=0, tiled=True)


def solution(mesh):
    batch_spec = P(("dp", "w"))
    cache_spec = P(None, ("dp", "w"))
    gain_spec = P(None, "w")
    weight_spec = P(None, "w", None)

    def per_device(hidden, positions, k_cache, v_cache, attn_norm, w_query, w_key, w_value, w_out, mlp_norm, w_gate, w_up, w_down):
        cos_tab, sin_tab = rope_tables(positions, k_cache.shape[-1])
        k_layers = []
        v_layers = []
        for layer_idx in range(k_cache.shape[0]):
            normed = rms_norm(hidden, gather_rows(attn_norm[layer_idx]))
            q_proj = jnp.dot(normed, gather_rows(w_query[layer_idx]), preferred_element_type=jnp.float32)
            k_proj = jnp.dot(normed, gather_rows(w_key[layer_idx]), preferred_element_type=jnp.float32)
            v_proj = jnp.dot(normed, gather_rows(w_value[layer_idx]), preferred_element_type=jnp.float32)
            attn_vals, k_layer, v_layer = attention_core(q_proj, k_proj, v_proj, positions, cos_tab, sin_tab, k_cache[layer_idx], v_cache[layer_idx])
            hid_mid = (hidden.astype(jnp.float32) + jnp.dot(attn_vals, gather_rows(w_out[layer_idx]), preferred_element_type=jnp.float32)).astype(jnp.bfloat16)
            normed_mlp = rms_norm(hid_mid, gather_rows(mlp_norm[layer_idx]))
            gate_pre = jnp.dot(normed_mlp, gather_rows(w_gate[layer_idx]), preferred_element_type=jnp.float32)
            up_pre = jnp.dot(normed_mlp, gather_rows(w_up[layer_idx]), preferred_element_type=jnp.float32)
            mlp_hidden = (jax.nn.gelu(gate_pre, approximate=True) * up_pre).astype(jnp.bfloat16)
            hidden = (hid_mid.astype(jnp.float32) + jnp.dot(mlp_hidden, gather_rows(w_down[layer_idx]), preferred_element_type=jnp.float32)).astype(jnp.bfloat16)
            k_layers.append(k_layer)
            v_layers.append(v_layer)
        return hidden, jnp.stack(k_layers), jnp.stack(v_layers)

    in_specs = (batch_spec, batch_spec, cache_spec, cache_spec, gain_spec, weight_spec, weight_spec, weight_spec, weight_spec, gain_spec, weight_spec, weight_spec, weight_spec)
    out_specs = (batch_spec, cache_spec, cache_spec)
    return jax.shard_map(per_device, mesh=mesh, in_specs=in_specs, out_specs=out_specs, check_vma=False)
```

profile of v0, /device:TPU:112, one launch (start us, length us, event | category | flops | bytes accessed | tf_op | source)
XLA Modules:
  0.0 616.5 jit_solution(17820078877957601256)
XLA Ops:
  7.2 1.9 fusion.157
  9.3 1.9 fusion.156
  11.3 4.3 fusion.154
  15.8 4.4 fusion.155
  20.4 4.4 fusion.153
  25.0 0.6 all-gather.39.cloned.1.call-update
  25.6 0.7 all-gather.41.cloned.1.call-update
  26.4 0.7 all-gather.43.cloned.1.call-update
  27.2 0.7 all-gather.47.cloned.1.call-update
  28.0 0.6 all-gather.45.cloned.1.call-update
  28.6 0.6 dynamic-slice
  29.9 0.3 dynamic-update-slice
  31.0 27.3 %all-reduce.4 = (f32[1152]{0:T(1024)S(1)}, f32[1152]{0:T(1024)S(1)}, f32[1152]{0:T(1024)S(1)}, f32[1152]{0:T(1024)S(1)}) all-reduce(f32[1152]{0:T(1024)S(1)} %dynamic-update-slice, f32[1152]{0:T(1024)S(1)} %dynamic-update-slice.1, f32[1152]{0:T(1024)S(1)} %dynamic-update-slice.2, ...), channel_id=2, replica_groups=mesh['dp'=2,'w'=8] {'w'}, use_global_device_ids=true, to_apply=%add | all-reduce | flops 4608 | bytes 36864
  58.4 22.6 %all-gather.2 = bf16[1,1152,256]{2,1,0:T(8,128)(2,1)S(1)} all-gather(bf16[1,144,256]{2,1,0:T(8,128)(2,1)S(1)} %get-tuple-element.27), channel_id=4, replica_groups=mesh['dp'=2,'w'=8] {'w'}, dimensions={1}, use_global_device_ids=true | all-gather | bytes 663552 | tf_op jit(solution)/shard_map/all_gather | solution.py:55
  81.2 0.3 convolution_bitcast_fusion.1
  81.5 0.3 fusion.145
  81.8 26.8 %all-gather.3 = bf16[1,1152,256]{2,1,0:T(8,128)(2,1)S(1)} all-gather(bf16[1,144,256]{2,1,0:T(8,128)(2,1)S(1)} %get-tuple-element.29), channel_id=5, replica_groups=mesh['dp'=2,'w'=8] {'w'}, dimensions={1}, use_global_device_ids=true | all-gather | bytes 663552 | tf_op jit(solution)/shard_map/all_gather | solution.py:55
  108.6 23.6 %all-gather.12 = bf16[1,1152,256]{2,1,0:T(8,128)(2,1)S(1)} all-gather(bf16[1,144,256]{2,1,0:T(8,128)(2,1)S(1)} %get-tuple-element.28), channel_id=14, replica_groups=mesh['dp'=2,'w'=8] {'w'}, dimensions={1}, use_global_device_ids=true | all-gather | bytes 663552 | tf_op jit(solution)/shard_map/all_gather | solution.py:55
  132.2 24.6 %all-gather.11 = bf16[1,1152,256]{2,1,0:T(8,128)(2,1)S(1)} all-gather(bf16[1,144,256]{2,1,0:T(8,128)(2,1)S(1)} %get-tuple-element.26), channel_id=13, replica_groups=mesh['dp'=2,'w'=8] {'w'}, dimensions={1}, use_global_device_ids=true | all-gather | bytes 663552 | tf_op jit(solution)/shard_map/all_gather | solution.py:55
  156.9 0.3 multiply_cosine_fusion.1
  157.2 0.3 convolution_convert_fusion.1
  157.6 2.2 fusion.81
  160.2 6.8 %fusion.162 = (f32[128,4]{1,0:T(8,128)S(1)}, f32[128,4,128]{2,1,0:T(4,128)S(1)}) fusion(pred[128,128]{1,0:T(8,128)(4,1)S(1)} %get-tuple-element.42, bf16[2,128,1,128,256]{4,3,1,2,0:T(8,128)(2,1)} %bitcast.139, bf16[128,256]{1,0:T(8,128)(2,1)S(1)} %pad_maximum_fusion.1, f32[128,4,128]{2,1,0:T(4,128)S(1)} %get-tuple-element.21, ...), kind=kOutput, calls=%fused_computation.176 | convolution fusion | flops 38272512 | bytes 9275392 | tf_op jit(solution)/shard_map/bkge,bkse->bkgs/dot_general | solution.py:43
  167.1 0.4 fusion.118
  167.5 1.0 slice-done.3
  168.5 5.4 fusion.86
  173.9 2.3 multiply_reduce_fusion.2
  176.2 10.2 %fusion.46 = f32[128,6912]{1,0:T(8,128)} fusion(bf16[1,1152,6912]{2,1,0:T(8,128)(2,1)} %all-gather.33.cloned.1.call-done, f32[128,1152]{1,0:T(8,128)S(1)} %get-tuple-element.46, f32[1152]{0:T(1024)S(1)} %broadcast_add_fusion.2, f32[128]{0:T(128)S(1)} %add_rsqrt_fusion.2), kind=kOutput, calls=%fused_computation.50 | convolution fusion | flops 2045952000 | bytes 20059136 | tf_op jit(solution)/shard_map/dot_general | solution.py:76
  186.4 41.5 %all-gather.37.cloned.1.call-done = bf16[1,6912,1152]{2,1,0:T(8,128)(2,1)} async-done(((bf16[1,864,1152]{2,1,0:T(8,128)(2,1)}), bf16[1,6912,1152]{2,1,0:T(8,128)(2,1)}) %all-gather.37.cloned.1.call-update) | async-done | bytes 15925264 | tf_op jit(solution)/shard_map/all_gather | solution.py:55
  227.9 79.4 %all-gather.35.cloned.1.call-done = bf16[1,1152,6912]{2,1,0:T(8,128)(2,1)} async-done(((bf16[1,144,6912]{2,1,0:T(8,128)(2,1)}), bf16[1,1152,6912]{2,1,0:T(8,128)(2,1)}) %all-gather.35.cloned.1.call-update) | async-done | bytes 15925264 | tf_op jit(solution)/shard_map/all_gather | solution.py:55
  307.3 16.0 %multiply_reduce_fusion.1 = (f32[128]{0:T(128)S(1)}, f32[128,1152]{1,0:T(8,128)S(1)}) fusion(f32[128,1152]{1,0:T(8,128)S(1)} %get-tuple-element.46, bf16[1,6912,1152]{2,1,0:T(8,128)(2,1)} %all-gather.37.cloned.1.call-done, f32[128,6912]{1,0:T(8,128)} %fusion.46, bf16[1,1152,6912]{2,1,0:T(8,128)(2,1)} %all-gather.35.cloned.1.call-done, ...), kind=kOutput, calls=%fused_computation.97 | convolution fusion | flops 4079812608 | bytes 36574720 | tf_op jit(solution)/shard_map/dot_general | solution.py:79
  323.5 8.0 %all-gather.39.cloned.1.call-done = bf16[1,1152,1024]{2,1,0:T(8,128)(2,1)} async-done(((bf16[1,144,1024]{2,1,0:T(8,128)(2,1)}), bf16[1,1152,1024]{2,1,0:T(8,128)(2,1)}) %all-gather.39.cloned.1.call-update) | async-done | bytes 2359312 | tf_op jit(solution)/shard_map/all_gather | solution.py:55
  331.5 2.2 fusion.78
  334.2 0.3 fusion.143
  334.8 6.9 %fusion.165 = (f32[128,4]{1,0:T(8,128)S(1)}, f32[128,4,128]{2,1,0:T(4,128)S(1)}) fusion(pred[128,128]{1,0:T(8,128)(4,1)S(1)} %get-tuple-element.42, bf16[2,128,1,128,256]{4,3,1,2,0:T(8,128)(2,1)} %bitcast.140, bf16[128,256]{1,0:T(8,128)(2,1)S(1)} %pad_maximum_fusion.2, f32[128,4,128]{2,1,0:T(4,128)S(1)} %get-tuple-element.19, ...), kind=kOutput, calls=%fused_computation.177 | convolution fusion | flops 38272512 | bytes 9275392 | tf_op jit(solution)/shard_map/bkge,bkse->bkgs/dot_general | solution.py:43
  341.6 0.4 fusion.120
  342.5 5.4 fusion.88
  348.0 7.2 %all-gather.41.cloned.1.call-done = bf16[1,1024,1152]{2,1,0:T(8,128)(2,1)} async-done(((bf16[1,128,1152]{2,1,0:T(8,128)(2,1)}), bf16[1,1024,1152]{2,1,0:T(8,128)(2,1)}) %all-gather.41.cloned.1.call-update) | async-done | bytes 2359312 | tf_op jit(solution)/shard_map/all_gather | solution.py:55
  355.2 3.0 multiply_reduce_fusion
  358.2 8.7 %broadcast_select_fusion.1 = (bf16[1,128,1,128,256]{4,3,1,2,0:T(8,128)(2,1)S(1)}, bf16[1,128,1,128,256]{4,3,1,2,0:T(8,128)(2,1)S(1)}, bf16[1,128,1,128,256]{4,3,2,1,0:T(8,128)(2,1)S(1)}) fusion(pred[128,128]{1,0:T(8,128)(4,1)S(1)} %get-tuple-element.42, bf16[2,128,1,128,256]{4,3,1,2,0:T(8,128)(2,1)} %bitcast.141, bf16[128,256]{1,0:T(8,128)(2,1)S(1)} %pad_maximum_fusion.1, ...), kind=kLoop, calls=%fused_computation.29 | loop fusion | flops 12582912 | bytes 50544640 | tf_op jit(solution)/shard_map/jit(_where)/select_n | solution.py:41
  366.9 6.8 %maximum_bitcast_fusion = bf16[2,128,1,128,256]{4,3,2,1,0:T(8,128)(2,1)} fusion(bf16[1,128,1,128,256]{4,3,1,2,0:T(8,128)(2,1)S(1)} %get-tuple-element.11, bf16[1,128,1,128,256]{4,3,1,2,0:T(8,128)(2,1)S(1)} %get-tuple-element.10), kind=kLoop, calls=%fused_computation | loop fusion | flops 8388608 | bytes 33554432
  373.7 5.3 bitcast_select_fusion
  379.0 6.8 %pad_maximum_fusion = bf16[2,128,1,128,256]{4,3,2,1,0:T(8,128)(2,1)} fusion(bf16[1,128,1,128,256]{4,3,2,1,0:T(8,128)(2,1)S(1)} %bitcast_select_fusion, bf16[1,128,1,128,256]{4,3,2,1,0:T(8,128)(2,1)S(1)} %get-tuple-element.34), kind=kLoop, calls=%fused_computation.1 | loop fusion | flops 8388608 | bytes 33554432 | tf_op jit(solution)/shard_map/stack | solution.py:82
  385.7 49.0 %all-gather.43.cloned.1.call-done = bf16[1,1152,6912]{2,1,0:T(8,128)(2,1)} async-done(((bf16[1,144,6912]{2,1,0:T(8,128)(2,1)}), bf16[1,1152,6912]{2,1,0:T(8,128)(2,1)}) %all-gather.43.cloned.1.call-update) | async-done | bytes 15925264 | tf_op jit(solution)/shard_map/all_gather | solution.py:55
  434.7 7.4 %fusion.55 = f32[128,6912]{1,0:T(8,128)S(1)} fusion(bf16[1,1152,6912]{2,1,0:T(8,128)(2,1)} %all-gather.43.cloned.1.call-done, f32[128,1152]{1,0:T(8,128)} %get-tuple-element.52, f32[1152]{0:T(1024)S(1)} %broadcast_add_fusion, f32[128]{0:T(128)S(1)} %add_rsqrt_fusion), kind=kOutput, calls=%fused_computation.57 | convolution fusion | flops 2045952000 | bytes 20059136 | tf_op jit(solution)/shard_map/dot_general | solution.py:76
  442.0 72.3 %all-gather.47.cloned.1.call-done = bf16[1,6912,1152]{2,1,0:T(8,128)(2,1)} async-done(((bf16[1,864,1152]{2,1,0:T(8,128)(2,1)}), bf16[1,6912,1152]{2,1,0:T(8,128)(2,1)}) %all-gather.47.cloned.1.call-update) | async-done | bytes 15925264 | tf_op jit(solution)/shard_map/all_gather | solution.py:55
  514.3 79.4 %all-gather.45.cloned.1.call-done = bf16[1,1152,6912]{2,1,0:T(8,128)(2,1)} async-done(((bf16[1,144,6912]{2,1,0:T(8,128)(2,1)}), bf16[1,1152,6912]{2,1,0:T(8,128)(2,1)}) %all-gather.45.cloned.1.call-update) | async-done | bytes 15925264 | tf_op jit(solution)/shard_map/all_gather | solution.py:55
  593.7 15.9 %fusion.64 = bf16[128,1152]{1,0:T(8,128)(2,1)} fusion(f32[128,1152]{1,0:T(8,128)} %get-tuple-element.52, bf16[1,6912,1152]{2,1,0:T(8,128)(2,1)} %all-gather.47.cloned.1.call-done, f32[128,6912]{1,0:T(8,128)S(1)} %fusion.55, bf16[1,1152,6912]{2,1,0:T(8,128)(2,1)} %all-gather.45.cloned.1.call-done, f32[1152]{0:T(1024)S(1)} %broadcast_add_fusion, ...), kind=kOutput, calls=%fused_computation.62 | convolution fusion | flops 4079370240 | bytes 36279296 | tf_op jit(solution)/shard_map/dot_general | solution.py:79
  (83 shorter events, 3.9 us)
Async XLA Ops:
  7.2 150.4 %all-gather.29.cloned.1.call-start = ((), (), s32[]{:S(2)}) async-start(), calls=%async_computation | async-start | bytes 2654208 | tf_op jit(solution)/shard_map/all_gather | solution.py:55
  9.2 164.7 %all-gather.31.cloned.1.call-start = ((), (), s32[]{:S(2)}) async-start(), calls=%async_computation.1 | async-start | bytes 2654208 | tf_op jit(solution)/shard_map/all_gather | solution.py:55
  11.3 164.9 %all-gather.33.cloned.1.call-start = ((), (), s32[]{:S(2)}) async-start(), calls=%async_computation.2 | async-start | bytes 17915904 | tf_op jit(solution)/shard_map/all_gather | solution.py:55
  15.7 212.1 %all-gather.37.cloned.1.call-start = ((), (), s32[]{:S(2)}) async-start(), calls=%async_computation.4 | async-start | bytes 17915904 | tf_op jit(solution)/shard_map/all_gather | solution.py:55
  20.3 8.3 %copy-start.5 = (s32[128]{0:T(128)S(1)}, s32[128]{0:T(128)}, u32[]{:S(2)}) copy-start(s32[128]{0:T(128)} %param.14) | copy-start | bytes 1540
  20.3 8.4 %copy-start.6 = (u32[16]{0:T(128)S(1)}, u32[16]{0:T(128)}, u32[]{:S(2)}) copy-start(u32[16]{0:T(128)} %constant.34) | copy-start | bytes 196
  20.3 9.6 %copy-start.3 = (f32[2,144]{1,0:T(2,128)S(1)}, f32[2,144]{1,0:T(2,128)}, u32[]{:S(2)}) copy-start(f32[2,144]{1,0:T(2,128)} %param.17) | copy-start | bytes 3460
  20.3 9.9 %copy-start.4 = (f32[2,144]{1,0:T(2,128)S(1)}, f32[2,144]{1,0:T(2,128)}, u32[]{:S(2)}) copy-start(f32[2,144]{1,0:T(2,128)} %param.22) | copy-start | bytes 3460
  20.3 38.0 %copy-start.1 = (bf16[2,144,256]{2,1,0:T(8,128)(2,1)S(1)}, bf16[2,144,256]{2,1,0:T(8,128)(2,1)}, u32[]{:S(2)}) copy-start(bf16[2,144,256]{2,1,0:T(8,128)(2,1)} %param.19) | copy-start | bytes 442372
  20.3 60.7 %copy-start = (bf16[128,1152]{1,0:T(8,128)(2,1)S(1)}, bf16[128,1152]{1,0:T(8,128)(2,1)}, u32[]{:S(2)}) copy-start(bf16[128,1152]{1,0:T(8,128)(2,1)} %param.13) | copy-start | bytes 884740
  20.3 61.5 %copy-start.2 = (bf16[2,144,256]{2,1,0:T(8,128)(2,1)S(1)}, bf16[2,144,256]{2,1,0:T(8,128)(2,1)}, u32[]{:S(2)}) copy-start(bf16[2,144,256]{2,1,0:T(8,128)(2,1)} %param.20) | copy-start | bytes 442372
  20.4 286.9 %all-gather.35.cloned.1.call-start = ((), (), s32[]{:S(2)}) async-start(), calls=%async_computation.3 | async-start | bytes 17915904 | tf_op jit(solution)/shard_map/all_gather | solution.py:55
  24.9 306.6 %all-gather.39.cloned.1.call-start = ((), (), s32[]{:S(2)}) async-start(), calls=%async_computation.5 | async-start | bytes 2654208 | tf_op jit(solution)/shard_map/all_gather | solution.py:55
  25.5 329.7 %all-gather.41.cloned.1.call-start = ((), (), s32[]{:S(2)}) async-start(), calls=%async_computation.6 | async-start | bytes 2654208 | tf_op jit(solution)/shard_map/all_gather | solution.py:55
  26.3 408.3 %all-gather.43.cloned.1.call-start = ((), (), s32[]{:S(2)}) async-start(), calls=%async_computation.7 | async-start | bytes 17915904 | tf_op jit(solution)/shard_map/all_gather | solution.py:55
  27.2 487.2 %all-gather.47.cloned.1.call-start = ((), (), s32[]{:S(2)}) async-start(), calls=%async_computation.9 | async-start | bytes 17915904 | tf_op jit(solution)/shard_map/all_gather | solution.py:55
  27.9 565.7 %all-gather.45.cloned.1.call-start = ((), (), s32[]{:S(2)}) async-start(), calls=%async_computation.8 | async-start | bytes 17915904 | tf_op jit(solution)/shard_map/all_gather | solution.py:55
  160.0 7.4 %slice-start = ((s8[16777216]{0:T(1024)(128)(4,1)}), s8[4194304]{0:T(1024)(128)(4,1)S(1)}, s32[]{:S(2)}) async-start(s8[16777216]{0:T(1024)(128)(4,1)} %bitcast.143), calls=%async_computation.10 | async-start | bytes 8388608
  160.2 7.3 %slice-start.1 = ((s8[16777216]{0:T(1024)(128)(4,1)}), s8[4194304]{0:T(1024)(128)(4,1)S(1)}, s32[]{:S(2)}) async-start(s8[16777216]{0:T(1024)(128)(4,1)} %bitcast.143), calls=%async_computation.11 | async-start | bytes 8388608
  160.2 7.3 %slice-start.2 = ((s8[16777216]{0:T(1024)(128)(4,1)}), s8[4194304]{0:T(1024)(128)(4,1)S(1)}, s32[]{:S(2)}) async-start(s8[16777216]{0:T(1024)(128)(4,1)} %bitcast.143), calls=%async_computation.12 | async-start | bytes 8388608
  160.2 8.2 %slice-start.3 = ((s8[16777216]{0:T(1024)(128)(4,1)}), s8[4194304]{0:T(1024)(128)(4,1)S(1)}, s32[]{:S(2)}) async-start(s8[16777216]{0:T(1024)(128)(4,1)} %bitcast.143), calls=%async_computation.13 | async-start | bytes 8388608
  333.9 8.3 %slice-start.4 = ((s8[16777216]{0:T(1024)(128)(4,1)}), s8[4194304]{0:T(1024)(128)(4,1)S(1)}, s32[]{:S(2)}) async-start(s8[16777216]{0:T(1024)(128)(4,1)} %bitcast.146), calls=%async_computation.14 | async-start | bytes 8388608
  334.7 7.5 %slice-start.5 = ((s8[16777216]{0:T(1024)(128)(4,1)}), s8[4194304]{0:T(1024)(128)(4,1)S(1)}, s32[]{:S(2)}) async-start(s8[16777216]{0:T(1024)(128)(4,1)} %bitcast.146), calls=%async_computation.15 | async-start | bytes 8388608
  334.7 7.5 %slice-start.6 = ((s8[16777216]{0:T(1024)(128)(4,1)}), s8[4194304]{0:T(1024)(128)(4,1)S(1)}, s32[]{:S(2)}) async-start(s8[16777216]{0:T(1024)(128)(4,1)} %bitcast.146), calls=%async_computation.16 | async-start | bytes 8388608
  334.7 7.8 %slice-start.7 = ((s8[16777216]{0:T(1024)(128)(4,1)}), s8[4194304]{0:T(1024)(128)(4,1)S(1)}, s32[]{:S(2)}) async-start(s8[16777216]{0:T(1024)(128)(4,1)} %bitcast.146), calls=%async_computation.17 | async-start | bytes 8388608
Sparse Core Ops, SparseCore 0:
  9.6 24.5 all-gather.28
  35.7 22.1 all-gather.30
  60.1 88.0 all-gather.32
  150.2 77.5 all-gather.36
  229.3 77.9 all-gather.34
  309.3 22.1 all-gather.38
  333.1 22.0 all-gather.40
  356.8 77.8 all-gather.42
  436.3 78.0 all-gather.46
  515.8 77.8 all-gather.44
where the time goes:
time: 617 us; the launch traced here: 616 us
  waiting for transfers between devices  340 us (55%)
  blocking collectives  125 us (20%)
  matrix products  84.7 us (14%)
  other arithmetic  29.9 us (5%)
  local copies, waits for them, and re-layouts  20.6 us (3%)
  between operations  15.3 us (2%)
    all_gather x10, waiting for transfers between devices, gather_rows(): return lax.all_gather(row_shard, 'w', axis=0, tiled=True)  337 us
    all_gather x4, blocking collectives, gather_rows(): return lax.all_gather(row_shard, 'w', axis=0, tiled=True)  97.5 us
    dot_general x2, matrix products, per_device(): jnp.dot(mlp_hidden, gather_rows(w_down[layer_idx]), preferred_element_typ...  32 us
    unnamed x1, blocking collectives  27.3 us
    dot_general x2, matrix products, per_device(): jnp.dot(normed_mlp, gather_rows(w_gate[layer_idx]), preferred_element_typ...  17.5 us
    dot_general x2, matrix products, attention_core(): jnp.einsum('bkge,bkse->bkgs', q_rot, k_layer, preferred_element_type=jnp....  13.7 us
  transfers between devices with their start and end apart: 10, of which 7 were waited for; matrix products, arithmetic and copies ran while one was open for 19% of the time, Pallas kernels for 0%

commit v1 on v0

v1 whole, which is shorter than its diff:
```python
import functools

import jax
import jax.numpy as jnp
from jax import lax
from jax.experimental import pallas as pl
from jax.experimental.pallas import tpu as pltpu
from jax.sharding import PartitionSpec as P

EPS = 1e-6
ROPE_BASE = 10000.0
LANES = 128
CORES = 2
CHIPS = 4
SEQ_GROUP = 32
MESH = pl.DeviceIdType.MESH
F32 = jnp.float32
BF16 = jnp.bfloat16


def rope_tables(positions, head_dim):
    half_dim = head_dim // 2
    inv_freq = ROPE_BASE ** (-2.0 * jnp.arange(half_dim, dtype=jnp.float32) / head_dim)
    angles = positions.astype(jnp.float32)[:, None] * inv_freq[None, :]
    return jnp.cos(angles), jnp.sin(angles)


def dot(a, b):
    return jnp.dot(a, b, preferred_element_type=F32)


def dot_t(a, b):
    return lax.dot_general(a, b, (((1,), (1,)), ((), ())), preferred_element_type=F32)


def decode_kernel(
    dims,
    hid_ref, cos_ref, sin_ref, gain_ref, pos_ref, kc_ref, vc_ref,
    wq_ref, wk_ref, wv_ref, wo_ref, wg_ref, wu_ref, wd_ref,
    out_ref, knew_ref, vnew_ref,
    gbuf, abuf_w, bbuf_w, gu_w, wd_w, tr_w, y_all, m_buf, part, r_t, r_f,
    kbuf, vbuf, qbuf, abuf, hbuf,
    send_sem, recv_sem, loc_sem, kv_sem,
):
    layers, rows, width, heads, head_dim, cache_len, n_dev, ff = dims
    half = head_dim // 2
    piece = width // n_dev
    chip_cols = ff // CHIPS
    win = gu_w.shape[-1]
    pad = win - chip_cols
    wd_rows = wd_ref.shape[1]
    q_half = wq_ref.shape[-1] // 2
    kv_half = head_dim // 2
    groups = rows // SEQ_GROUP
    w = lax.axis_index("w")
    dp = lax.axis_index("dp")
    x, c = lax.div(w, CORES), lax.rem(w, CORES)
    h = lax.rem(dp, 2)
    xr, xo, xl = lax.rem(x + 1, CHIPS), lax.rem(x + 2, CHIPS), lax.rem(x + 3, CHIPS)
    right, left = (dp, xr * CORES + c), (dp, xl * CORES + c)
    twin = (dp, x * CORES + 1 - c)
    pair = (dp + 1 - 2 * h, w)

    msg_ids = {}
    pending = []

    def mid(name):
        return msg_ids.setdefault(name, len(msg_ids))

    def put(name, pairs, dev):
        for src, dst in pairs:
            pltpu.make_async_remote_copy(src, dst, send_sem.at[mid(name)], recv_sem.at[mid(name)], device_id=dev, device_id_type=MESH).start()

    def send(name, pairs, dev, view=None):
        put(name, pairs, dev)
        pending.append((name, pairs[0][0] if view is None else view))

    def got(name, view):
        pltpu.make_async_remote_copy(view, view, send_sem.at[mid(name)], recv_sem.at[mid(name)], device_id=right, device_id_type=MESH).wait_recv()

    def sent(name, view):
        pltpu.make_async_remote_copy(view, view, send_sem.at[mid(name)], recv_sem.at[mid(name)], device_id=right, device_id_type=MESH).wait_send()

    def drain():
        for name, view in pending:
            sent(name, view)
        pending.clear()

    def col_start(xx):
        return pl.multiple_of(lax.div(chip_cols * xx, LANES) * LANES, LANES)

    def wd_at(layer, cc):
        offset = lax.rem(chip_cols * x, LANES) + wd_rows * cc
        return wd_w.at[layer, pl.ds(pl.multiple_of(offset, 32), wd_rows), :]

    def a_pairs(l):
        out = []
        for hf in range(2):
            dst = abuf_w.at[l, hf, x, c]
            out.append((wq_ref.at[l, :, pl.ds(hf * q_half, q_half)], dst.at[:, pl.ds(0, q_half)]))
            out.append((wk_ref.at[l, :, pl.ds(hf * kv_half, kv_half)], dst.at[:, pl.ds(q_half, kv_half)]))
            out.append((wv_ref.at[l, :, pl.ds(hf * kv_half, kv_half)], dst.at[:, pl.ds(q_half + kv_half, kv_half)]))
        return out

    def local_start(sem, pairs):
        for src, dst in pairs:
            pltpu.make_async_copy(src, dst, loc_sem.at[sem]).start()

    def local_wait(sem, view):
        pltpu.make_async_copy(view, view, loc_sem.at[sem]).wait()

    def kv_copies(i, slot):
        layer, group = lax.div(i, groups), lax.rem(i, groups)
        seqs = pl.ds(group * SEQ_GROUP, SEQ_GROUP)
        return (
            pltpu.make_async_copy(kc_ref.at[layer, seqs, 0], kbuf.at[slot], kv_sem.at[slot, 0]),
            pltpu.make_async_copy(vc_ref.at[layer, seqs, 0], vbuf.at[slot], kv_sem.at[slot, 1]),
        )

    def kv_start(i, slot):
        for copy in kv_copies(i, slot):
            copy.start()

    def a_own(l):
        for name, dev in (("aR", right), ("aL", left)):
            send(f"{name}{l}", a_pairs(l), dev, abuf_w.at[l, :, x, c])

    def a_forward(l):
        got(f"aR{l}", abuf_w.at[l, :, xl, c])
        view = abuf_w.at[l, 0, xl, c]
        send(f"afR{l}", [(view, view)], right)
        got(f"aL{l}", abuf_w.at[l, :, xr, c])
        view = abuf_w.at[l, 1, xr, c]
        send(f"afL{l}", [(view, view)], left)

    def a_twin(l):
        got(f"afR{l}", abuf_w.at[l, 0, xo, c])
        got(f"afL{l}", abuf_w.at[l, 1, xo, c])
        local_wait(4 * l, abuf_w.at[l, :, x, c])
        view = abuf_w.at[l, :, :, c]
        send(f"aT{l}", [(view, view)], twin)

    def a_ready(l):
        got(f"aT{l}", abuf_w.at[l, :, :, 1 - c])

    def b_own(l):
        dst = bbuf_w.at[l, x, c]
        for name, dev in (("bR", right), ("bL", left)):
            send(f"{name}{l}", [(wo_ref.at[l], dst)], dev)

    def b_forward(l):
        mid_row = bbuf_w.shape[3] // 2
        got(f"bR{l}", bbuf_w.at[l, xl, c])
        view = bbuf_w.at[l, xl, c, pl.ds(0, mid_row)]
        send(f"bfR{l}", [(view, view)], right)
        got(f"bL{l}", bbuf_w.at[l, xr, c])
        view = bbuf_w.at[l, xr, c, pl.ds(mid_row, mid_row)]
        send(f"bfL{l}", [(view, view)], left)

    def b_twin(l):
        mid_row = bbuf_w.shape[3] // 2
        got(f"bfR{l}", bbuf_w.at[l, xo, c, pl.ds(0, mid_row)])
        got(f"bfL{l}", bbuf_w.at[l, xo, c, pl.ds(mid_row, mid_row)])
        local_wait(4 * l + 1, bbuf_w.at[l, x, c])
        view = bbuf_w.at[l, :, c]
        send(f"bT{l}", [(view, view)], twin)

    def b_ready(l):
        got(f"bT{l}", bbuf_w.at[l, :, 1 - c])

    def by_matrix(l, name, xx, lo, size, dst, dev):
        cols = pl.ds(pl.multiple_of(col_start(xx) + lo, LANES), size)
        for value, ref in ((0, wg_ref), (1, wu_ref)):
            @pl.when(h == value)
            def _():
                put(name, [(ref.at[l, :, cols], dst)], dev)
        pending.append((name, dst))

    def c_direct(l):
        by_matrix(l, f"cR{l}", xr, 0, win, gu_w.at[l, h, x, c], right)
        by_matrix(l, f"cL{l}", xl, 0, win, gu_w.at[l, h, x, c], left)

    def c_transit(l):
        by_matrix(l, f"tR{l}", xo, 0, win // 2, tr_w.at[l, 0], right)
        by_matrix(l, f"tL{l}", xo, win // 2, win // 2, tr_w.at[l, 1], left)

    def c_forward(l):
        got(f"tR{l}", tr_w.at[l, 0])
        send(f"cfR{l}", [(tr_w.at[l, 0], gu_w.at[l, h, xl, c, :, pl.ds(0, win // 2)])], right)
        got(f"tL{l}", tr_w.at[l, 1])
        send(f"cfL{l}", [(tr_w.at[l, 1], gu_w.at[l, h, xr, c, :, pl.ds(win // 2, win // 2)])], left)

    def c_pair_near(l):
        for name, xx in (("cR", xl), ("cL", xr)):
            view = gu_w.at[l, h, xx, c]
            got(f"{name}{l}", view)
            send(f"p{name}{l}", [(view, view)], pair)

    def c_pair_far(l):
        got(f"cfR{l}", gu_w.at[l, h, xo, c, :, pl.ds(0, win // 2)])
        got(f"cfL{l}", gu_w.at[l, h, xo, c, :, pl.ds(win // 2, win // 2)])
        view = gu_w.at[l, h, xo, c]
        send(f"pcF{l}", [(view, view)], pair)
        local_wait(4 * l + 2, gu_w.at[l, :, x, c])
        view = gu_w.at[l, h, :, c]
        send(f"cT0{l}", [(view, view)], twin)

    def c_twin(l):
        got(f"pcR{l}", gu_w.at[l, 1 - h, xl, c])
        got(f"pcL{l}", gu_w.at[l, 1 - h, xr, c])
        got(f"pcF{l}", gu_w.at[l, 1 - h, xo, c])
        view = gu_w.at[l, 1 - h, :, c]
        send(f"cT1{l}", [(view, view)], twin)

    def c_ready(l):
        got(f"cT0{l}", gu_w.at[l, h, :, 1 - c])
        got(f"cT1{l}", gu_w.at[l, 1 - h, :, 1 - c])

    def d_twin(l):
        send(f"dT{l}", [(wd_ref.at[l], wd_at(l, c))], twin)

    def d_ready(l):
        local_wait(4 * l + 3, wd_at(l, c))
        got(f"dT{l}", wd_at(l, 1 - c))

    for l in range(layers):
        start = pl.multiple_of(jnp.where(lax.rem(x, 2) == 0, chip_cols, 0), 64)
        wd_w[l, pl.ds(start, pad), :] = jnp.zeros((pad, width), BF16)
    barrier = pltpu.get_barrier_semaphore()
    for i in range(1, n_dev):
        pl.semaphore_signal(barrier, inc=1, device_id=(dp, lax.rem(w + i, n_dev)), device_id_type=MESH)
    pl.semaphore_signal(barrier, inc=1, device_id=pair, device_id_type=MESH)
    pl.semaphore_wait(barrier, n_dev)

    for i in range(1, n_dev):
        put("gain", [(gain_ref, gbuf.at[w])], (dp, lax.rem(w + i, n_dev)))
    pending.append(("gain", gbuf.at[pl.ds(0, n_dev - 1)]))
    a_own(0)
    b_own(0)
    gain_copy = pltpu.make_async_copy(gain_ref, gbuf.at[w], loc_sem.at[4 * layers])
    gain_copy.start()
    kv_start(0, 0)
    for l in range(layers):
        local_start(4 * l, a_pairs(l))
        local_start(4 * l + 1, [(wo_ref.at[l], bbuf_w.at[l, x, c])])
        cols = pl.ds(col_start(x), win)
        local_start(4 * l + 2, [(wg_ref.at[l, :, cols], gu_w.at[l, 0, x, c]), (wu_ref.at[l, :, cols], gu_w.at[l, 1, x, c])])
        local_start(4 * l + 3, [(wd_ref.at[l], wd_at(l, c))])
        d_twin(l)
    kv_start(1, 1)

    gain_copy.wait()
    got("gain", gbuf.at[pl.ds(0, n_dev - 1)])
    tiles = []
    for j in range(width // LANES):
        total = None
        for s in range(n_dev):
            lo = (s * piece) // LANES
            for k in range(2):
                if lo + k == j:
                    block = gbuf[s, :, k * LANES:(k + 1) * LANES]
                    total = block if total is None else total + block
        tiles.append(total)
    gains = 1.0 + jnp.concatenate(tiles, axis=1)

    def rms(hid, row):
        mean_sq = jnp.sum(hid * hid, axis=-1, keepdims=True) / width
        return (hid * lax.rsqrt(mean_sq + EPS) * gains[row:row + 1, :]).astype(BF16)

    lane_seq = lax.rem(lax.broadcasted_iota(jnp.int32, (cache_len, LANES), 1), SEQ_GROUP)
    row_seq = lax.rem(lax.broadcasted_iota(jnp.int32, (LANES, cache_len), 0), SEQ_GROUP)
    row_t = lax.broadcasted_iota(jnp.int32, (cache_len, LANES), 0)
    lane_new = lax.rem(lax.broadcasted_iota(jnp.int32, (SEQ_GROUP, LANES), 1), SEQ_GROUP)
    row_new = lax.broadcasted_iota(jnp.int32, (SEQ_GROUP, LANES), 0)
    chunk = 4

    def attend(l, group):
        i = l * groups + group
        slot = lax.rem(group, 2)
        for copy in kv_copies(i, slot):
            copy.wait()
        seqs = pl.ds(pl.multiple_of(group * SEQ_GROUP, SEQ_GROUP), SEQ_GROUP)
        query = jnp.concatenate([qbuf[j, seqs, :] for j in range(heads)], axis=0)
        scores = jnp.zeros((cache_len, LANES), F32)
        for b in range(0, SEQ_GROUP, chunk):
            block = kbuf[slot, b:b + chunk].reshape(chunk * cache_len, head_dim)
            prod = dot_t(block, query)
            for j in range(chunk):
                scores = jnp.where(lane_seq == b + j, prod[j * cache_len:(j + 1) * cache_len], scores)
        k_new = knew_ref[l, seqs, :]
        v_new = vnew_ref[l, seqs, :]
        new_score = jnp.sum(jnp.where(row_new == lane_new, dot_t(k_new, query), 0.0), axis=0, keepdims=True)
        pos = pos_ref[group]
        scores = jnp.where(row_t < pos, scores, -1e30)
        top = jnp.maximum(jnp.max(scores, axis=0, keepdims=True), new_score)
        prob = jnp.exp(scores - top)
        prob_new = jnp.exp(new_score - top)
        total = jnp.sum(prob, axis=0, keepdims=True) + prob_new
        prob_t = prob.T
        total_t = jnp.broadcast_to(total, (LANES, LANES)).T
        new_t = jnp.broadcast_to(prob_new, (LANES, LANES)).T.astype(BF16).astype(F32)
        v_rep = jnp.concatenate([v_new] * heads, axis=0).astype(F32)
        acc = jnp.concatenate([new_t] * (head_dim // LANES), axis=1) * v_rep
        for b in range(0, SEQ_GROUP, chunk):
            spread = jnp.concatenate([jnp.where(row_seq == b + j, prob_t, 0.0).astype(BF16) for j in range(chunk)], axis=1)
            acc = acc + dot(spread, vbuf[slot, b:b + chunk].reshape(chunk * cache_len, head_dim))
        attn = (acc / jnp.concatenate([total_t] * (head_dim // LANES), axis=1)).astype(BF16)
        for j in range(heads):
            abuf[seqs, j * head_dim:(j + 1) * head_dim] = attn[j * SEQ_GROUP:(j + 1) * SEQ_GROUP, :]

        @pl.when(i + 2 < layers * groups)
        def _():
            kv_start(i + 2, slot)

    hbuf[...] = hid_ref[...]
    cos_tab, sin_tab = cos_ref[...], sin_ref[...]

    def qkv(l):
        normed = rms(hbuf[...].astype(F32), l)
        halves = [dot(normed, abuf_w[l, hf].reshape(width, abuf_w.shape[-1])) for hf in range(2)]

        def rope(lead, tail):
            return jnp.concatenate([lead * cos_tab - tail * sin_tab, tail * cos_tab + lead * sin_tab], axis=1)

        for j in range(heads):
            out, lo = halves[j // (heads // 2)], (j % (heads // 2)) * head_dim
            qbuf[j] = (rope(out[:, lo:lo + half], out[:, lo + half:lo + head_dim]) * head_dim ** -0.5).astype(BF16)
        knew_ref[l] = rope(halves[0][:, q_half:q_half + half], halves[1][:, q_half:q_half + half]).astype(BF16)
        vnew_ref[l] = jnp.concatenate([hv[:, q_half + half:q_half + 2 * half] for hv in halves], axis=1).astype(BF16)

    r2 = rows // 2

    def y_send(l):
        top, bottom = y_all.at[l, x, pl.ds(0, r2)], y_all.at[l, x, pl.ds(r2, r2)]
        send(f"yR1{l}", [(top, top)], right)
        send(f"yL1{l}", [(bottom, bottom)], left)
        send(f"yR2{l}", [(bottom, bottom)], right)
        send(f"yL2{l}", [(top, top)], left)

    def y_forward(l):
        view = y_all.at[l, xl, pl.ds(0, r2)]
        got(f"yR1{l}", view)
        send(f"yfR{l}", [(view, view)], right)
        view = y_all.at[l, xr, pl.ds(r2, r2)]
        got(f"yL1{l}", view)
        send(f"yfL{l}", [(view, view)], left)

    def y_ready(l):
        got(f"yR2{l}", y_all.at[l, xl, pl.ds(r2, r2)])
        got(f"yL2{l}", y_all.at[l, xr, pl.ds(0, r2)])
        got(f"yfR{l}", y_all.at[l, xo, pl.ds(0, r2)])
        got(f"yfL{l}", y_all.at[l, xo, pl.ds(r2, r2)])

    n_tile = 2 * LANES

    def gate_up(l):
        @pl.loop(0, win // n_tile)
        def _(n):
            cols = pl.ds(pl.multiple_of(n * n_tile, n_tile), n_tile)
            w_g = gu_w[l, 0, :, :, :, cols].reshape(width, n_tile)
            w_u = gu_w[l, 1, :, :, :, cols].reshape(width, n_tile)
            for r in range(0, CHIPS, 2):
                act = y_all[l, r:r + 2].reshape(2 * rows, width)
                gate = dot(act, w_g)
                up = dot(act, w_u)
                m_buf[r:r + 2, :, cols] = (jax.nn.gelu(gate, approximate=True) * up).astype(BF16).reshape(2, rows, n_tile)

    def down(l, xx):
        part[xx] = dot(m_buf[xx], wd_w[l])

    def reduce_far(l):
        down(l, xo)
        send(f"eR1{l}", [(part.at[xo, pl.ds(0, r2)], r_t.at[l, 0])], right)
        send(f"eL1{l}", [(part.at[xo, pl.ds(r2, r2)], r_t.at[l, 1])], left)

    def reduce_near(l):
        down(l, xr)
        send(f"eR2{l}", [(part.at[xr, pl.ds(r2, r2)], r_f.at[l, 0, pl.ds(r2, r2)])], right)
        down(l, xl)
        send(f"eL2{l}", [(part.at[xl, pl.ds(0, r2)], r_f.at[l, 1, pl.ds(0, r2)])], left)

    def reduce_relay(l):
        got(f"eR1{l}", r_t.at[l, 0])
        part[xr, 0:r2] = part[xr, 0:r2] + r_t[l, 0]
        send(f"eR3{l}", [(part.at[xr, pl.ds(0, r2)], r_f.at[l, 0, pl.ds(0, r2)])], right)
        got(f"eL1{l}", r_t.at[l, 1])
        part[xl, r2:rows] = part[xl, r2:rows] + r_t[l, 1]
        send(f"eL3{l}", [(part.at[xl, pl.ds(r2, r2)], r_f.at[l, 1, pl.ds(r2, r2)])], left)

    def reduce_done(l):
        got(f"eR2{l}", r_f.at[l, 0, pl.ds(r2, r2)])
        got(f"eL2{l}", r_f.at[l, 1, pl.ds(0, r2)])
        got(f"eR3{l}", r_f.at[l, 0, pl.ds(0, r2)])
        got(f"eL3{l}", r_f.at[l, 1, pl.ds(r2, r2)])
        return part[x] + r_f[l, 0] + r_f[l, 1]

    def attention(l, lo, hi):
        @pl.loop(lo, hi)
        def _(group):
            attend(l, group)

    def mix_out(l):
        mixed = dot(abuf[...], bbuf_w[l].reshape(heads * head_dim, width))
        hid_mid = (hbuf[...].astype(F32) + mixed).astype(BF16)
        hbuf[...] = hid_mid
        y_all[l, x] = rms(hid_mid.astype(F32), layers + l)

    a_forward(0)
    c_direct(0)
    c_transit(0)
    b_forward(0)
    a_twin(0)
    a_ready(0)
    qkv(0)
    attention(0, 0, groups // 2)
    b_twin(0)
    c_pair_near(0)
    c_forward(0)
    attention(0, groups // 2, groups)
    b_ready(0)
    mix_out(0)
    y_send(0)
    c_pair_far(0)
    y_forward(0)
    a_own(1)
    b_own(1)
    y_ready(0)
    c_twin(0)
    c_ready(0)
    d_ready(0)
    c_direct(1)
    a_forward(1)
    gate_up(0)
    reduce_far(0)
    reduce_near(0)
    b_forward(1)
    reduce_relay(0)
    c_transit(1)
    a_twin(1)
    c_pair_near(1)
    down(0, x)
    hbuf[...] = (hbuf[...].astype(F32) + reduce_done(0)).astype(BF16)
    a_ready(1)
    qkv(1)
    c_forward(1)
    b_twin(1)
    attention(1, 0, groups // 2)
    c_pair_far(1)
    attention(1, groups // 2, groups)
    b_ready(1)
    mix_out(1)
    y_send(1)
    c_twin(1)
    y_forward(1)
    y_ready(1)
    c_ready(1)
    d_ready(1)
    gate_up(1)
    drain()
    reduce_far(1)
    reduce_near(1)
    reduce_relay(1)
    down(1, x)
    out_ref[...] = (hbuf[...].astype(F32) + reduce_done(1)).astype(BF16)
    drain()
    assert len(msg_ids) <= send_sem.shape[0]


def decode(hidden, positions, k_cache, v_cache, attn_norm, w_query, w_key, w_value, w_out, mlp_norm, w_gate, w_up, w_down):
    layers, rows, _, cache_len, head_dim = k_cache.shape
    width = hidden.shape[1]
    n_dev = lax.axis_size("w")
    ff = w_gate.shape[-1]
    heads = w_query.shape[-1] // head_dim
    chip_cols = ff // CHIPS
    win = -(-(chip_cols + LANES // 2) // LANES) * LANES
    piece = width // n_dev
    groups = rows // SEQ_GROUP
    assert n_dev == CHIPS * CORES and heads * SEQ_GROUP == LANES and cache_len == LANES
    cos_tab, sin_tab = rope_tables(positions, head_dim)
    offset = lax.rem(lax.axis_index("w") * piece, LANES)
    gain = lax.dynamic_update_slice(jnp.zeros((8, 2 * LANES), F32), jnp.concatenate([attn_norm, mlp_norm], axis=0), (0, offset))
    pos_lane = jnp.tile(positions.reshape(groups, 1, SEQ_GROUP), (1, 1, heads))
    dims = (layers, rows, width, heads, head_dim, cache_len, n_dev, ff)
    vmem, anym = pl.BlockSpec(memory_space=pltpu.VMEM), pl.BlockSpec(memory_space=pl.ANY)
    new_shape = jax.ShapeDtypeStruct((layers, rows, head_dim), BF16)
    n_msg = 96
    return pl.pallas_call(
        functools.partial(decode_kernel, dims),
        out_shape=(jax.ShapeDtypeStruct(hidden.shape, BF16), new_shape, new_shape),
        in_specs=[vmem] * 5 + [anym] * 9,
        out_specs=(vmem,) * 3,
        scratch_shapes=[
            pltpu.VMEM((n_dev, 8, 2 * LANES), F32),
            pltpu.VMEM((layers, 2, CHIPS, CORES, piece, w_query.shape[-1] // 2 + head_dim), BF16),
            pltpu.VMEM((layers, CHIPS, CORES, w_out.shape[1], width), BF16),
            pltpu.VMEM((layers, 2, CHIPS, CORES, piece, win), BF16),
            pltpu.VMEM((layers, win, width), BF16),
            pltpu.VMEM((layers, 2, piece, win // 2), BF16),
            pltpu.VMEM((layers, CHIPS, rows, width), BF16),
            pltpu.VMEM((CHIPS, rows, win), BF16),
            pltpu.VMEM((CHIPS, rows, width), F32),
            pltpu.VMEM((layers, 2, rows // 2, width), F32),
            pltpu.VMEM((layers, 2, rows, width), F32),
            pltpu.VMEM((2, SEQ_GROUP, cache_len, head_dim), BF16),
            pltpu.VMEM((2, SEQ_GROUP, cache_len, head_dim), BF16),
            pltpu.VMEM((heads, rows, head_dim), BF16),
            pltpu.VMEM((rows, heads * head_dim), BF16),
            pltpu.VMEM((rows, width), BF16),
            pltpu.SemaphoreType.DMA((n_msg,)),
            pltpu.SemaphoreType.DMA((n_msg,)),
            pltpu.SemaphoreType.DMA((4 * layers + 1,)),
            pltpu.SemaphoreType.DMA((2, 2)),
        ],
        compiler_params=pltpu.CompilerParams(collective_id=0, has_side_effects=True, vmem_limit_bytes=67043328),
        name="decode",
    )(hidden, cos_tab, sin_tab, gain, pos_lane, k_cache, v_cache, w_query, w_key, w_value, w_out, w_gate, w_up, w_down)


TILE_ROWS = 16
CACHE_BLOCK = 16
CACHE_SLOTS = 6


def cache_kernel(pos_ref, kc_ref, vc_ref, kn_ref, vn_ref, ko_ref, vo_ref, buf, in_sem, out_sem):
    layers, rows = kc_ref.shape[:2]
    blocks = rows // CACHE_BLOCK
    steps = [(src, new, dst, l, b) for l in range(layers) for src, new, dst in ((kc_ref, kn_ref, ko_ref), (vc_ref, vn_ref, vo_ref)) for b in range(blocks)]

    def load(i):
        src, _, _, l, b = steps[i]
        slot = i % CACHE_SLOTS
        return pltpu.make_async_copy(src.at[l, pl.ds(b * CACHE_BLOCK, CACHE_BLOCK), 0], buf.at[slot], in_sem.at[slot])

    def store(i):
        _, _, dst, l, b = steps[i]
        slot = i % CACHE_SLOTS
        return pltpu.make_async_copy(buf.at[slot], dst.at[l, pl.ds(b * CACHE_BLOCK, CACHE_BLOCK), 0], out_sem.at[slot])

    ahead = CACHE_SLOTS // 2
    for i in range(ahead):
        load(i).start()
    row = lax.broadcasted_iota(jnp.int32, (TILE_ROWS, buf.shape[-1]), 0)
    for i in range(len(steps)):
        load(i).wait()
        _, new, _, l, b = steps[i]
        slot = i % CACHE_SLOTS

        @pl.loop(0, CACHE_BLOCK)
        def _(s):
            pos = pos_ref[b * CACHE_BLOCK + s]
            base = pl.multiple_of(pos // TILE_ROWS * TILE_ROWS, TILE_ROWS)
            tile = buf[slot, s, pl.ds(base, TILE_ROWS), :].astype(F32)
            fresh = new[l, pl.ds(b * CACHE_BLOCK + s, 1), :]
            buf[slot, s, pl.ds(base, TILE_ROWS), :] = jnp.where(row == pos - base, fresh, tile).astype(BF16)

        store(i).start()
        nxt = i + ahead
        if nxt < len(steps):
            if nxt >= CACHE_SLOTS:
                store(nxt - CACHE_SLOTS).wait()
            load(nxt).start()
    for i in range(max(0, len(steps) - CACHE_SLOTS), len(steps)):
        store(i).wait()


def write_caches(positions, k_cache, v_cache, k_new, v_new):
    cache_len, head_dim = k_cache.shape[-2:]
    vmem, anym = pl.BlockSpec(memory_space=pltpu.VMEM), pl.BlockSpec(memory_space=pl.ANY)
    shape = jax.ShapeDtypeStruct(k_cache.shape, BF16)
    return pl.pallas_call(
        cache_kernel,
        out_shape=(shape, shape),
        in_specs=[pl.BlockSpec(memory_space=pltpu.SMEM), anym, anym, vmem, vmem],
        out_specs=(anym, anym),
        scratch_shapes=[
            pltpu.VMEM((CACHE_SLOTS, CACHE_BLOCK, cache_len, head_dim), BF16),
            pltpu.SemaphoreType.DMA((CACHE_SLOTS,)),
            pltpu.SemaphoreType.DMA((CACHE_SLOTS,)),
        ],
        compiler_params=pltpu.CompilerParams(vmem_limit_bytes=60 * 2**20),
        name="caches",
    )(positions, k_cache, v_cache, k_new.astype(F32), v_new.astype(F32))


def solution(mesh):
    batch_spec = P(("dp", "w"))
    cache_spec = P(None, ("dp", "w"))
    gain_spec = P(None, "w")
    weight_spec = P(None, "w", None)

    def per_device(hidden, positions, k_cache, v_cache, *weights):
        hidden_out, k_new, v_new = decode(hidden, positions, k_cache, v_cache, *weights)
        k_out, v_out = write_caches(positions, k_cache, v_cache, k_new, v_new)
        return hidden_out, k_out, v_out

    in_specs = (batch_spec, batch_spec, cache_spec, cache_spec, gain_spec, weight_spec, weight_spec, weight_spec, weight_spec, gain_spec, weight_spec, weight_spec, weight_spec)
    out_specs = (batch_spec, cache_spec, cache_spec)
    return jax.shard_map(per_device, mesh=mesh, in_specs=in_specs, out_specs=out_specs, check_vma=False)
```

time: 617 us -> 227 us (0.37)
  waiting for transfers between devices: 340 us -> 0 us
  Pallas kernels: 0 us -> 216 us
  blocking collectives: 125 us -> 0 us
  matrix products: 84.7 us -> 0 us
  other arithmetic: 29.9 us -> 5.58 us
  local copies, waits for them, and re-layouts: 20.6 us -> 4.1 us
  between operations: 15.3 us -> 0.68 us
    all_gather x10 -> x0, waiting for transfers between devices: 337 us -> none  [gather_rows(): return lax.all_gather(row_shard, 'w', axis=0, tiled=True)]
    pallas_call x0 -> x2, Pallas kernels: none -> 216 us  [the longest x1 189 us: decode(): pl.pallas_call(functools.partial(decode_kernel, dims), out_shape=(jax.Sha...]
    all_gather x4 -> x0, blocking collectives: 97.5 us -> none  [gather_rows(): return lax.all_gather(row_shard, 'w', axis=0, tiled=True)]
    dot_general x16 -> x0, matrix products: 84.7 us -> none  [the longest x2 32 us: per_device(): jnp.dot(mlp_hidden, gather_rows(w_down[layer_idx]), preferred_element_typ...]
    unnamed x1 -> x0, blocking collectives: 27.3 us -> none
    slice x9 -> x0, local copies, waits for them, and re-layouts: 17 us -> none  [the longest x1 4.4 us: per_device(): w_up[layer_idx]]
    select_n x2 -> x0, other arithmetic: 14 us -> none  [the longest x1 8.71 us: attention_core(): k_layer = jnp.where(write_mask, k_rot[:, :, None, :], k_layer)]
    unnamed x3 -> x0, other arithmetic: 6.75 us -> none
  transfers between devices with their start and end apart: 10 -> 0, of which waited for: 7 -> 0; matrix products, arithmetic and copies ran while one was open for 19% -> 0% of each run, Pallas kernels for 0% -> 0%
where the time goes in v1:
time: 227 us; the launch traced here: 226 us
  Pallas kernels  216 us (95%)
  other arithmetic  5.58 us (2%)
  local copies, waits for them, and re-layouts  4.1 us (2%)
    pallas_call x1, Pallas kernels, decode(): pl.pallas_call(functools.partial(decode_kernel, dims), out_shape=(jax.Sha...  189 us
    pallas_call x1, Pallas kernels, write_caches(): pl.pallas_call(cache_kernel, out_shape=(shape, shape), in_specs=[pl.Block...  26.9 us

profile of v1, /device:TPU:112, one launch (start us, length us, event | category | flops | bytes accessed | tf_op | source)
XLA Modules:
  0.0 226.5 jit_solution(7408918601598610568)
XLA Ops:
  0.6 0.7 convert_element_type.9
  1.3 0.7 tile.10
  2.1 0.7 pad_maximum_fusion
  2.8 0.7 tile.12.pos_ref
  3.4 0.6 broadcast_in_dim.2
  4.0 1.4 dynamic_update_slice.3.gain_ref
  5.4 1.0 multiply_sine_fusion
  6.4 189.2 %decode.1 = (bf16[128,1152]{1,0:T(8,128)(2,1)}, bf16[2,128,256]{2,1,0:T(8,128)(2,1)}, bf16[2,128,256]{2,1,0:T(8,128)(2,1)}) custom-call(bf16[128,1152]{1,0:T(8,128)(2,1)} %hid_ref.1, f32[128,128]{1,0:T(8,128)} %get-tuple-element.14.cos_ref, f32[128,128]{1,0:T(8,128)} %get-tuple-element.13.sin_ref, f32[8,256]{1,0:T(8,128)} %dynamic_update_slice.3.gain_ref, ...), custom_call_target="tpu_custom_call" | custom-call | tf_op jit(solution)/shard_map/decode/pallas_call | solution.py:488
  195.6 1.6 convert_element_type.10.kn_ref
  197.2 1.6 convert_element_type.11.vn_ref
  198.8 0.0 copy-start
  198.8 26.9 %caches.1 = (bf16[2,128,1,128,256]{4,3,2,1,0:T(8,128)(2,1)}, bf16[2,128,1,128,256]{4,3,2,1,0:T(8,128)(2,1)}) custom-call(s32[128]{0:T(128)} %pos_ref.1, bf16[2,128,1,128,256]{4,3,2,1,0:T(8,128)(2,1)} %kc_ref.3, bf16[2,128,1,128,256]{4,3,2,1,0:T(8,128)(2,1)} %vc_ref.3, f32[2,128,256]{2,1,0:T(8,128)} %convert_element_type.10.kn_ref, ...), custom_call_target="tpu_custom_call" | custom-call | tf_op jit(solution)/shard_map/caches/pallas_call | solution.py:571
  225.7 0.0 copy-done
  225.7 0.7 copy.18
  (2 shorter events, 0.0 us)
Async XLA Ops:
  198.8 26.9 %copy-start = (bf16[128,1152]{1,0:T(8,128)(2,1)S(1)}, bf16[128,1152]{1,0:T(8,128)(2,1)}, u32[]{:S(2)}) copy-start(bf16[128,1152]{1,0:T(8,128)(2,1)} %get-tuple-element.18) | copy-start | bytes 884740

commit v2 on v1

v2 whole, which is shorter than its diff:
```python
import functools

import jax
import jax.numpy as jnp
from jax import lax
from jax.experimental import pallas as pl
from jax.experimental.pallas import tpu as pltpu
from jax.sharding import PartitionSpec as P

EPS = 1e-6
ROPE_BASE = 10000.0
LANES = 128
CORES = 2
CHIPS = 4
SEQ_GROUP = 32
MESH = pl.DeviceIdType.MESH
F32 = jnp.float32
BF16 = jnp.bfloat16


def rope_tables(positions, head_dim):
    half_dim = head_dim // 2
    inv_freq = ROPE_BASE ** (-2.0 * jnp.arange(half_dim, dtype=jnp.float32) / head_dim)
    angles = positions.astype(jnp.float32)[:, None] * inv_freq[None, :]
    return jnp.cos(angles), jnp.sin(angles)


def dot(a, b):
    return jnp.dot(a, b, preferred_element_type=F32)


def dot_t(a, b):
    return lax.dot_general(a, b, (((1,), (1,)), ((), ())), preferred_element_type=F32)


ORDER = (
    "bo0", "ao0", "ct0", "bf0", "af0", "cf0", "cd0", "ct1", "bx0", "ax0", "cx0", "aw0", "dt0", "qkv0",
    "att0", "bw0", "ao1", "att0", "att0", "cd1", "cn0", "af1", "att0", "mix0", "yf0", "cf1", "cw0", "ax1", "dt1",
    "gua0", "near0", "cn1", "gub0", "far0", "bo1", "er0", "own0", "bf1", "aw1", "cx1", "done0", "qkv1",
    "att1", "att1", "bx1", "att1", "att1", "mix1", "cw1", "yf1", "gua1", "near1", "gub1", "far1", "er1", "own1", "done1",
)
SHARE_A = (True, True)
SHARE_B = (True, False)


def decode_kernel(
    dims,
    hid_ref, cos_ref, sin_ref, an_ref, mn_ref, pos_ref, kc_ref, vc_ref,
    wq_ref, wk_ref, wv_ref, wo_ref, wg_ref, wu_ref, wd_ref,
    out_ref, knew_ref, vnew_ref,
    gsrc, gbuf, pos_buf, abuf_w, bbuf_w, gu_w, wd_w, tr_w, y_all, m_buf, part, r_t, r_f,
    kbuf, vbuf, qbuf, abuf, hbuf,
    send_sem, recv_sem, loc_sem, kv_sem,
):
    layers, rows, width, heads, head_dim, cache_len, n_dev, ff = dims
    half = head_dim // 2
    piece = width // n_dev
    chip_cols = ff // CHIPS
    win = gu_w.shape[-1]
    pad = win - chip_cols
    wd_rows = wd_ref.shape[1]
    wo_rows = wo_ref.shape[1]
    q_half = wq_ref.shape[-1] // 2
    kv_half = half
    a_cols = abuf_w.shape[-1]
    groups = rows // SEQ_GROUP
    w = lax.axis_index("w")
    dp = lax.axis_index("dp")
    x, c = lax.div(w, CORES), lax.rem(w, CORES)
    h = lax.rem(dp, 2)
    xr, xo, xl = lax.rem(x + 1, CHIPS), lax.rem(x + 2, CHIPS), lax.rem(x + 3, CHIPS)
    cc = 1 - c
    hh = 1 - h
    right, left = (dp, xr * CORES + c), (dp, xl * CORES + c)
    twin = (dp, x * CORES + cc)
    pair = (dp + 1 - 2 * h, w)
    b_half, b_quarter = wo_rows // 2, wo_rows // 4
    b_mine = pl.multiple_of(h * b_half, b_quarter)
    b_mid = pl.multiple_of(h * b_half + b_quarter, b_quarter)
    b_other = pl.multiple_of(hh * b_half, b_quarter)
    q_mine = pl.multiple_of(h * q_half, LANES)
    kv_mine = pl.multiple_of(h * kv_half, LANES)
    starts = [pl.multiple_of(lax.div(chip_cols * xx, LANES) * LANES, LANES) for xx in (x, xr, xo, xl)]
    x_start, xr_start, xo_start, xl_start = starts
    xo_mid = pl.multiple_of(xo_start + win // 2, LANES)
    shift = lax.rem(chip_cols * x, LANES)
    wd_mine = pl.ds(pl.multiple_of(shift + wd_rows * c, 32), wd_rows)
    wd_twin = pl.ds(pl.multiple_of(shift + wd_rows * cc, 32), wd_rows)

    msg_ids = {}
    pending = {}

    def copy_of(name, src, dst, dev):
        i = msg_ids.setdefault(name, len(msg_ids))
        return pltpu.make_async_remote_copy(src, dst, send_sem.at[i], recv_sem.at[i], device_id=dev, device_id_type=MESH)

    def send(name, pairs, dev, view=None):
        for src, dst in pairs:
            copy_of(name, src, dst, dev).start()
        pending[name] = pairs[0][0] if view is None else view

    def got(name, view):
        copy_of(name, view, view, right).wait_recv()

    def drain(names):
        for name in names:
            view = pending.pop(name)
            copy_of(name, view, view, right).wait_send()

    def local_start(sem, pairs):
        for src, dst in pairs:
            pltpu.make_async_copy(src, dst, loc_sem.at[sem]).start()

    def local_wait(sem, view):
        pltpu.make_async_copy(view, view, loc_sem.at[sem]).wait()

    def kv_copies(i, slot):
        layer, group = lax.div(i, groups), lax.rem(i, groups)
        seqs = pl.ds(group * SEQ_GROUP, SEQ_GROUP)
        return (
            pltpu.make_async_copy(kc_ref.at[layer, seqs, 0], kbuf.at[slot], kv_sem.at[slot, 0]),
            pltpu.make_async_copy(vc_ref.at[layer, seqs, 0], vbuf.at[slot], kv_sem.at[slot, 1]),
        )

    def kv_start(i, slot):
        for copy in kv_copies(i, slot):
            copy.start()

    def a_pairs(l, hf, q_lo, kv_lo):
        dst = abuf_w.at[l, hf, x, c]
        return [
            (wq_ref.at[l, :, pl.ds(q_lo, q_half)], dst.at[:, pl.ds(0, q_half)]),
            (wk_ref.at[l, :, pl.ds(kv_lo, kv_half)], dst.at[:, pl.ds(q_half, kv_half)]),
            (wv_ref.at[l, :, pl.ds(kv_lo, kv_half)], dst.at[:, pl.ds(q_half + kv_half, kv_half)]),
        ]

    def a_both(l):
        return a_pairs(l, 0, 0, 0) + a_pairs(l, 1, q_half, kv_half)

    def a_block(l, xx):
        return abuf_w.at[l, h, xx, c] if SHARE_A[l] else abuf_w.at[l, :, xx, c]

    def a_lead(l, xx):
        return abuf_w.at[l, h, xx, c, :, pl.ds(0, a_cols // 2)] if SHARE_A[l] else abuf_w.at[l, 0, xx, c]

    def a_tail(l, xx):
        return abuf_w.at[l, h, xx, c, :, pl.ds(a_cols // 2, a_cols // 2)] if SHARE_A[l] else abuf_w.at[l, 1, xx, c]

    def ao(l):
        pairs = a_pairs(l, h, q_mine, kv_mine) if SHARE_A[l] else a_both(l)
        send(f"aR{l}", pairs, right, a_block(l, x))
        send(f"aL{l}", pairs, left, a_block(l, x))

    def to_pair(name, view):
        send(name, [(view, view)], pair)

    def af(l):
        got(f"aR{l}", a_block(l, xl))
        send(f"afR{l}", [(a_lead(l, xl), a_lead(l, xl))], right)
        got(f"aL{l}", a_block(l, xr))
        send(f"afL{l}", [(a_tail(l, xr), a_tail(l, xr))], left)
        if SHARE_A[l]:
            to_pair(f"paR{l}", a_block(l, xl))
            to_pair(f"paL{l}", a_block(l, xr))

    def ax(l):
        got(f"afR{l}", a_lead(l, xo))
        got(f"afL{l}", a_tail(l, xo))
        if SHARE_A[l]:
            to_pair(f"paF{l}", a_block(l, xo))
        local_wait(4 * l, abuf_w.at[l, :, x, c])
        view = abuf_w.at[l, h, :, c] if SHARE_A[l] else abuf_w.at[l, :, :, c]
        send(f"aT{l}", [(view, view)], twin)

    def aw(l):
        for name, xx in (("paR", xl), ("paL", xr), ("paF", xo)):
            got(f"{name}{l}", abuf_w.at[l, hh, xx, c])
        view = abuf_w.at[l, hh, :, c]
        send(f"aT1{l}", [(view, view)], twin)

    def a_ready(l):
        if SHARE_A[l]:
            got(f"aT{l}", abuf_w.at[l, h, :, cc])
            got(f"aT1{l}", abuf_w.at[l, hh, :, cc])
        else:
            got(f"aT{l}", abuf_w.at[l, :, :, cc])

    def b_block(l, xx):
        return bbuf_w.at[l, xx, c, pl.ds(b_mine, b_half)] if SHARE_B[l] else bbuf_w.at[l, xx, c]

    def b_lead(l, xx):
        return bbuf_w.at[l, xx, c, pl.ds(b_mine, b_quarter)] if SHARE_B[l] else bbuf_w.at[l, xx, c, pl.ds(0, b_half)]

    def b_tail(l, xx):
        return bbuf_w.at[l, xx, c, pl.ds(b_mid, b_quarter)] if SHARE_B[l] else bbuf_w.at[l, xx, c, pl.ds(b_half, b_half)]

    def bo(l):
        src = wo_ref.at[l, pl.ds(b_mine, b_half)] if SHARE_B[l] else wo_ref.at[l]
        send(f"bR{l}", [(src, b_block(l, x))], right)
        send(f"bL{l}", [(src, b_block(l, x))], left)

    def bf(l):
        got(f"bR{l}", b_block(l, xl))
        send(f"bfR{l}", [(b_lead(l, xl), b_lead(l, xl))], right)
        got(f"bL{l}", b_block(l, xr))
        send(f"bfL{l}", [(b_tail(l, xr), b_tail(l, xr))], left)
        if SHARE_B[l]:
            to_pair(f"pbR{l}", b_block(l, xl))
            to_pair(f"pbL{l}", b_block(l, xr))

    def bx(l):
        got(f"bfR{l}", b_lead(l, xo))
        got(f"bfL{l}", b_tail(l, xo))
        if SHARE_B[l]:
            to_pair(f"pbF{l}", b_block(l, xo))
        local_wait(4 * l + 1, bbuf_w.at[l, x, c])
        view = bbuf_w.at[l, :, c, pl.ds(b_mine, b_half)] if SHARE_B[l] else bbuf_w.at[l, :, c]
        send(f"bT{l}", [(view, view)], twin)

    def bw(l):
        for name, xx in (("pbR", xl), ("pbL", xr), ("pbF", xo)):
            got(f"{name}{l}", bbuf_w.at[l, xx, c, pl.ds(b_other, b_half)])
        view = bbuf_w.at[l, :, c, pl.ds(b_other, b_half)]
        send(f"bT1{l}", [(view, view)], twin)

    def b_ready(l):
        if SHARE_B[l]:
            got(f"bT{l}", bbuf_w.at[l, :, cc, pl.ds(b_mine, b_half)])
            got(f"bT1{l}", bbuf_w.at[l, :, cc, pl.ds(b_other, b_half)])
        else:
            got(f"bT{l}", bbuf_w.at[l, :, cc])

    def by_matrix(l, name, lo, size, dst, dev):
        for value, ref in ((0, wg_ref), (1, wu_ref)):
            @pl.when(h == value)
            def _():
                copy_of(name, ref.at[l, :, pl.ds(lo, size)], dst, dev).start()
        pending[name] = dst

    def cd(l):
        by_matrix(l, f"cR{l}", xr_start, win, gu_w.at[l, h, x, c], right)
        by_matrix(l, f"cL{l}", xl_start, win, gu_w.at[l, h, x, c], left)

    def ct(l):
        by_matrix(l, f"tR{l}", xo_start, win // 2, tr_w.at[l, 0], right)
        by_matrix(l, f"tL{l}", xo_mid, win // 2, tr_w.at[l, 1], left)

    def cf(l):
        got(f"tR{l}", tr_w.at[l, 0])
        send(f"cfR{l}", [(tr_w.at[l, 0], gu_w.at[l, h, xl, c, :, pl.ds(0, win // 2)])], right)
        got(f"tL{l}", tr_w.at[l, 1])
        send(f"cfL{l}", [(tr_w.at[l, 1], gu_w.at[l, h, xr, c, :, pl.ds(win // 2, win // 2)])], left)

    def cn(l):
        for name, xx in (("cR", xl), ("cL", xr)):
            got(f"{name}{l}", gu_w.at[l, h, xx, c])
            to_pair(f"p{name}{l}", gu_w.at[l, h, xx, c])

    def cx(l):
        got(f"cfR{l}", gu_w.at[l, h, xo, c, :, pl.ds(0, win // 2)])
        got(f"cfL{l}", gu_w.at[l, h, xo, c, :, pl.ds(win // 2, win // 2)])
        to_pair(f"pcF{l}", gu_w.at[l, h, xo, c])

    def cw(l):
        local_wait(4 * l + 2, gu_w.at[l, :, x, c])
        view = gu_w.at[l, h, :, c]
        send(f"cT{l}", [(view, view)], twin)
        for name, xx in (("pcR", xl), ("pcL", xr), ("pcF", xo)):
            got(f"{name}{l}", gu_w.at[l, hh, xx, c])
        view = gu_w.at[l, hh, :, c]
        send(f"cT1{l}", [(view, view)], twin)

    def c_ready(l):
        got(f"cT{l}", gu_w.at[l, h, :, cc])
        got(f"cT1{l}", gu_w.at[l, hh, :, cc])

    def dt(l):
        send(f"dT{l}", [(wd_ref.at[l], wd_w.at[l, wd_mine])], twin)

    def d_ready(l):
        local_wait(4 * l + 3, wd_w.at[l, wd_mine])
        got(f"dT{l}", wd_w.at[l, wd_twin])

    for l in range(layers):
        start = pl.multiple_of(jnp.where(lax.rem(x, 2) == 0, chip_cols, 0), 64)
        wd_w[l, pl.ds(start, pad), :] = jnp.zeros((pad, width), BF16)
    gsrc[...] = jnp.zeros_like(gsrc)
    gsrc[0:layers, 0:piece] = an_ref[...]
    gsrc[layers:2 * layers, 0:piece] = mn_ref[...]
    gsrc[...] = pltpu.roll(gsrc[...], lax.rem(w * piece, LANES), 1)
    barrier = pltpu.get_barrier_semaphore()
    for i in range(1, n_dev):
        pl.semaphore_signal(barrier, inc=1, device_id=(dp, lax.rem(w + i, n_dev)), device_id_type=MESH)
    pl.semaphore_signal(barrier, inc=1, device_id=pair, device_id_type=MESH)
    pl.semaphore_wait(barrier, n_dev)

    def entry():
        for i in range(1, n_dev):
            copy_of("gain", gsrc, gbuf.at[w], (dp, lax.rem(w + i, n_dev))).start()
        pending["gain"] = gbuf.at[pl.ds(0, n_dev - 1)]
        gbuf[w] = gsrc[...]
        kv_start(0, 0)
        for l in range(layers):
            local_start(4 * l, a_both(l))
            local_start(4 * l + 1, [(wo_ref.at[l], bbuf_w.at[l, x, c])])
            cols = pl.ds(x_start, win)
            local_start(4 * l + 2, [(wg_ref.at[l, :, cols], gu_w.at[l, 0, x, c]), (wu_ref.at[l, :, cols], gu_w.at[l, 1, x, c])])
            local_start(4 * l + 3, [(wd_ref.at[l], wd_w.at[l, wd_mine])])
        kv_start(1, 1)
        hbuf[...] = hid_ref[...]
        lane_block = lax.div(lax.broadcasted_iota(jnp.int32, (1, LANES), 1), SEQ_GROUP)
        for g in range(groups):
            line = pos_ref[...]
            for j in range(heads):
                moved = pltpu.roll(pos_ref[...], lax.rem(w * 0 + (j - g + heads) * SEQ_GROUP, LANES), 1)
                line = jnp.where(lane_block == j, moved, line)
            pos_buf[g] = line

    def all_gains():
        tiles = []
        for j in range(width // LANES):
            total = None
            for s in range(n_dev):
                lo = (s * piece) // LANES
                for k in range(2):
                    if lo + k == j:
                        block = gbuf[s, :, k * LANES:(k + 1) * LANES]
                        total = block if total is None else total + block
            tiles.append(total)
        return 1.0 + jnp.concatenate(tiles, axis=1)

    def rms(hid, row):
        mean_sq = jnp.sum(hid * hid, axis=-1, keepdims=True) / width
        return (hid * lax.rsqrt(mean_sq + EPS) * all_gains()[row:row + 1, :]).astype(BF16)

    chunk = 4

    def attend(l, group):
        lane_seq = lax.rem(lax.broadcasted_iota(jnp.int32, (cache_len, LANES), 1), SEQ_GROUP)
        row_seq = lax.rem(lax.broadcasted_iota(jnp.int32, (LANES, cache_len), 0), SEQ_GROUP)
        row_t = lax.broadcasted_iota(jnp.int32, (cache_len, LANES), 0)
        lane_new = lax.rem(lax.broadcasted_iota(jnp.int32, (SEQ_GROUP, LANES), 1), SEQ_GROUP)
        row_new = lax.broadcasted_iota(jnp.int32, (SEQ_GROUP, LANES), 0)
        i = l * groups + group
        slot = lax.rem(group, 2)
        for copy in kv_copies(i, slot):
            copy.wait()
        seqs = pl.ds(pl.multiple_of(group * SEQ_GROUP, SEQ_GROUP), SEQ_GROUP)
        query = jnp.concatenate([qbuf[j, seqs, :] for j in range(heads)], axis=0)
        scores = jnp.zeros((cache_len, LANES), F32)
        for b in range(0, SEQ_GROUP, chunk):
            block = kbuf[slot, b:b + chunk].reshape(chunk * cache_len, head_dim)
            prod = dot_t(block, query)
            for j in range(chunk):
                scores = jnp.where(lane_seq == b + j, prod[j * cache_len:(j + 1) * cache_len], scores)
        k_new = knew_ref[l, seqs, :].astype(BF16)
        v_new = vnew_ref[l, seqs, :]
        new_score = jnp.sum(jnp.where(row_new == lane_new, dot_t(k_new, query), 0.0), axis=0, keepdims=True)
        scores = jnp.where(row_t < pos_buf[group], scores, -1e30)
        top = jnp.maximum(jnp.max(scores, axis=0, keepdims=True), new_score)
        prob = jnp.exp(scores - top)
        prob_new = jnp.exp(new_score - top)
        total = jnp.sum(prob, axis=0, keepdims=True) + prob_new
        prob_t = prob.T
        total_t = jnp.broadcast_to(total, (LANES, LANES)).T
        new_t = jnp.broadcast_to(prob_new, (LANES, LANES)).T.astype(BF16).astype(F32)
        v_rep = jnp.concatenate([v_new] * heads, axis=0)
        acc = jnp.concatenate([new_t] * (head_dim // LANES), axis=1) * v_rep
        for b in range(0, SEQ_GROUP, chunk):
            spread = jnp.concatenate([jnp.where(row_seq == b + j, prob_t, 0.0).astype(BF16) for j in range(chunk)], axis=1)
            acc = acc + dot(spread, vbuf[slot, b:b + chunk].reshape(chunk * cache_len, head_dim))
        attn = (acc / jnp.concatenate([total_t] * (head_dim // LANES), axis=1)).astype(BF16)
        for j in range(heads):
            abuf[seqs, j * head_dim:(j + 1) * head_dim] = attn[j * SEQ_GROUP:(j + 1) * SEQ_GROUP, :]

        @pl.when(i + 2 < layers * groups)
        def _():
            kv_start(i + 2, slot)

    def qkv(l):
        a_ready(l)
        if l == 0:
            got("gain", gbuf.at[pl.ds(0, n_dev - 1)])
        cos_tab, sin_tab = cos_ref[...], sin_ref[...]
        normed = rms(hbuf[...].astype(F32), l)
        halves = [dot(normed, abuf_w[l, hf].reshape(width, a_cols)) for hf in range(2)]

        def rope(lead, tail):
            return jnp.concatenate([lead * cos_tab - tail * sin_tab, tail * cos_tab + lead * sin_tab], axis=1)

        for j in range(heads):
            out, lo = halves[j // (heads // 2)], (j % (heads // 2)) * head_dim
            qbuf[j] = (rope(out[:, lo:lo + half], out[:, lo + half:lo + head_dim]) * head_dim ** -0.5).astype(BF16)
        knew_ref[l] = rope(halves[0][:, q_half:q_half + half], halves[1][:, q_half:q_half + half]).astype(BF16).astype(F32)
        vnew_ref[l] = jnp.concatenate([hv[:, q_half + half:q_half + 2 * half] for hv in halves], axis=1).astype(BF16).astype(F32)

    r2 = rows // 2
    upper, lower = pl.ds(0, r2), pl.ds(r2, r2)

    def mix(l):
        b_ready(l)
        mixed = dot(abuf[...], bbuf_w[l].reshape(heads * head_dim, width))
        hid_mid = (hbuf[...].astype(F32) + mixed).astype(BF16)
        hbuf[...] = hid_mid
        y_all[l, x] = rms(hid_mid.astype(F32), layers + l)
        top, bottom = y_all.at[l, x, upper], y_all.at[l, x, lower]
        send(f"yR1{l}", [(top, top)], right)
        send(f"yL1{l}", [(bottom, bottom)], left)
        send(f"yR2{l}", [(bottom, bottom)], right)
        send(f"yL2{l}", [(top, top)], left)

    def yf(l):
        view = y_all.at[l, xl, upper]
        got(f"yR1{l}", view)
        send(f"yfR{l}", [(view, view)], right)
        view = y_all.at[l, xr, lower]
        got(f"yL1{l}", view)
        send(f"yfL{l}", [(view, view)], left)

    n_tile = 2 * LANES

    def gate_up(l, blocks):
        @pl.loop(0, win // n_tile)
        def _(n):
            cols = pl.ds(pl.multiple_of(n * n_tile, n_tile), n_tile)
            act = jnp.concatenate([y_all[l, b] for b in blocks], axis=0)
            gate = dot(act, gu_w[l, 0, :, :, :, cols].reshape(width, n_tile))
            up = dot(act, gu_w[l, 1, :, :, :, cols].reshape(width, n_tile))
            mid = (jax.nn.gelu(gate, approximate=True) * up).astype(BF16)
            for k, b in enumerate(blocks):
                m_buf[b, :, cols] = mid[k * rows:(k + 1) * rows]

    def gua(l):
        got(f"yR2{l}", y_all.at[l, xl, lower])
        got(f"yL2{l}", y_all.at[l, xr, upper])
        c_ready(l)
        gate_up(l, (xl, xr))

    def gub(l):
        got(f"yfR{l}", y_all.at[l, xo, upper])
        got(f"yfL{l}", y_all.at[l, xo, lower])
        gate_up(l, (xo, x))

    def down(l, xx):
        part[xx] = dot(m_buf[xx], wd_w[l])

    def near(l):
        d_ready(l)
        if l:
            drain([f"{name}{l - 1}" for name in ("eR1", "eL1", "eR2", "eL2", "eR3", "eL3")])
        down(l, xr)
        send(f"eR2{l}", [(part.at[xr, lower], r_f.at[l, 0, lower])], right)
        down(l, xl)
        send(f"eL2{l}", [(part.at[xl, upper], r_f.at[l, 1, upper])], left)

    def far(l):
        down(l, xo)
        send(f"eR1{l}", [(part.at[xo, upper], r_t.at[l, 0])], right)
        send(f"eL1{l}", [(part.at[xo, lower], r_t.at[l, 1])], left)

    def er(l):
        got(f"eR1{l}", r_t.at[l, 0])
        part[xr, 0:r2] = part[xr, 0:r2] + r_t[l, 0]
        send(f"eR3{l}", [(part.at[xr, upper], r_f.at[l, 0, upper])], right)
        got(f"eL1{l}", r_t.at[l, 1])
        part[xl, r2:rows] = part[xl, r2:rows] + r_t[l, 1]
        send(f"eL3{l}", [(part.at[xl, lower], r_f.at[l, 1, lower])], left)

    def own(l):
        down(l, x)

    def done(l):
        got(f"eR2{l}", r_f.at[l, 0, lower])
        got(f"eL2{l}", r_f.at[l, 1, upper])
        got(f"eR3{l}", r_f.at[l, 0, upper])
        got(f"eL3{l}", r_f.at[l, 1, lower])
        hid_next = (hbuf[...].astype(F32) + (part[x] + r_f[l, 0] + r_f[l, 1])).astype(BF16)
        if l + 1 < layers:
            hbuf[...] = hid_next
        else:
            out_ref[...] = hid_next

    table = dict(
        ao=ao, af=af, ax=ax, aw=aw, bo=bo, bf=bf, bx=bx, bw=bw, cd=cd, ct=ct, cf=cf, cn=cn, cx=cx, cw=cw, dt=dt,
        qkv=qkv, mix=mix, yf=yf, gua=gua, gub=gub, near=near, far=far, er=er, own=own, done=done,
    )

    def run(step):
        table[step[:-1]](int(step[-1]))

    entry()
    at = 0
    reached = [0] * layers
    while at < len(ORDER):
        step = ORDER[at]
        if not step.startswith("att"):
            run(step)
            at += 1
            continue
        l, count = int(step[-1]), 0
        while ORDER[at] == step:
            count += 1
            at += 1
        first = reached[l]
        reached[l] += count

        @pl.loop(first, first + count)
        def _(group):
            attend(l, group)

    drain(list(pending))
    assert len(msg_ids) <= send_sem.shape[0]


def decode(hidden, positions, k_cache, v_cache, attn_norm, w_query, w_key, w_value, w_out, mlp_norm, w_gate, w_up, w_down):
    layers, rows, _, cache_len, head_dim = k_cache.shape
    width = hidden.shape[1]
    n_dev = lax.axis_size("w")
    ff = w_gate.shape[-1]
    heads = w_query.shape[-1] // head_dim
    chip_cols = ff // CHIPS
    win = -(-(chip_cols + LANES // 2) // LANES) * LANES
    piece = width // n_dev
    groups = rows // SEQ_GROUP
    assert n_dev == CHIPS * CORES and heads * SEQ_GROUP == LANES and cache_len == LANES and rows == LANES
    assert lax.axis_size("dp") % 2 == 0
    cos_tab, sin_tab = rope_tables(positions, head_dim)
    dims = (layers, rows, width, heads, head_dim, cache_len, n_dev, ff)
    vmem, anym = pl.BlockSpec(memory_space=pltpu.VMEM), pl.BlockSpec(memory_space=pl.ANY)
    new_shape = jax.ShapeDtypeStruct((layers, rows, head_dim), F32)
    n_msg = 96
    return pl.pallas_call(
        functools.partial(decode_kernel, dims),
        out_shape=(jax.ShapeDtypeStruct(hidden.shape, BF16), new_shape, new_shape),
        in_specs=[vmem] * 6 + [anym] * 9,
        out_specs=(vmem,) * 3,
        scratch_shapes=[
            pltpu.VMEM((8, 2 * LANES), F32),
            pltpu.VMEM((n_dev, 8, 2 * LANES), F32),
            pltpu.VMEM((groups, 1, LANES), jnp.int32),
            pltpu.VMEM((layers, 2, CHIPS, CORES, piece, w_query.shape[-1] // 2 + head_dim), BF16),
            pltpu.VMEM((layers, CHIPS, CORES, w_out.shape[1], width), BF16),
            pltpu.VMEM((layers, 2, CHIPS, CORES, piece, win), BF16),
            pltpu.VMEM((layers, win, width), BF16),
            pltpu.VMEM((layers, 2, piece, win // 2), BF16),
            pltpu.VMEM((layers, CHIPS, rows, width), BF16),
            pltpu.VMEM((CHIPS, rows, win), BF16),
            pltpu.VMEM((CHIPS, rows, width), F32),
            pltpu.VMEM((layers, 2, rows // 2, width), F32),
            pltpu.VMEM((layers, 2, rows, width), F32),
            pltpu.VMEM((2, SEQ_GROUP, cache_len, head_dim), BF16),
            pltpu.VMEM((2, SEQ_GROUP, cache_len, head_dim), BF16),
            pltpu.VMEM((heads, rows, head_dim), BF16),
            pltpu.VMEM((rows, heads * head_dim), BF16),
            pltpu.VMEM((rows, width), BF16),
            pltpu.SemaphoreType.DMA((n_msg,)),
            pltpu.SemaphoreType.DMA((n_msg,)),
            pltpu.SemaphoreType.DMA((4 * layers,)),
            pltpu.SemaphoreType.DMA((2, 2)),
        ],
        compiler_params=pltpu.CompilerParams(collective_id=0, has_side_effects=True, vmem_limit_bytes=67043328),
        name="decode",
    )(hidden, cos_tab, sin_tab, attn_norm, mlp_norm, positions.reshape(1, rows), k_cache, v_cache, w_query, w_key, w_value, w_out, w_gate, w_up, w_down)


TILE_ROWS = 16
CACHE_BLOCK = 32
CACHE_SLOTS = 6


def cache_kernel(pos_ref, kc_ref, vc_ref, kn_ref, vn_ref, ko_ref, vo_ref, buf, in_sem, out_sem):
    layers, rows = kc_ref.shape[:2]
    blocks = rows // CACHE_BLOCK
    steps = [(src, new, dst, l, b) for l in range(layers) for src, new, dst in ((kc_ref, kn_ref, ko_ref), (vc_ref, vn_ref, vo_ref)) for b in range(blocks)]

    def load(i):
        src, _, _, l, b = steps[i]
        slot = i % CACHE_SLOTS
        return pltpu.make_async_copy(src.at[l, pl.ds(b * CACHE_BLOCK, CACHE_BLOCK), 0], buf.at[slot], in_sem.at[slot])

    def store(i):
        _, _, dst, l, b = steps[i]
        slot = i % CACHE_SLOTS
        return pltpu.make_async_copy(buf.at[slot], dst.at[l, pl.ds(b * CACHE_BLOCK, CACHE_BLOCK), 0], out_sem.at[slot])

    ahead = CACHE_SLOTS // 2
    for i in range(ahead):
        load(i).start()
    row = lax.broadcasted_iota(jnp.int32, (TILE_ROWS, buf.shape[-1]), 0)
    for i in range(len(steps)):
        load(i).wait()
        _, new, _, l, b = steps[i]
        slot = i % CACHE_SLOTS

        @pl.loop(0, CACHE_BLOCK)
        def _(s):
            pos = pos_ref[b * CACHE_BLOCK + s]
            base = pl.multiple_of(pos // TILE_ROWS * TILE_ROWS, TILE_ROWS)
            tile = buf[slot, s, pl.ds(base, TILE_ROWS), :].astype(F32)
            fresh = new[l, pl.ds(b * CACHE_BLOCK + s, 1), :]
            buf[slot, s, pl.ds(base, TILE_ROWS), :] = jnp.where(row == pos - base, fresh, tile).astype(BF16)

        store(i).start()
        nxt = i + ahead
        if nxt < len(steps):
            if nxt >= CACHE_SLOTS:
                store(nxt - CACHE_SLOTS).wait()
            load(nxt).start()
    for i in range(max(0, len(steps) - CACHE_SLOTS), len(steps)):
        store(i).wait()


def write_caches(positions, k_cache, v_cache, k_new, v_new):
    cache_len, head_dim = k_cache.shape[-2:]
    vmem, anym = pl.BlockSpec(memory_space=pltpu.VMEM), pl.BlockSpec(memory_space=pl.ANY)
    shape = jax.ShapeDtypeStruct(k_cache.shape, BF16)
    return pl.pallas_call(
        cache_kernel,
        out_shape=(shape, shape),
        in_specs=[pl.BlockSpec(memory_space=pltpu.SMEM), anym, anym, vmem, vmem],
        out_specs=(anym, anym),
        scratch_shapes=[
            pltpu.VMEM((CACHE_SLOTS, CACHE_BLOCK, cache_len, head_dim), BF16),
            pltpu.SemaphoreType.DMA((CACHE_SLOTS,)),
            pltpu.SemaphoreType.DMA((CACHE_SLOTS,)),
        ],
        compiler_params=pltpu.CompilerParams(vmem_limit_bytes=60 * 2**20),
        name="caches",
    )(positions, k_cache, v_cache, k_new, v_new)


def solution(mesh):
    batch_spec = P(("dp", "w"))
    cache_spec = P(None, ("dp", "w"))
    gain_spec = P(None, "w")
    weight_spec = P(None, "w", None)

    def per_device(hidden, positions, k_cache, v_cache, *weights):
        hidden_out, k_new, v_new = decode(hidden, positions, k_cache, v_cache, *weights)
        k_out, v_out = write_caches(positions, k_cache, v_cache, k_new, v_new)
        return hidden_out, k_out, v_out

    in_specs = (batch_spec, batch_spec, cache_spec, cache_spec, gain_spec, weight_spec, weight_spec, weight_spec, weight_spec, gain_spec, weight_spec, weight_spec, weight_spec)
    out_specs = (batch_spec, cache_spec, cache_spec)
    return jax.shard_map(per_device, mesh=mesh, in_specs=in_specs, out_specs=out_specs, check_vma=False)
```

time: 227 us -> 186 us (0.82)
  Pallas kernels: 216 us -> 183 us
  other arithmetic: 5.58 us -> 1.64 us
  local copies, waits for them, and re-layouts: 4.1 us -> 0.72 us
    pallas_call x1, Pallas kernels: 189 us -> 158 us  [decode(): pl.pallas_call(functools.partial(decode_kernel, dims), out_shape=(jax.Sha...]
    convert_element_type x2 -> x0, other arithmetic: 3.24 us -> none  [the longest x1 1.63 us: write_caches(): k_new.astype(F32)]
    pallas_call x1, Pallas kernels: 26.9 us -> 24.4 us  [write_caches(): pl.pallas_call(cache_kernel, out_shape=(shape, shape), in_specs=[pl.Block...]
where the time goes in v2:
time: 186 us
  Pallas kernels  183 us (98%)
    pallas_call x1, Pallas kernels, decode(): pl.pallas_call(functools.partial(decode_kernel, dims), out_shape=(jax.Sha...  158 us
    pallas_call x1, Pallas kernels, write_caches(): pl.pallas_call(cache_kernel, out_shape=(shape, shape), in_specs=[pl.Block...  24.4 us

profile of v2, /device:TPU:112, one launch (start us, length us, event | category | flops | bytes accessed | tf_op | source)
XLA Modules:
  0.0 185.8 jit_solution(4031512821862545760)
XLA Ops:
  0.6 0.7 convert_element_type.3
  1.3 1.0 multiply_sine_fusion
  2.3 158.3 %decode.1 = (bf16[128,1152]{1,0:T(8,128)(2,1)}, f32[2,128,256]{2,1,0:T(8,128)}, f32[2,128,256]{2,1,0:T(8,128)}) custom-call(bf16[128,1152]{1,0:T(8,128)(2,1)} %hid_ref.1, f32[128,128]{1,0:T(8,128)} %get-tuple-element.14.cos_ref, f32[128,128]{1,0:T(8,128)} %get-tuple-element.13.sin_ref, f32[2,144]{1,0:T(2,128)} %an_ref.1, f32[2,144]{1,0:T(2,128)} %mn_ref.1, ...), custom_call_target="tpu_custom_call" | custom-call | tf_op jit(solution)/shard_map/decode/pallas_call | solution.py:532
  160.6 0.0 copy-start
  160.6 24.4 %caches.1 = (bf16[2,128,1,128,256]{4,3,2,1,0:T(8,128)(2,1)}, bf16[2,128,1,128,256]{4,3,2,1,0:T(8,128)(2,1)}) custom-call(s32[128]{0:T(128)} %pos_ref.1, bf16[2,128,1,128,256]{4,3,2,1,0:T(8,128)(2,1)} %kc_ref.3, bf16[2,128,1,128,256]{4,3,2,1,0:T(8,128)(2,1)} %vc_ref.3, f32[2,128,256]{2,1,0:T(8,128)} %get-tuple-element.9.kn_ref, ...), custom_call_target="tpu_custom_call" | custom-call | tf_op jit(solution)/shard_map/caches/pallas_call | solution.py:617
  185.1 0.0 copy-done
  185.1 0.7 copy.17
  (1 shorter events, 0.0 us)
Async XLA Ops:
  160.6 24.4 %copy-start = (bf16[128,1152]{1,0:T(8,128)(2,1)S(1)}, bf16[128,1152]{1,0:T(8,128)(2,1)}, u32[]{:S(2)}) copy-start(bf16[128,1152]{1,0:T(8,128)(2,1)} %get-tuple-element.18) | copy-start | bytes 884740

commit v3 on v2

--- a/solution.py
+++ b/solution.py
@@ -35,9 +35,9 @@
 
 ORDER = (
     "bo0", "ao0", "ct0", "bf0", "af0", "cf0", "cd0", "ct1", "bx0", "ax0", "cx0", "aw0", "dt0", "qkv0",
-    "att0", "bw0", "ao1", "att0", "att0", "cd1", "cn0", "af1", "att0", "mix0", "yf0", "cf1", "cw0", "ax1", "dt1",
-    "gua0", "near0", "cn1", "gub0", "far0", "bo1", "er0", "own0", "bf1", "aw1", "cx1", "done0", "qkv1",
-    "att1", "att1", "bx1", "att1", "att1", "mix1", "cw1", "yf1", "gua1", "near1", "gub1", "far1", "er1", "own1", "done1",
+    "att0", "bw0", "ao1", "att0", "att0", "cd1", "cn0", "af1", "att0", "mix0", "yf0", "cf1", "cw0", "ax1", "dt1", "dr0",
+    "gua0", "near0", "cn1", "gub0", "far0", "bo1", "er0", "guo0", "own0", "bf1", "aw1", "cx1", "done0", "qkv1",
+    "att1", "att1", "bx1", "att1", "att1", "mix1", "cw1", "yf1", "guo1", "dr1", "own1", "gua1", "near1", "gub1", "far1",
 )
 SHARE_A = (True, True)
 SHARE_B = (True, False)
@@ -47,10 +47,10 @@
     dims,
     hid_ref, cos_ref, sin_ref, an_ref, mn_ref, pos_ref, kc_ref, vc_ref,
     wq_ref, wk_ref, wv_ref, wo_ref, wg_ref, wu_ref, wd_ref,
-    out_ref, knew_ref, vnew_ref,
+    hid_out, knew_ref, vnew_ref, far_r, far_l, near_r, near_l, next_r, next_l, own_out,
     gsrc, gbuf, pos_buf, abuf_w, bbuf_w, gu_w, wd_w, tr_w, y_all, m_buf, part, r_t, r_f,
     kbuf, vbuf, qbuf, abuf, hbuf,
-    send_sem, recv_sem, loc_sem, kv_sem,
+    send_sem, recv_sem, loc_sem, kv_sem, out_sem,
 ):
     layers, rows, width, heads, head_dim, cache_len, n_dev, ff = dims
     half = head_dim // 2
@@ -430,33 +430,60 @@
             for k, b in enumerate(blocks):
                 m_buf[b, :, cols] = mid[k * rows:(k + 1) * rows]
 
+    def guo(l):
+        if l:
+            c_ready(l)
+        gate_up(l, (x,))
+
     def gua(l):
         got(f"yR2{l}", y_all.at[l, xl, lower])
         got(f"yL2{l}", y_all.at[l, xr, upper])
-        c_ready(l)
+        if not l:
+            c_ready(l)
         gate_up(l, (xl, xr))
 
     def gub(l):
         got(f"yfR{l}", y_all.at[l, xo, upper])
         got(f"yfL{l}", y_all.at[l, xo, lower])
-        gate_up(l, (xo, x))
+        gate_up(l, (xo,))
 
     def down(l, xx):
         part[xx] = dot(m_buf[xx], wd_w[l])
 
+    last = layers - 1
+
+    def export(src, dst):
+        pltpu.make_async_copy(src, dst, out_sem.at[len(exports)]).start()
+        exports.append((src, dst))
+
+    exports = []
+
     def near(l):
-        d_ready(l)
         if l:
-            drain([f"{name}{l - 1}" for name in ("eR1", "eL1", "eR2", "eL2", "eR3", "eL3")])
+            drain([f"{name}{l - 1}" for name in ("eR2", "eL2", "eR3", "eL3")])
         down(l, xr)
-        send(f"eR2{l}", [(part.at[xr, lower], r_f.at[l, 0, lower])], right)
+        if l == last:
+            export(part.at[xr, lower], near_r)
+            export(part.at[xr, upper], next_r)
+        else:
+            send(f"eR2{l}", [(part.at[xr, lower], r_f.at[l, 0, lower])], right)
         down(l, xl)
-        send(f"eL2{l}", [(part.at[xl, upper], r_f.at[l, 1, upper])], left)
+        if l == last:
+            export(part.at[xl, upper], near_l)
+            export(part.at[xl, lower], next_l)
+        else:
+            send(f"eL2{l}", [(part.at[xl, upper], r_f.at[l, 1, upper])], left)
 
     def far(l):
+        if l:
+            drain([f"{name}{l - 1}" for name in ("eR1", "eL1")])
         down(l, xo)
-        send(f"eR1{l}", [(part.at[xo, upper], r_t.at[l, 0])], right)
-        send(f"eL1{l}", [(part.at[xo, lower], r_t.at[l, 1])], left)
+        if l == last:
+            export(part.at[xo, upper], far_r)
+            export(part.at[xo, lower], far_l)
+        else:
+            send(f"eR1{l}", [(part.at[xo, upper], r_t.at[l, 0])], right)
+            send(f"eL1{l}", [(part.at[xo, lower], r_t.at[l, 1])], left)
 
     def er(l):
         got(f"eR1{l}", r_t.at[l, 0])
@@ -468,21 +495,20 @@
 
     def own(l):
         down(l, x)
+        if l == last:
+            export(part.at[x], own_out)
+            hid_out[...] = hbuf[...]
 
     def done(l):
         got(f"eR2{l}", r_f.at[l, 0, lower])
         got(f"eL2{l}", r_f.at[l, 1, upper])
         got(f"eR3{l}", r_f.at[l, 0, upper])
         got(f"eL3{l}", r_f.at[l, 1, lower])
-        hid_next = (hbuf[...].astype(F32) + (part[x] + r_f[l, 0] + r_f[l, 1])).astype(BF16)
-        if l + 1 < layers:
-            hbuf[...] = hid_next
-        else:
-            out_ref[...] = hid_next
+        hbuf[...] = (hbuf[...].astype(F32) + (part[x] + r_f[l, 0] + r_f[l, 1])).astype(BF16)
 
     table = dict(
         ao=ao, af=af, ax=ax, aw=aw, bo=bo, bf=bf, bx=bx, bw=bw, cd=cd, ct=ct, cf=cf, cn=cn, cx=cx, cw=cw, dt=dt,
-        qkv=qkv, mix=mix, yf=yf, gua=gua, gub=gub, near=near, far=far, er=er, own=own, done=done,
+        qkv=qkv, mix=mix, yf=yf, guo=guo, gua=gua, gub=gub, dr=d_ready, near=near, far=far, er=er, own=own, done=done,
     )
 
     def run(step):
@@ -509,6 +535,8 @@
             attend(l, group)
 
     drain(list(pending))
+    for i, (src, dst) in enumerate(exports):
+        pltpu.make_async_copy(src, dst, out_sem.at[i]).wait()
     assert len(msg_ids) <= send_sem.shape[0]
 
 
@@ -528,12 +556,13 @@
     dims = (layers, rows, width, heads, head_dim, cache_len, n_dev, ff)
     vmem, anym = pl.BlockSpec(memory_space=pltpu.VMEM), pl.BlockSpec(memory_space=pl.ANY)
     new_shape = jax.ShapeDtypeStruct((layers, rows, head_dim), F32)
+    half_sum = jax.ShapeDtypeStruct((rows // 2, width), F32)
     n_msg = 96
     return pl.pallas_call(
         functools.partial(decode_kernel, dims),
-        out_shape=(jax.ShapeDtypeStruct(hidden.shape, BF16), new_shape, new_shape),
+        out_shape=(jax.ShapeDtypeStruct(hidden.shape, BF16), new_shape, new_shape) + (half_sum,) * 6 + (jax.ShapeDtypeStruct(hidden.shape, F32),),
         in_specs=[vmem] * 6 + [anym] * 9,
-        out_specs=(vmem,) * 3,
+        out_specs=(vmem,) * 3 + (anym,) * 7,
         scratch_shapes=[
             pltpu.VMEM((8, 2 * LANES), F32),
             pltpu.VMEM((n_dev, 8, 2 * LANES), F32),
@@ -546,8 +575,8 @@
             pltpu.VMEM((layers, CHIPS, rows, width), BF16),
             pltpu.VMEM((CHIPS, rows, win), BF16),
             pltpu.VMEM((CHIPS, rows, width), F32),
-            pltpu.VMEM((layers, 2, rows // 2, width), F32),
-            pltpu.VMEM((layers, 2, rows, width), F32),
+            pltpu.VMEM((layers - 1, 2, rows // 2, width), F32),
+            pltpu.VMEM((layers - 1, 2, rows, width), F32),
             pltpu.VMEM((2, SEQ_GROUP, cache_len, head_dim), BF16),
             pltpu.VMEM((2, SEQ_GROUP, cache_len, head_dim), BF16),
             pltpu.VMEM((heads, rows, head_dim), BF16),
@@ -557,6 +586,7 @@
             pltpu.SemaphoreType.DMA((n_msg,)),
             pltpu.SemaphoreType.DMA((4 * layers,)),
             pltpu.SemaphoreType.DMA((2, 2)),
+            pltpu.SemaphoreType.DMA((7,)),
         ],
         compiler_params=pltpu.CompilerParams(collective_id=0, has_side_effects=True, vmem_limit_bytes=67043328),
         name="decode",
@@ -568,20 +598,20 @@
 CACHE_SLOTS = 6
 
 
-def cache_kernel(pos_ref, kc_ref, vc_ref, kn_ref, vn_ref, ko_ref, vo_ref, buf, in_sem, out_sem):
-    layers, rows = kc_ref.shape[:2]
+def cache_kernel(pos_ref, old_ref, new_ref, out_ref, buf, in_sem, out_sem):
+    layers, rows = old_ref.shape[:2]
     blocks = rows // CACHE_BLOCK
-    steps = [(src, new, dst, l, b) for l in range(layers) for src, new, dst in ((kc_ref, kn_ref, ko_ref), (vc_ref, vn_ref, vo_ref)) for b in range(blocks)]
+    steps = [(l, b) for l in range(layers) for b in range(blocks)]
 
     def load(i):
-        src, _, _, l, b = steps[i]
+        l, b = steps[i]
         slot = i % CACHE_SLOTS
-        return pltpu.make_async_copy(src.at[l, pl.ds(b * CACHE_BLOCK, CACHE_BLOCK), 0], buf.at[slot], in_sem.at[slot])
+        return pltpu.make_async_copy(old_ref.at[l, pl.ds(b * CACHE_BLOCK, CACHE_BLOCK), 0], buf.at[slot], in_sem.at[slot])
 
     def store(i):
-        _, _, dst, l, b = steps[i]
+        l, b = steps[i]
         slot = i % CACHE_SLOTS
-        return pltpu.make_async_copy(buf.at[slot], dst.at[l, pl.ds(b * CACHE_BLOCK, CACHE_BLOCK), 0], out_sem.at[slot])
+        return pltpu.make_async_copy(buf.at[slot], out_ref.at[l, pl.ds(b * CACHE_BLOCK, CACHE_BLOCK), 0], out_sem.at[slot])
 
     ahead = CACHE_SLOTS // 2
     for i in range(ahead):
@@ -589,7 +619,7 @@
     row = lax.broadcasted_iota(jnp.int32, (TILE_ROWS, buf.shape[-1]), 0)
     for i in range(len(steps)):
         load(i).wait()
-        _, new, _, l, b = steps[i]
+        l, b = steps[i]
         slot = i % CACHE_SLOTS
 
         @pl.loop(0, CACHE_BLOCK)
@@ -597,7 +627,7 @@
             pos = pos_ref[b * CACHE_BLOCK + s]
             base = pl.multiple_of(pos // TILE_ROWS * TILE_ROWS, TILE_ROWS)
             tile = buf[slot, s, pl.ds(base, TILE_ROWS), :].astype(F32)
-            fresh = new[l, pl.ds(b * CACHE_BLOCK + s, 1), :]
+            fresh = new_ref[l, pl.ds(b * CACHE_BLOCK + s, 1), :]
             buf[slot, s, pl.ds(base, TILE_ROWS), :] = jnp.where(row == pos - base, fresh, tile).astype(BF16)
 
         store(i).start()
@@ -610,23 +640,23 @@
         store(i).wait()
 
 
-def write_caches(positions, k_cache, v_cache, k_new, v_new):
-    cache_len, head_dim = k_cache.shape[-2:]
+def write_cache(positions, cache, new_rows):
+    cache_len, head_dim = cache.shape[-2:]
     vmem, anym = pl.BlockSpec(memory_space=pltpu.VMEM), pl.BlockSpec(memory_space=pl.ANY)
-    shape = jax.ShapeDtypeStruct(k_cache.shape, BF16)
     return pl.pallas_call(
         cache_kernel,
-        out_shape=(shape, shape),
-        in_specs=[pl.BlockSpec(memory_space=pltpu.SMEM), anym, anym, vmem, vmem],
-        out_specs=(anym, anym),
+        out_shape=jax.ShapeDtypeStruct(cache.shape, BF16),
+        in_specs=[pl.BlockSpec(memory_space=pltpu.SMEM), anym, vmem],
+        out_specs=anym,
         scratch_shapes=[
             pltpu.VMEM((CACHE_SLOTS, CACHE_BLOCK, cache_len, head_dim), BF16),
             pltpu.SemaphoreType.DMA((CACHE_SLOTS,)),
             pltpu.SemaphoreType.DMA((CACHE_SLOTS,)),
         ],
+        cost_estimate=pl.CostEstimate(flops=10**11, bytes_accessed=4 * cache.size, transcendentals=0),
         compiler_params=pltpu.CompilerParams(vmem_limit_bytes=60 * 2**20),
-        name="caches",
-    )(positions, k_cache, v_cache, k_new, v_new)
+        name="cache",
+    )(positions, cache, new_rows)
 
 
 def solution(mesh):
@@ -636,8 +666,20 @@
     weight_spec = P(None, "w", None)
 
     def per_device(hidden, positions, k_cache, v_cache, *weights):
-        hidden_out, k_new, v_new = decode(hidden, positions, k_cache, v_cache, *weights)
-        k_out, v_out = write_caches(positions, k_cache, v_cache, k_new, v_new)
+        hid_mid, k_new, v_new, far_r, far_l, near_r, near_l, next_r, next_l, own = decode(hidden, positions, k_cache, v_cache, *weights)
+        n_dev = mesh.shape["w"]
+        ahead = [(i, (i + CORES) % n_dev) for i in range(n_dev)]
+        back = [(i, (i - CORES) % n_dev) for i in range(n_dev)]
+        got_r = lax.ppermute(far_r, "w", ahead)
+        got_l = lax.ppermute(far_l, "w", back)
+        low = lax.ppermute(near_r, "w", ahead)
+        high = lax.ppermute(near_l, "w", back)
+        k_out = write_cache(positions, k_cache, k_new)
+        far_high = lax.ppermute(next_r + got_r, "w", ahead)
+        far_low = lax.ppermute(next_l + got_l, "w", back)
+        v_out = write_cache(positions, v_cache, v_new)
+        total = own + jnp.concatenate([high + far_high, low + far_low], axis=0)
+        hidden_out = (hid_mid.astype(F32) + total).astype(BF16)
         return hidden_out, k_out, v_out
 
     in_specs = (batch_spec, batch_spec, cache_spec, cache_spec, gain_spec, weight_spec, weight_spec, weight_spec, weight_spec, gain_spec, weight_spec, weight_spec, weight_spec)

time: 186 us -> 183 us (0.984)
  Pallas kernels: 183 us -> 168 us
  starting transfers between devices: 0 us -> 9.59 us
  other arithmetic: 1.64 us -> 4.48 us
    pallas_call x1, Pallas kernels: 158 us -> 140 us  [decode(): pl.pallas_call(functools.partial(decode_kernel, dims), out_shape=(jax.Sha...]
    ppermute x0 -> x6, starting transfers between devices: none -> 9.59 us  [the longest x1 3.27 us: per_device(): far_low = lax.ppermute(next_l + got_l, 'w', back)]
    pallas_call x1 -> x2, Pallas kernels: 24.4 us -> 27.2 us  [write_cache(): pl.pallas_call(cache_kernel, out_shape=jax.ShapeDtypeStruct(cache.shape,...]
    add x0 -> x4, other arithmetic: none -> 2.05 us  [the longest x2 1.99 us: per_device(): total = own + jnp.concatenate([high + far_high, low + far_low], axis=0)]
  transfers between devices with their start and end apart: 0 -> 6, of which waited for: 0 -> 0; matrix products, arithmetic and copies ran while one was open for 0% -> 1% of each run, Pallas kernels for 0% -> 15%
where the time goes in v3:
time: 183 us; the launch traced here: 182 us
  Pallas kernels  168 us (92%)
  starting transfers between devices  9.59 us (5%)
  other arithmetic  4.48 us (2%)
    pallas_call x1, Pallas kernels, decode(): pl.pallas_call(functools.partial(decode_kernel, dims), out_shape=(jax.Sha...  140 us
    pallas_call x2, Pallas kernels, write_cache(): pl.pallas_call(cache_kernel, out_shape=jax.ShapeDtypeStruct(cache.shape,...  27.2 us
  transfers between devices with their start and end apart: 6, of which 0 were waited for; matrix products, arithmetic and copies ran while one was open for 1% of the time, Pallas kernels for 15%

profile of v3, /device:TPU:112, one launch (start us, length us, event | category | flops | bytes accessed | tf_op | source)
XLA Modules:
  0.0 182.5 jit_solution(8523861523359879701)
XLA Ops:
  0.6 0.7 convert_element_type.9
  1.3 1.0 multiply_sine_fusion
  2.3 140.4 %decode.1 = (bf16[128,1152]{1,0:T(8,128)(2,1)}, f32[2,128,256]{2,1,0:T(8,128)}, f32[2,128,256]{2,1,0:T(8,128)}, f32[64,1152]{1,0:T(8,128)}, f32[64,1152]{1,0:T(8...) custom-call(bf16[128,1152]{1,0:T(8,128)(2,1)} %hid_ref.1, ...), custom_call_target="tpu_custom_call" | custom-call | tf_op jit(solution)/shard_map/decode/pallas_call | solution.py:561
  142.7 3.0 %collective-permute-start = (f32[64,1152]{1,0:T(8,128)}, f32[64,1152]{1,0:T(8,128)}, u32[]{:S(2)}, u32[]{:S(2)}) collective-permute-start(f32[64,1152]{1,0:T(8,128)} %get-tuple-element.15), channel_id=1, source_target_pairs={{0,6},{1,7},{2,0},{3,1},{4,2},{5,3},{6,4},{7,5},{8,14},{9,15},{10,... | collective-permute-start | bytes 884744 | tf_op jit(solution)/shard_map/ppermute | solution.py:676
  145.7 0.0 collective-permute-start.1
  145.7 0.3 collective-permute-start.3
  146.0 2.9 %collective-permute-start.4 = (f32[64,1152]{1,0:T(8,128)}, f32[64,1152]{1,0:T(8,128)S(1)}, u32[]{:S(2)}, u32[]{:S(2)}) collective-permute-start(f32[64,1152]{1,0:T(8,128)} %get-tuple-element.20), channel_id=1, source_target_pairs={{0,6},{1,7},{2,0},{3,1},{4,2},{5,3},{6,4},{7,5},{8,14},{9,15},{10,... | collective-permute-start | bytes 884744 | tf_op jit(solution)/shard_map/ppermute | solution.py:674
  148.9 0.0 copy-start.3
  148.9 0.0 copy-start.2
  148.9 13.6 %cache.2 = bf16[2,128,1,128,256]{4,3,2,1,0:T(8,128)(2,1)} custom-call(s32[128]{0:T(128)} %pos_ref.3, bf16[2,128,1,128,256]{4,3,2,1,0:T(8,128)(2,1)} %old_ref.2, f32[2,128,256]{2,1,0:T(8,128)} %get-tuple-element.21.new_ref), custom_call_target="tpu_custom_call" | custom-call | flops 99999997952 | bytes 33554432 | tf_op jit(solution)/shard_map/cache/pallas_call | solution.py:646
  162.5 0.0 collective-permute-done.1
  162.5 0.0 copy-done.3
  162.6 0.1 collective-permute-start.2
  162.7 0.0 collective-permute-done.4
  162.7 0.0 copy-done.2
  162.8 3.3 %collective-permute-start.5 = (f32[64,1152]{1,0:T(8,128)S(1)}, f32[64,1152]{1,0:T(8,128)S(1)}, u32[]{:S(2)}, u32[]{:S(2)}) collective-permute-start(f32[64,1152]{1,0:T(8,128)S(1)} %add.20), channel_id=1, source_target_pairs={{0,6},{1,7},{2,0},{3,1},{4,2},{5,3},{6,4},{7,5},{8,14},{9,15},{10,... | collective-permute-start | bytes 884744 | tf_op jit(solution)/shard_map/ppermute | solution.py:679
  166.0 0.0 copy-start
  166.0 0.0 copy-start.1
  166.0 13.6 %cache.3 = bf16[2,128,1,128,256]{4,3,2,1,0:T(8,128)(2,1)} custom-call(s32[128]{0:T(128)} %pos_ref.3, bf16[2,128,1,128,256]{4,3,2,1,0:T(8,128)(2,1)} %old_ref.3, f32[2,128,256]{2,1,0:T(8,128)} %get-tuple-element.22.new_ref), custom_call_target="tpu_custom_call" | custom-call | flops 99999997952 | bytes 33554432 | tf_op jit(solution)/shard_map/cache/pallas_call | solution.py:646
  179.6 0.0 collective-permute-done
  179.7 0.0 collective-permute-done.2
  179.7 1.0 add.19
  180.7 0.0 collective-permute-done.3
  180.7 0.0 collective-permute-done.5
  180.7 1.0 add.21
  181.7 0.0 copy-done
  181.7 0.0 copy-done.1
  181.7 0.8 fusion.1
  (3 shorter events, 0.1 us)
Async XLA Ops:
  142.7 36.9 %collective-permute-start = (f32[64,1152]{1,0:T(8,128)}, f32[64,1152]{1,0:T(8,128)}, u32[]{:S(2)}, u32[]{:S(2)}) collective-permute-start(f32[64,1152]{1,0:T(8,128)} %get-tuple-element.15), channel_id=1, source_target_pairs={{0,6},{1,7},{2,0},{3,1},{4,2},{5,3},{6,4},{7,5},{8,14},{9,15},{10,... | collective-permute-start | bytes 884744 | tf_op jit(solution)/shard_map/ppermute | solution.py:676
  145.7 16.9 %collective-permute-start.1 = (f32[64,1152]{1,0:T(8,128)}, f32[64,1152]{1,0:T(8,128)S(1)}, u32[]{:S(2)}, u32[]{:S(2)}) collective-permute-start(f32[64,1152]{1,0:T(8,128)} %get-tuple-element.17), channel_id=1, source_target_pairs={{0,2},{1,3},{2,4},{3,5},{4,6},{5,7},{6,0},{7,1},{8,10},{9,11},{10,... | collective-permute-start | bytes 884744 | tf_op jit(solution)/shard_map/ppermute | solution.py:673
  145.7 35.0 %collective-permute-start.3 = (f32[64,1152]{1,0:T(8,128)}, f32[64,1152]{1,0:T(8,128)}, u32[]{:S(2)}, u32[]{:S(2)}) collective-permute-start(f32[64,1152]{1,0:T(8,128)} %get-tuple-element.18), channel_id=1, source_target_pairs={{0,2},{1,3},{2,4},{3,5},{4,6},{5,7},{6,0},{7,1},{8,10},{9,11},{10,... | collective-permute-start | bytes 884744 | tf_op jit(solution)/shard_map/ppermute | solution.py:675
  146.0 16.7 %collective-permute-start.4 = (f32[64,1152]{1,0:T(8,128)}, f32[64,1152]{1,0:T(8,128)S(1)}, u32[]{:S(2)}, u32[]{:S(2)}) collective-permute-start(f32[64,1152]{1,0:T(8,128)} %get-tuple-element.20), channel_id=1, source_target_pairs={{0,6},{1,7},{2,0},{3,1},{4,2},{5,3},{6,4},{7,5},{8,14},{9,15},{10,... | collective-permute-start | bytes 884744 | tf_op jit(solution)/shard_map/ppermute | solution.py:674
  148.9 13.6 %copy-start.3 = (f32[64,1152]{1,0:T(8,128)S(1)}, f32[64,1152]{1,0:T(8,128)}, u32[]{:S(2)}) copy-start(f32[64,1152]{1,0:T(8,128)} %get-tuple-element.16) | copy-start | bytes 884740
  148.9 13.8 %copy-start.2 = (f32[64,1152]{1,0:T(8,128)S(1)}, f32[64,1152]{1,0:T(8,128)}, u32[]{:S(2)}) copy-start(f32[64,1152]{1,0:T(8,128)} %get-tuple-element.19) | copy-start | bytes 884740
  162.6 17.1 %collective-permute-start.2 = (f32[64,1152]{1,0:T(8,128)S(1)}, f32[64,1152]{1,0:T(8,128)S(1)}, u32[]{:S(2)}, u32[]{:S(2)}) collective-permute-start(f32[64,1152]{1,0:T(8,128)S(1)} %add.18), channel_id=1, source_target_pairs={{0,2},{1,3},{2,4},{3,5},{4,6},{5,7},{6,0},{7,1},{8,10},{9,11},{10,... | collective-permute-start | bytes 884744 | tf_op jit(solution)/shard_map/ppermute | solution.py:678
  162.8 17.9 %collective-permute-start.5 = (f32[64,1152]{1,0:T(8,128)S(1)}, f32[64,1152]{1,0:T(8,128)S(1)}, u32[]{:S(2)}, u32[]{:S(2)}) collective-permute-start(f32[64,1152]{1,0:T(8,128)S(1)} %add.20), channel_id=1, source_target_pairs={{0,6},{1,7},{2,0},{3,1},{4,2},{5,3},{6,4},{7,5},{8,14},{9,15},{10,... | collective-permute-start | bytes 884744 | tf_op jit(solution)/shard_map/ppermute | solution.py:679
  166.0 15.7 %copy-start = (f32[128,1152]{1,0:T(8,128)S(1)}, f32[128,1152]{1,0:T(8,128)}, u32[]{:S(2)}) copy-start(f32[128,1152]{1,0:T(8,128)} %get-tuple-element.14) | copy-start | bytes 1769476
  166.0 15.7 %copy-start.1 = (bf16[128,1152]{1,0:T(8,128)(2,1)S(1)}, bf16[128,1152]{1,0:T(8,128)(2,1)}, u32[]{:S(2)}) copy-start(bf16[128,1152]{1,0:T(8,128)(2,1)} %get-tuple-element.13) | copy-start | bytes 884740

commit v4 on v3

--- a/solution.py
+++ b/solution.py
@@ -18,13 +18,6 @@
 BF16 = jnp.bfloat16
 
 
-def rope_tables(positions, head_dim):
-    half_dim = head_dim // 2
-    inv_freq = ROPE_BASE ** (-2.0 * jnp.arange(half_dim, dtype=jnp.float32) / head_dim)
-    angles = positions.astype(jnp.float32)[:, None] * inv_freq[None, :]
-    return jnp.cos(angles), jnp.sin(angles)
-
-
 def dot(a, b):
     return jnp.dot(a, b, preferred_element_type=F32)
 
@@ -45,10 +38,10 @@
 
 def decode_kernel(
     dims,
-    hid_ref, cos_ref, sin_ref, an_ref, mn_ref, pos_ref, kc_ref, vc_ref,
+    hid_ref, freq_ref, an_ref, mn_ref, pos_ref, kc_ref, vc_ref,
     wq_ref, wk_ref, wv_ref, wo_ref, wg_ref, wu_ref, wd_ref,
-    hid_out, knew_ref, vnew_ref, far_r, far_l, near_r, near_l, next_r, next_l, own_out,
-    gsrc, gbuf, pos_buf, abuf_w, bbuf_w, gu_w, wd_w, tr_w, y_all, m_buf, part, r_t, r_f,
+    hid_out, knew_ref, vnew_ref, first_r, first_l, next_r, next_l, own_out,
+    cos_buf, sin_buf, act_buf, gsrc, gbuf, pos_buf, abuf_w, bbuf_w, gu_w, wd_w, tr_w, y_all, m_buf, part, r_t, r_f,
     kbuf, vbuf, qbuf, abuf, hbuf,
     send_sem, recv_sem, loc_sem, kv_sem, out_sem,
 ):
@@ -315,6 +308,9 @@
                 moved = pltpu.roll(pos_ref[...], lax.rem(w * 0 + (j - g + heads) * SEQ_GROUP, LANES), 1)
                 line = jnp.where(lane_block == j, moved, line)
             pos_buf[g] = line
+        angles = jnp.broadcast_to(pos_ref[...].astype(F32), (rows, rows)).T * freq_ref[...]
+        cos_buf[...] = jnp.cos(angles)
+        sin_buf[...] = jnp.sin(angles)
 
     def all_gains():
         tiles = []
@@ -381,7 +377,7 @@
         a_ready(l)
         if l == 0:
             got("gain", gbuf.at[pl.ds(0, n_dev - 1)])
-        cos_tab, sin_tab = cos_ref[...], sin_ref[...]
+        cos_tab, sin_tab = cos_buf[...], sin_buf[...]
         normed = rms(hbuf[...].astype(F32), l)
         halves = [dot(normed, abuf_w[l, hf].reshape(width, a_cols)) for hf in range(2)]
 
@@ -420,15 +416,33 @@
     n_tile = 2 * LANES
 
     def gate_up(l, blocks):
-        @pl.loop(0, win // n_tile)
-        def _(n):
-            cols = pl.ds(pl.multiple_of(n * n_tile, n_tile), n_tile)
+        span = slice(0, len(blocks) * rows)
+
+        def at_tile(n):
+            return pl.ds(pl.multiple_of(n * n_tile, n_tile), n_tile)
+
+        def multiply(n, slot):
             act = jnp.concatenate([y_all[l, b] for b in blocks], axis=0)
-            gate = dot(act, gu_w[l, 0, :, :, :, cols].reshape(width, n_tile))
-            up = dot(act, gu_w[l, 1, :, :, :, cols].reshape(width, n_tile))
-            mid = (jax.nn.gelu(gate, approximate=True) * up).astype(BF16)
+            for k in range(2):
+                act_buf[slot, k, span] = dot(act, gu_w[l, k, :, :, :, at_tile(n)].reshape(width, n_tile))
+
+        def activate(n, slot):
+            mid = (jax.nn.gelu(act_buf[slot, 0, span], approximate=True) * act_buf[slot, 1, span]).astype(BF16)
             for k, b in enumerate(blocks):
-                m_buf[b, :, cols] = mid[k * rows:(k + 1) * rows]
+                m_buf[b, :, at_tile(n)] = mid[k * rows:(k + 1) * rows]
+
+        tiles = win // n_tile
+        assert tiles % 2 == 1
+        multiply(0, 0)
+
+        @pl.loop(0, tiles // 2)
+        def _(k):
+            multiply(2 * k + 1, 1)
+            activate(2 * k, 0)
+            multiply(2 * k + 2, 0)
+            activate(2 * k + 1, 1)
+
+        activate(tiles - 1, 0)
 
     def guo(l):
         if l:
@@ -463,13 +477,13 @@
             drain([f"{name}{l - 1}" for name in ("eR2", "eL2", "eR3", "eL3")])
         down(l, xr)
         if l == last:
-            export(part.at[xr, lower], near_r)
+            export(part.at[xr, lower], first_r.at[lower])
             export(part.at[xr, upper], next_r)
         else:
             send(f"eR2{l}", [(part.at[xr, lower], r_f.at[l, 0, lower])], right)
         down(l, xl)
         if l == last:
-            export(part.at[xl, upper], near_l)
+            export(part.at[xl, upper], first_l.at[upper])
             export(part.at[xl, lower], next_l)
         else:
             send(f"eL2{l}", [(part.at[xl, upper], r_f.at[l, 1, upper])], left)
@@ -479,8 +493,8 @@
             drain([f"{name}{l - 1}" for name in ("eR1", "eL1")])
         down(l, xo)
         if l == last:
-            export(part.at[xo, upper], far_r)
-            export(part.at[xo, lower], far_l)
+            export(part.at[xo, upper], first_r.at[upper])
+            export(part.at[xo, lower], first_l.at[lower])
         else:
             send(f"eR1{l}", [(part.at[xo, upper], r_t.at[l, 0])], right)
             send(f"eL1{l}", [(part.at[xo, lower], r_t.at[l, 1])], left)
@@ -552,18 +566,22 @@
     groups = rows // SEQ_GROUP
     assert n_dev == CHIPS * CORES and heads * SEQ_GROUP == LANES and cache_len == LANES and rows == LANES
     assert lax.axis_size("dp") % 2 == 0
-    cos_tab, sin_tab = rope_tables(positions, head_dim)
+    inv_freq = ROPE_BASE ** (-2.0 * jnp.arange(head_dim // 2, dtype=F32) / head_dim)
     dims = (layers, rows, width, heads, head_dim, cache_len, n_dev, ff)
     vmem, anym = pl.BlockSpec(memory_space=pltpu.VMEM), pl.BlockSpec(memory_space=pl.ANY)
     new_shape = jax.ShapeDtypeStruct((layers, rows, head_dim), F32)
+    whole_sum = jax.ShapeDtypeStruct(hidden.shape, F32)
     half_sum = jax.ShapeDtypeStruct((rows // 2, width), F32)
     n_msg = 96
     return pl.pallas_call(
         functools.partial(decode_kernel, dims),
-        out_shape=(jax.ShapeDtypeStruct(hidden.shape, BF16), new_shape, new_shape) + (half_sum,) * 6 + (jax.ShapeDtypeStruct(hidden.shape, F32),),
-        in_specs=[vmem] * 6 + [anym] * 9,
-        out_specs=(vmem,) * 3 + (anym,) * 7,
+        out_shape=(jax.ShapeDtypeStruct(hidden.shape, BF16), new_shape, new_shape) + (whole_sum, whole_sum, half_sum, half_sum, whole_sum),
+        in_specs=[vmem] * 5 + [anym] * 9,
+        out_specs=(vmem,) * 3 + (anym,) * 5,
         scratch_shapes=[
+            pltpu.VMEM((rows, head_dim // 2), F32),
+            pltpu.VMEM((rows, head_dim // 2), F32),
+            pltpu.VMEM((2, 2, 2 * rows, 2 * LANES), F32),
             pltpu.VMEM((8, 2 * LANES), F32),
             pltpu.VMEM((n_dev, 8, 2 * LANES), F32),
             pltpu.VMEM((groups, 1, LANES), jnp.int32),
@@ -586,16 +604,16 @@
             pltpu.SemaphoreType.DMA((n_msg,)),
             pltpu.SemaphoreType.DMA((4 * layers,)),
             pltpu.SemaphoreType.DMA((2, 2)),
-            pltpu.SemaphoreType.DMA((7,)),
+            pltpu.SemaphoreType.DMA((8,)),
         ],
         compiler_params=pltpu.CompilerParams(collective_id=0, has_side_effects=True, vmem_limit_bytes=67043328),
         name="decode",
-    )(hidden, cos_tab, sin_tab, attn_norm, mlp_norm, positions.reshape(1, rows), k_cache, v_cache, w_query, w_key, w_value, w_out, w_gate, w_up, w_down)
+    )(hidden, inv_freq.reshape(1, head_dim // 2), attn_norm, mlp_norm, positions.reshape(1, rows), k_cache, v_cache, w_query, w_key, w_value, w_out, w_gate, w_up, w_down)
 
 
 TILE_ROWS = 16
-CACHE_BLOCK = 32
-CACHE_SLOTS = 6
+CACHE_BLOCK = 8
+CACHE_SLOTS = 24
 
 
 def cache_kernel(pos_ref, old_ref, new_ref, out_ref, buf, in_sem, out_sem):
@@ -666,19 +684,18 @@
     weight_spec = P(None, "w", None)
 
     def per_device(hidden, positions, k_cache, v_cache, *weights):
-        hid_mid, k_new, v_new, far_r, far_l, near_r, near_l, next_r, next_l, own = decode(hidden, positions, k_cache, v_cache, *weights)
-        n_dev = mesh.shape["w"]
+        hid_mid, k_new, v_new, first_r, first_l, next_r, next_l, own = decode(hidden, positions, k_cache, v_cache, *weights)
+        n_dev, half = mesh.shape["w"], hidden.shape[0] // 2
         ahead = [(i, (i + CORES) % n_dev) for i in range(n_dev)]
         back = [(i, (i - CORES) % n_dev) for i in range(n_dev)]
-        got_r = lax.ppermute(far_r, "w", ahead)
-        got_l = lax.ppermute(far_l, "w", back)
-        low = lax.ppermute(near_r, "w", ahead)
-        high = lax.ppermute(near_l, "w", back)
+        got_r = lax.ppermute(first_r, "w", ahead)
+        got_l = lax.ppermute(first_l, "w", back)
         k_out = write_cache(positions, k_cache, k_new)
-        far_high = lax.ppermute(next_r + got_r, "w", ahead)
-        far_low = lax.ppermute(next_l + got_l, "w", back)
+        upper = lax.ppermute(next_r + got_r[:half], "w", ahead)
+        lower = lax.ppermute(next_l + got_l[half:], "w", back)
         v_out = write_cache(positions, v_cache, v_new)
-        total = own + jnp.concatenate([high + far_high, low + far_low], axis=0)
+        is_upper = lax.broadcasted_iota(jnp.int32, own.shape, 0) < half
+        total = own + jnp.where(is_upper, got_l, got_r) + jnp.concatenate([upper, lower], axis=0)
         hidden_out = (hid_mid.astype(F32) + total).astype(BF16)
         return hidden_out, k_out, v_out
 

time: 183 us -> 174 us (0.951)
  starting transfers between devices: 9.59 us -> 6.37 us
  Pallas kernels: 168 us -> 165 us
  other arithmetic: 4.48 us -> 1.49 us
    ppermute x6 -> x4, starting transfers between devices: 9.59 us -> 6.37 us  [the longest x1 3.31 us: per_device(): lower = lax.ppermute(next_l + got_l[half:], 'w', back)]
    pallas_call x1, Pallas kernels: 140 us -> 138 us  [decode(): pl.pallas_call(functools.partial(decode_kernel, dims), out_shape=(jax.Sha...]
    add x4 -> x2, other arithmetic: 2.05 us -> 0.06 us  [the longest x1 0.03 us: per_device(): lower = lax.ppermute(next_l + got_l[half:], 'w', back)]
  transfers between devices with their start and end apart: 6 -> 4, of which waited for: 0 -> 0; matrix products, arithmetic and copies ran while one was open for 1% -> 0% of each run, Pallas kernels for 15% -> 15%
where the time goes in v4:
time: 174 us; the launch traced here: 173 us
  Pallas kernels  165 us (95%)
  starting transfers between devices  6.37 us (4%)
    pallas_call x1, Pallas kernels, decode(): pl.pallas_call(functools.partial(decode_kernel, dims), out_shape=(jax.Sha...  138 us
    pallas_call x2, Pallas kernels, write_cache(): pl.pallas_call(cache_kernel, out_shape=jax.ShapeDtypeStruct(cache.shape,...  26.7 us
  transfers between devices with their start and end apart: 4, of which 0 were waited for; matrix products, arithmetic and copies ran while one was open for 0% of the time, Pallas kernels for 15%

profile of v4, /device:TPU:112, one launch (start us, length us, event | category | flops | bytes accessed | tf_op | source)
XLA Modules:
  0.0 173.5 jit_solution(8287292909094205929)
XLA Ops:
  0.6 0.5 multiply_power_fusion.freq_ref
  1.2 138.1 %decode.1 = (bf16[128,1152]{1,0:T(8,128)(2,1)}, f32[2,128,256]{2,1,0:T(8,128)}, f32[2,128,256]{2,1,0:T(8,128)}, f32[128,1152]{1,0:T(8,128)}, f32[128,1152]{1,0:T...) custom-call(bf16[128,1152]{1,0:T(8,128)(2,1)} %hid_ref.1, ...), custom_call_target="tpu_custom_call" | custom-call | tf_op jit(solution)/shard_map/decode/pallas_call | solution.py:576
  139.3 3.0 %collective-permute-start = (f32[128,1152]{1,0:T(8,128)}, f32[128,1152]{1,0:T(8,128)S(1)}, u32[]{:S(2)}, u32[]{:S(2)}) collective-permute-start(f32[128,1152]{1,0:T(8,128)} %get-tuple-element.13), channel_id=1, source_target_pairs={{0,6},{1,7},{2,0},{3,1},{4,2},{5,3},{6,4},{7,5},{8,14},{9,15},{10,... | collective-permute-start | bytes 1769480 | tf_op jit(solution)/shard_map/ppermute | solution.py:692
  142.2 0.0 collective-permute-start.1
  142.2 0.0 copy-start.3
  142.2 0.0 copy-start.2
  142.2 13.3 %cache.2 = bf16[2,128,1,128,256]{4,3,2,1,0:T(8,128)(2,1)} custom-call(s32[128]{0:T(128)} %pos_ref.3, bf16[2,128,1,128,256]{4,3,2,1,0:T(8,128)(2,1)} %old_ref.2, f32[2,128,256]{2,1,0:T(8,128)} %get-tuple-element.17.new_ref), custom_call_target="tpu_custom_call" | custom-call | flops 99999997952 | bytes 33554432 | tf_op jit(solution)/shard_map/cache/pallas_call | solution.py:664
  155.6 0.0 collective-permute-done
  155.6 0.0 copy-done.3
  155.7 3.3 %collective-permute-start.3 = (f32[64,1152]{1,0:T(8,128)S(1)}, f32[64,1152]{1,0:T(8,128)S(1)}, u32[]{:S(2)}, u32[]{:S(2)}) collective-permute-start(f32[64,1152]{1,0:T(8,128)S(1)} %slice_add_fusion), channel_id=1, source_target_pairs={{0,6},{1,7},{2,0},{3,1},{4,2},{5,3},{6,4},{7,5},{8,14},{9,15},{10,... | collective-permute-start | bytes 884744 | tf_op jit(solution)/shard_map/ppermute | solution.py:695
  159.0 0.0 collective-permute-done.1
  159.0 0.0 copy-done.2
  159.0 0.1 collective-permute-start.2
  159.1 0.0 copy-start
  159.1 0.0 copy-start.1
  159.1 13.4 %cache.3 = bf16[2,128,1,128,256]{4,3,2,1,0:T(8,128)(2,1)} custom-call(s32[128]{0:T(128)} %pos_ref.3, bf16[2,128,1,128,256]{4,3,2,1,0:T(8,128)(2,1)} %old_ref.3, f32[2,128,256]{2,1,0:T(8,128)} %get-tuple-element.18.new_ref), custom_call_target="tpu_custom_call" | custom-call | flops 99999997952 | bytes 33554432 | tf_op jit(solution)/shard_map/cache/pallas_call | solution.py:664
  172.5 0.0 collective-permute-done.3
  172.5 0.0 collective-permute-done.2
  172.5 0.0 copy-done
  172.6 0.0 copy-done.1
  172.6 0.9 fusion.1
  (3 shorter events, 0.1 us)
Async XLA Ops:
  139.3 16.3 %collective-permute-start = (f32[128,1152]{1,0:T(8,128)}, f32[128,1152]{1,0:T(8,128)S(1)}, u32[]{:S(2)}, u32[]{:S(2)}) collective-permute-start(f32[128,1152]{1,0:T(8,128)} %get-tuple-element.13), channel_id=1, source_target_pairs={{0,6},{1,7},{2,0},{3,1},{4,2},{5,3},{6,4},{7,5},{8,14},{9,15},{10,... | collective-permute-start | bytes 1769480 | tf_op jit(solution)/shard_map/ppermute | solution.py:692
  142.2 16.7 %collective-permute-start.1 = (f32[128,1152]{1,0:T(8,128)}, f32[128,1152]{1,0:T(8,128)S(1)}, u32[]{:S(2)}, u32[]{:S(2)}) collective-permute-start(f32[128,1152]{1,0:T(8,128)} %get-tuple-element.14), channel_id=1, source_target_pairs={{0,2},{1,3},{2,4},{3,5},{4,6},{5,7},{6,0},{7,1},{8,10},{9,11},{10,... | collective-permute-start | bytes 1769480 | tf_op jit(solution)/shard_map/ppermute | solution.py:691
  142.2 13.4 %copy-start.3 = (f32[64,1152]{1,0:T(8,128)S(1)}, f32[64,1152]{1,0:T(8,128)}, u32[]{:S(2)}) copy-start(f32[64,1152]{1,0:T(8,128)} %get-tuple-element.16) | copy-start | bytes 884740
  142.2 16.7 %copy-start.2 = (f32[64,1152]{1,0:T(8,128)S(1)}, f32[64,1152]{1,0:T(8,128)}, u32[]{:S(2)}) copy-start(f32[64,1152]{1,0:T(8,128)} %get-tuple-element.15) | copy-start | bytes 884740
  155.7 16.9 %collective-permute-start.3 = (f32[64,1152]{1,0:T(8,128)S(1)}, f32[64,1152]{1,0:T(8,128)S(1)}, u32[]{:S(2)}, u32[]{:S(2)}) collective-permute-start(f32[64,1152]{1,0:T(8,128)S(1)} %slice_add_fusion), channel_id=1, source_target_pairs={{0,6},{1,7},{2,0},{3,1},{4,2},{5,3},{6,4},{7,5},{8,14},{9,15},{10,... | collective-permute-start | bytes 884744 | tf_op jit(solution)/shard_map/ppermute | solution.py:695
  159.0 13.5 %collective-permute-start.2 = (f32[64,1152]{1,0:T(8,128)S(1)}, f32[64,1152]{1,0:T(8,128)S(1)}, u32[]{:S(2)}, u32[]{:S(2)}) collective-permute-start(f32[64,1152]{1,0:T(8,128)S(1)} %slice_add_fusion.1), channel_id=1, source_target_pairs={{0,2},{1,3},{2,4},{3,5},{4,6},{5,7},{6,0},{7,1},{8,10},{9,11},{10,... | collective-permute-start | bytes 884744 | tf_op jit(solution)/shard_map/ppermute | solution.py:694
  159.1 13.4 %copy-start = (f32[128,1152]{1,0:T(8,128)S(1)}, f32[128,1152]{1,0:T(8,128)}, u32[]{:S(2)}) copy-start(f32[128,1152]{1,0:T(8,128)} %get-tuple-element.12) | copy-start | bytes 1769476
  159.1 13.4 %copy-start.1 = (bf16[128,1152]{1,0:T(8,128)(2,1)S(1)}, bf16[128,1152]{1,0:T(8,128)(2,1)}, u32[]{:S(2)}) copy-start(bf16[128,1152]{1,0:T(8,128)(2,1)} %get-tuple-element.11) | copy-start | bytes 884740

commit v5 on v4

--- a/solution.py
+++ b/solution.py
@@ -13,6 +13,7 @@
 CORES = 2
 CHIPS = 4
 SEQ_GROUP = 32
+KV_SLOTS = 3
 MESH = pl.DeviceIdType.MESH
 F32 = jnp.float32
 BF16 = jnp.bfloat16
@@ -27,10 +28,11 @@
 
 
 ORDER = (
-    "bo0", "ao0", "ct0", "bf0", "af0", "cf0", "cd0", "ct1", "bx0", "ax0", "cx0", "aw0", "dt0", "qkv0",
-    "att0", "bw0", "ao1", "att0", "att0", "cd1", "cn0", "af1", "att0", "mix0", "yf0", "cf1", "cw0", "ax1", "dt1", "dr0",
-    "gua0", "near0", "cn1", "gub0", "far0", "bo1", "er0", "guo0", "own0", "bf1", "aw1", "cx1", "done0", "qkv1",
-    "att1", "att1", "bx1", "att1", "att1", "mix1", "cw1", "yf1", "guo1", "dr1", "own1", "gua1", "near1", "gub1", "far1",
+    "bo0", "ao0", "ce0", "in0", "bp0", "af0", "ct0", "bf0", "cd0", "dt1", "ap0", "ao1", "ce1", "cm0", "at0", "ax0",
+    "cf0", "cn0", "bx0", "aw0", "dt0", "af1", "qkv0", "att0", "bo1", "att0", "cx0", "ct1", "att0", "bt0", "bw0", "att0",
+    "mix0", "cm1", "cf1", "yf0", "cw0", "cu0", "ap1", "cd1", "gua0", "dr0", "near0", "ax1", "gub0", "far0", "cn1", "cu1",
+    "aw1", "er0", "bf1", "guo0", "at1", "own0", "cx1", "done0", "qkv1", "att1", "att1", "bx1", "bt1", "att1", "att1", "mix1",
+    "cw1", "yf1", "guo1", "dr1", "own1", "gua1", "near1", "gub1", "far1",
 )
 SHARE_A = (True, True)
 SHARE_B = (True, False)
@@ -41,9 +43,9 @@
     hid_ref, freq_ref, an_ref, mn_ref, pos_ref, kc_ref, vc_ref,
     wq_ref, wk_ref, wv_ref, wo_ref, wg_ref, wu_ref, wd_ref,
     hid_out, knew_ref, vnew_ref, first_r, first_l, next_r, next_l, own_out,
-    cos_buf, sin_buf, act_buf, gsrc, gbuf, pos_buf, abuf_w, bbuf_w, gu_w, wd_w, tr_w, y_all, m_buf, part, r_t, r_f,
+    cos_buf, sin_buf, act_buf, an_buf, mn_buf, freq_buf, pos_in, know, vnow, gsrc, gbuf, pos_buf, abuf_w, bbuf_w, gu_w, wd_w, tr_w, y_all, m_buf, part, r_t, r_f,
     kbuf, vbuf, qbuf, abuf, hbuf,
-    send_sem, recv_sem, loc_sem, kv_sem, out_sem,
+    send_sem, recv_sem, loc_sem, kv_sem, out_sem, in_sem,
 ):
     layers, rows, width, heads, head_dim, cache_len, n_dev, ff = dims
     half = head_dim // 2
@@ -75,7 +77,7 @@
     kv_mine = pl.multiple_of(h * kv_half, LANES)
     starts = [pl.multiple_of(lax.div(chip_cols * xx, LANES) * LANES, LANES) for xx in (x, xr, xo, xl)]
     x_start, xr_start, xo_start, xl_start = starts
-    xo_mid = pl.multiple_of(xo_start + win // 2, LANES)
+    xr_mid, xo_mid, xl_mid = [pl.multiple_of(xx + win // 2, LANES) for xx in starts[1:]]
     shift = lax.rem(chip_cols * x, LANES)
     wd_mine = pl.ds(pl.multiple_of(shift + wd_rows * c, 32), wd_rows)
     wd_twin = pl.ds(pl.multiple_of(shift + wd_rows * cc, 32), wd_rows)
@@ -92,8 +94,12 @@
             copy_of(name, src, dst, dev).start()
         pending[name] = pairs[0][0] if view is None else view
 
+    arrived = set()
+
     def got(name, view):
-        copy_of(name, view, view, right).wait_recv()
+        if name not in arrived:
+            arrived.add(name)
+            copy_of(name, view, view, right).wait_recv()
 
     def drain(names):
         for name in names:
@@ -105,7 +111,9 @@
             pltpu.make_async_copy(src, dst, loc_sem.at[sem]).start()
 
     def local_wait(sem, view):
-        pltpu.make_async_copy(view, view, loc_sem.at[sem]).wait()
+        if sem not in arrived:
+            arrived.add(sem)
+            pltpu.make_async_copy(view, view, loc_sem.at[sem]).wait()
 
     def kv_copies(i, slot):
         layer, group = lax.div(i, groups), lax.rem(i, groups)
@@ -147,20 +155,32 @@
     def to_pair(name, view):
         send(name, [(view, view)], pair)
 
-    def af(l):
+    def a_near(l):
         got(f"aR{l}", a_block(l, xl))
-        send(f"afR{l}", [(a_lead(l, xl), a_lead(l, xl))], right)
         got(f"aL{l}", a_block(l, xr))
-        send(f"afL{l}", [(a_tail(l, xr), a_tail(l, xr))], left)
-        if SHARE_A[l]:
-            to_pair(f"paR{l}", a_block(l, xl))
-            to_pair(f"paL{l}", a_block(l, xr))
-
-    def ax(l):
+
+    def a_far(l):
         got(f"afR{l}", a_lead(l, xo))
         got(f"afL{l}", a_tail(l, xo))
+
+    def af(l):
+        a_near(l)
+        send(f"afR{l}", [(a_lead(l, xl), a_lead(l, xl))], right)
+        send(f"afL{l}", [(a_tail(l, xr), a_tail(l, xr))], left)
+
+    def ap(l):
+        a_near(l)
+        to_pair(f"paR{l}", a_block(l, xl))
+        to_pair(f"paL{l}", a_block(l, xr))
+
+    def ax(l):
+        a_far(l)
         if SHARE_A[l]:
             to_pair(f"paF{l}", a_block(l, xo))
+
+    def at(l):
+        a_near(l)
+        a_far(l)
         local_wait(4 * l, abuf_w.at[l, :, x, c])
         view = abuf_w.at[l, h, :, c] if SHARE_A[l] else abuf_w.at[l, :, :, c]
         send(f"aT{l}", [(view, view)], twin)
@@ -168,6 +188,7 @@
     def aw(l):
         for name, xx in (("paR", xl), ("paL", xr), ("paF", xo)):
             got(f"{name}{l}", abuf_w.at[l, hh, xx, c])
+        local_wait(4 * l, abuf_w.at[l, :, x, c])
         view = abuf_w.at[l, hh, :, c]
         send(f"aT1{l}", [(view, view)], twin)
 
@@ -192,20 +213,32 @@
         send(f"bR{l}", [(src, b_block(l, x))], right)
         send(f"bL{l}", [(src, b_block(l, x))], left)
 
-    def bf(l):
+    def b_near(l):
         got(f"bR{l}", b_block(l, xl))
-        send(f"bfR{l}", [(b_lead(l, xl), b_lead(l, xl))], right)
         got(f"bL{l}", b_block(l, xr))
-        send(f"bfL{l}", [(b_tail(l, xr), b_tail(l, xr))], left)
-        if SHARE_B[l]:
-            to_pair(f"pbR{l}", b_block(l, xl))
-            to_pair(f"pbL{l}", b_block(l, xr))
-
-    def bx(l):
+
+    def b_far(l):
         got(f"bfR{l}", b_lead(l, xo))
         got(f"bfL{l}", b_tail(l, xo))
+
+    def bf(l):
+        b_near(l)
+        send(f"bfR{l}", [(b_lead(l, xl), b_lead(l, xl))], right)
+        send(f"bfL{l}", [(b_tail(l, xr), b_tail(l, xr))], left)
+
+    def bp(l):
+        b_near(l)
+        to_pair(f"pbR{l}", b_block(l, xl))
+        to_pair(f"pbL{l}", b_block(l, xr))
+
+    def bx(l):
+        b_far(l)
         if SHARE_B[l]:
             to_pair(f"pbF{l}", b_block(l, xo))
+
+    def bt(l):
+        b_near(l)
+        b_far(l)
         local_wait(4 * l + 1, bbuf_w.at[l, x, c])
         view = bbuf_w.at[l, :, c, pl.ds(b_mine, b_half)] if SHARE_B[l] else bbuf_w.at[l, :, c]
         send(f"bT{l}", [(view, view)], twin)
@@ -213,6 +246,7 @@
     def bw(l):
         for name, xx in (("pbR", xl), ("pbL", xr), ("pbF", xo)):
             got(f"{name}{l}", bbuf_w.at[l, xx, c, pl.ds(b_other, b_half)])
+        local_wait(4 * l + 1, bbuf_w.at[l, x, c])
         view = bbuf_w.at[l, :, c, pl.ds(b_other, b_half)]
         send(f"bT1{l}", [(view, view)], twin)
 
@@ -230,9 +264,15 @@
                 copy_of(name, ref.at[l, :, pl.ds(lo, size)], dst, dev).start()
         pending[name] = dst
 
+    fore, aft = pl.ds(0, win // 2), pl.ds(win // 2, win // 2)
+
     def cd(l):
-        by_matrix(l, f"cR{l}", xr_start, win, gu_w.at[l, h, x, c], right)
-        by_matrix(l, f"cL{l}", xl_start, win, gu_w.at[l, h, x, c], left)
+        by_matrix(l, f"cR{l}", xr_start, win // 2, gu_w.at[l, h, x, c, :, fore], right)
+        by_matrix(l, f"cL{l}", xl_start, win // 2, gu_w.at[l, h, x, c, :, fore], left)
+
+    def ce(l):
+        by_matrix(l, f"dR{l}", xr_mid, win // 2, gu_w.at[l, h, x, c, :, aft], right)
+        by_matrix(l, f"dL{l}", xl_mid, win // 2, gu_w.at[l, h, x, c, :, aft], left)
 
     def ct(l):
         by_matrix(l, f"tR{l}", xo_start, win // 2, tr_w.at[l, 0], right)
@@ -240,26 +280,45 @@
 
     def cf(l):
         got(f"tR{l}", tr_w.at[l, 0])
-        send(f"cfR{l}", [(tr_w.at[l, 0], gu_w.at[l, h, xl, c, :, pl.ds(0, win // 2)])], right)
+        send(f"cfR{l}", [(tr_w.at[l, 0], gu_w.at[l, h, xl, c, :, fore])], right)
         got(f"tL{l}", tr_w.at[l, 1])
-        send(f"cfL{l}", [(tr_w.at[l, 1], gu_w.at[l, h, xr, c, :, pl.ds(win // 2, win // 2)])], left)
+        send(f"cfL{l}", [(tr_w.at[l, 1], gu_w.at[l, h, xr, c, :, aft])], left)
+
+    def c_near(l, part_name, cols):
+        got(f"{part_name}R{l}", gu_w.at[l, h, xl, c, :, cols])
+        got(f"{part_name}L{l}", gu_w.at[l, h, xr, c, :, cols])
+
+    def c_far(l):
+        got(f"cfR{l}", gu_w.at[l, h, xo, c, :, fore])
+        got(f"cfL{l}", gu_w.at[l, h, xo, c, :, aft])
 
     def cn(l):
-        for name, xx in (("cR", xl), ("cL", xr)):
-            got(f"{name}{l}", gu_w.at[l, h, xx, c])
-            to_pair(f"p{name}{l}", gu_w.at[l, h, xx, c])
+        c_near(l, "c", fore)
+        to_pair(f"pcR{l}", gu_w.at[l, h, xl, c, :, fore])
+        to_pair(f"pcL{l}", gu_w.at[l, h, xr, c, :, fore])
+
+    def cm(l):
+        c_near(l, "d", aft)
+        to_pair(f"pdR{l}", gu_w.at[l, h, xl, c, :, aft])
+        to_pair(f"pdL{l}", gu_w.at[l, h, xr, c, :, aft])
 
     def cx(l):
-        got(f"cfR{l}", gu_w.at[l, h, xo, c, :, pl.ds(0, win // 2)])
-        got(f"cfL{l}", gu_w.at[l, h, xo, c, :, pl.ds(win // 2, win // 2)])
+        c_far(l)
         to_pair(f"pcF{l}", gu_w.at[l, h, xo, c])
 
-    def cw(l):
+    def cu(l):
+        c_near(l, "c", fore)
+        c_near(l, "d", aft)
+        c_far(l)
         local_wait(4 * l + 2, gu_w.at[l, :, x, c])
         view = gu_w.at[l, h, :, c]
         send(f"cT{l}", [(view, view)], twin)
-        for name, xx in (("pcR", xl), ("pcL", xr), ("pcF", xo)):
-            got(f"{name}{l}", gu_w.at[l, hh, xx, c])
+
+    def cw(l):
+        for name, xx, cols in (("pcR", xl, fore), ("pcL", xr, fore), ("pdR", xl, aft), ("pdL", xr, aft)):
+            got(f"{name}{l}", gu_w.at[l, hh, xx, c, :, cols])
+        got(f"pcF{l}", gu_w.at[l, hh, xo, c])
+        local_wait(4 * l + 2, gu_w.at[l, :, x, c])
         view = gu_w.at[l, hh, :, c]
         send(f"cT1{l}", [(view, view)], twin)
 
@@ -274,43 +333,51 @@
         local_wait(4 * l + 3, wd_w.at[l, wd_mine])
         got(f"dT{l}", wd_w.at[l, wd_twin])
 
-    for l in range(layers):
-        start = pl.multiple_of(jnp.where(lax.rem(x, 2) == 0, chip_cols, 0), 64)
-        wd_w[l, pl.ds(start, pad), :] = jnp.zeros((pad, width), BF16)
-    gsrc[...] = jnp.zeros_like(gsrc)
-    gsrc[0:layers, 0:piece] = an_ref[...]
-    gsrc[layers:2 * layers, 0:piece] = mn_ref[...]
-    gsrc[...] = pltpu.roll(gsrc[...], lax.rem(w * piece, LANES), 1)
+    small = [(an_ref, an_buf), (mn_ref, mn_buf), (freq_ref, freq_buf), (pos_ref, pos_in)]
+    for i, (src, dst) in enumerate(small):
+        pltpu.make_async_copy(src, dst, in_sem.at[i]).start()
     barrier = pltpu.get_barrier_semaphore()
     for i in range(1, n_dev):
         pl.semaphore_signal(barrier, inc=1, device_id=(dp, lax.rem(w + i, n_dev)), device_id_type=MESH)
     pl.semaphore_signal(barrier, inc=1, device_id=pair, device_id_type=MESH)
     pl.semaphore_wait(barrier, n_dev)
 
-    def entry():
-        for i in range(1, n_dev):
-            copy_of("gain", gsrc, gbuf.at[w], (dp, lax.rem(w + i, n_dev))).start()
-        pending["gain"] = gbuf.at[pl.ds(0, n_dev - 1)]
-        gbuf[w] = gsrc[...]
-        kv_start(0, 0)
+    def entry(_):
+        hid_copy = pltpu.make_async_copy(hid_ref, hbuf, in_sem.at[len(small)])
+        hid_copy.start()
+        for i in range(KV_SLOTS):
+            kv_start(i, i)
         for l in range(layers):
             local_start(4 * l, a_both(l))
             local_start(4 * l + 1, [(wo_ref.at[l], bbuf_w.at[l, x, c])])
             cols = pl.ds(x_start, win)
             local_start(4 * l + 2, [(wg_ref.at[l, :, cols], gu_w.at[l, 0, x, c]), (wu_ref.at[l, :, cols], gu_w.at[l, 1, x, c])])
             local_start(4 * l + 3, [(wd_ref.at[l], wd_w.at[l, wd_mine])])
-        kv_start(1, 1)
-        hbuf[...] = hid_ref[...]
+        for i, (src, dst) in enumerate(small):
+            pltpu.make_async_copy(src, dst, in_sem.at[i]).wait()
+        gsrc[...] = jnp.zeros_like(gsrc)
+        gsrc[0:layers, 0:piece] = an_buf[...]
+        gsrc[layers:2 * layers, 0:piece] = mn_buf[...]
+        own_gain = pltpu.roll(gsrc[...], lax.rem(w * piece, LANES), 1)
+        gsrc[...] = own_gain
+        gbuf[w] = own_gain
+        for l in range(layers):
+            start = pl.multiple_of(jnp.where(lax.rem(x, 2) == 0, chip_cols, 0), 64)
+            wd_w[l, pl.ds(start, pad), :] = jnp.zeros((pad, width), BF16)
         lane_block = lax.div(lax.broadcasted_iota(jnp.int32, (1, LANES), 1), SEQ_GROUP)
         for g in range(groups):
-            line = pos_ref[...]
+            line = pos_in[...]
             for j in range(heads):
-                moved = pltpu.roll(pos_ref[...], lax.rem(w * 0 + (j - g + heads) * SEQ_GROUP, LANES), 1)
+                moved = pltpu.roll(pos_in[...], ((j - g) * SEQ_GROUP) % LANES, 1)
                 line = jnp.where(lane_block == j, moved, line)
             pos_buf[g] = line
-        angles = jnp.broadcast_to(pos_ref[...].astype(F32), (rows, rows)).T * freq_ref[...]
+        angles = jnp.broadcast_to(pos_in[...].astype(F32), (rows, rows)).T * freq_buf[...]
         cos_buf[...] = jnp.cos(angles)
         sin_buf[...] = jnp.sin(angles)
+        for i in range(1, n_dev):
+            copy_of("gain", gsrc, gbuf.at[w], (dp, lax.rem(w + i, n_dev))).start()
+        pending["gain"] = gbuf.at[pl.ds(0, n_dev - 1)]
+        hid_copy.wait()
 
     def all_gains():
         tiles = []
@@ -338,7 +405,7 @@
         lane_new = lax.rem(lax.broadcasted_iota(jnp.int32, (SEQ_GROUP, LANES), 1), SEQ_GROUP)
         row_new = lax.broadcasted_iota(jnp.int32, (SEQ_GROUP, LANES), 0)
         i = l * groups + group
-        slot = lax.rem(group, 2)
+        slot = lax.rem(i, KV_SLOTS)
         for copy in kv_copies(i, slot):
             copy.wait()
         seqs = pl.ds(pl.multiple_of(group * SEQ_GROUP, SEQ_GROUP), SEQ_GROUP)
@@ -349,8 +416,8 @@
             prod = dot_t(block, query)
             for j in range(chunk):
                 scores = jnp.where(lane_seq == b + j, prod[j * cache_len:(j + 1) * cache_len], scores)
-        k_new = knew_ref[l, seqs, :].astype(BF16)
-        v_new = vnew_ref[l, seqs, :]
+        k_new = know[l, seqs, :].astype(BF16)
+        v_new = vnow[l, seqs, :]
         new_score = jnp.sum(jnp.where(row_new == lane_new, dot_t(k_new, query), 0.0), axis=0, keepdims=True)
         scores = jnp.where(row_t < pos_buf[group], scores, -1e30)
         top = jnp.maximum(jnp.max(scores, axis=0, keepdims=True), new_score)
@@ -369,9 +436,16 @@
         for j in range(heads):
             abuf[seqs, j * head_dim:(j + 1) * head_dim] = attn[j * SEQ_GROUP:(j + 1) * SEQ_GROUP, :]
 
-        @pl.when(i + 2 < layers * groups)
+        @pl.when(i + KV_SLOTS < layers * groups)
         def _():
-            kv_start(i + 2, slot)
+            kv_start(i + KV_SLOTS, slot)
+
+    last = layers - 1
+    exports = []
+
+    def export(src, dst):
+        pltpu.make_async_copy(src, dst, out_sem.at[len(exports)]).start()
+        exports.append((src, dst))
 
     def qkv(l):
         a_ready(l)
@@ -387,8 +461,10 @@
         for j in range(heads):
             out, lo = halves[j // (heads // 2)], (j % (heads // 2)) * head_dim
             qbuf[j] = (rope(out[:, lo:lo + half], out[:, lo + half:lo + head_dim]) * head_dim ** -0.5).astype(BF16)
-        knew_ref[l] = rope(halves[0][:, q_half:q_half + half], halves[1][:, q_half:q_half + half]).astype(BF16).astype(F32)
-        vnew_ref[l] = jnp.concatenate([hv[:, q_half + half:q_half + 2 * half] for hv in halves], axis=1).astype(BF16).astype(F32)
+        know[l] = rope(halves[0][:, q_half:q_half + half], halves[1][:, q_half:q_half + half]).astype(BF16).astype(F32)
+        vnow[l] = jnp.concatenate([hv[:, q_half + half:q_half + 2 * half] for hv in halves], axis=1).astype(BF16).astype(F32)
+        export(know.at[l], knew_ref.at[l])
+        export(vnow.at[l], vnew_ref.at[l])
 
     r2 = rows // 2
     upper, lower = pl.ds(0, r2), pl.ds(r2, r2)
@@ -463,14 +539,6 @@
 
     def down(l, xx):
         part[xx] = dot(m_buf[xx], wd_w[l])
-
-    last = layers - 1
-
-    def export(src, dst):
-        pltpu.make_async_copy(src, dst, out_sem.at[len(exports)]).start()
-        exports.append((src, dst))
-
-    exports = []
 
     def near(l):
         if l:
@@ -511,7 +579,7 @@
         down(l, x)
         if l == last:
             export(part.at[x], own_out)
-            hid_out[...] = hbuf[...]
+            export(hbuf, hid_out)
 
     def done(l):
         got(f"eR2{l}", r_f.at[l, 0, lower])
@@ -521,26 +589,26 @@
         hbuf[...] = (hbuf[...].astype(F32) + (part[x] + r_f[l, 0] + r_f[l, 1])).astype(BF16)
 
     table = dict(
-        ao=ao, af=af, ax=ax, aw=aw, bo=bo, bf=bf, bx=bx, bw=bw, cd=cd, ct=ct, cf=cf, cn=cn, cx=cx, cw=cw, dt=dt,
+        ao=ao, af=af, ap=ap, ax=ax, at=at, aw=aw, bo=bo, bf=bf, bp=bp, bx=bx, bt=bt, bw=bw, cd=cd, ce=ce, ct=ct, cf=cf,
+        cn=cn, cm=cm, cx=cx, cu=cu, cw=cw, dt=dt, **{"in": entry},
         qkv=qkv, mix=mix, yf=yf, guo=guo, gua=gua, gub=gub, dr=d_ready, near=near, far=far, er=er, own=own, done=done,
     )
 
     def run(step):
         table[step[:-1]](int(step[-1]))
 
-    entry()
-    at = 0
+    here = 0
     reached = [0] * layers
-    while at < len(ORDER):
-        step = ORDER[at]
+    while here < len(ORDER):
+        step = ORDER[here]
         if not step.startswith("att"):
             run(step)
-            at += 1
+            here += 1
             continue
         l, count = int(step[-1]), 0
-        while ORDER[at] == step:
+        while ORDER[here] == step:
             count += 1
-            at += 1
+            here += 1
         first = reached[l]
         reached[l] += count
 
@@ -568,7 +636,7 @@
     assert lax.axis_size("dp") % 2 == 0
     inv_freq = ROPE_BASE ** (-2.0 * jnp.arange(head_dim // 2, dtype=F32) / head_dim)
     dims = (layers, rows, width, heads, head_dim, cache_len, n_dev, ff)
-    vmem, anym = pl.BlockSpec(memory_space=pltpu.VMEM), pl.BlockSpec(memory_space=pl.ANY)
+    anym = pl.BlockSpec(memory_space=pl.ANY)
     new_shape = jax.ShapeDtypeStruct((layers, rows, head_dim), F32)
     whole_sum = jax.ShapeDtypeStruct(hidden.shape, F32)
     half_sum = jax.ShapeDtypeStruct((rows // 2, width), F32)
@@ -576,12 +644,18 @@
     return pl.pallas_call(
         functools.partial(decode_kernel, dims),
         out_shape=(jax.ShapeDtypeStruct(hidden.shape, BF16), new_shape, new_shape) + (whole_sum, whole_sum, half_sum, half_sum, whole_sum),
-        in_specs=[vmem] * 5 + [anym] * 9,
-        out_specs=(vmem,) * 3 + (anym,) * 5,
+        in_specs=[anym] * 14,
+        out_specs=(anym,) * 8,
         scratch_shapes=[
             pltpu.VMEM((rows, head_dim // 2), F32),
             pltpu.VMEM((rows, head_dim // 2), F32),
             pltpu.VMEM((2, 2, 2 * rows, 2 * LANES), F32),
+            pltpu.VMEM(attn_norm.shape, F32),
+            pltpu.VMEM(mlp_norm.shape, F32),
+            pltpu.VMEM((1, head_dim // 2), F32),
+            pltpu.VMEM((1, rows), jnp.int32),
+            pltpu.VMEM((layers, rows, head_dim), F32),
+            pltpu.VMEM((layers, rows, head_dim), F32),
             pltpu.VMEM((8, 2 * LANES), F32),
             pltpu.VMEM((n_dev, 8, 2 * LANES), F32),
             pltpu.VMEM((groups, 1, LANES), jnp.int32),
@@ -595,15 +669,16 @@
             pltpu.VMEM((CHIPS, rows, width), F32),
             pltpu.VMEM((layers - 1, 2, rows // 2, width), F32),
             pltpu.VMEM((layers - 1, 2, rows, width), F32),
-            pltpu.VMEM((2, SEQ_GROUP, cache_len, head_dim), BF16),
-            pltpu.VMEM((2, SEQ_GROUP, cache_len, head_dim), BF16),
+            pltpu.VMEM((KV_SLOTS, SEQ_GROUP, cache_len, head_dim), BF16),
+            pltpu.VMEM((KV_SLOTS, SEQ_GROUP, cache_len, head_dim), BF16),
             pltpu.VMEM((heads, rows, head_dim), BF16),
             pltpu.VMEM((rows, heads * head_dim), BF16),
             pltpu.VMEM((rows, width), BF16),
             pltpu.SemaphoreType.DMA((n_msg,)),
             pltpu.SemaphoreType.DMA((n_msg,)),
             pltpu.SemaphoreType.DMA((4 * layers,)),
-            pltpu.SemaphoreType.DMA((2, 2)),
+            pltpu.SemaphoreType.DMA((KV_SLOTS, 2)),
+            pltpu.SemaphoreType.DMA((16,)),
             pltpu.SemaphoreType.DMA((8,)),
         ],
         compiler_params=pltpu.CompilerParams(collective_id=0, has_side_effects=True, vmem_limit_bytes=67043328),
@@ -612,49 +687,55 @@
 
 
 TILE_ROWS = 16
-CACHE_BLOCK = 8
-CACHE_SLOTS = 24
+CACHE_BLOCK = 16
+CACHE_SLOTS = 12
 
 
 def cache_kernel(pos_ref, old_ref, new_ref, out_ref, buf, in_sem, out_sem):
     layers, rows = old_ref.shape[:2]
     blocks = rows // CACHE_BLOCK
-    steps = [(l, b) for l in range(layers) for b in range(blocks)]
+    steps = layers * blocks
+
+    def split(i):
+        return i // blocks, i % blocks, i % CACHE_SLOTS
 
     def load(i):
-        l, b = steps[i]
-        slot = i % CACHE_SLOTS
+        l, b, slot = split(i)
         return pltpu.make_async_copy(old_ref.at[l, pl.ds(b * CACHE_BLOCK, CACHE_BLOCK), 0], buf.at[slot], in_sem.at[slot])
 
     def store(i):
-        l, b = steps[i]
-        slot = i % CACHE_SLOTS
+        l, b, slot = split(i)
         return pltpu.make_async_copy(buf.at[slot], out_ref.at[l, pl.ds(b * CACHE_BLOCK, CACHE_BLOCK), 0], out_sem.at[slot])
 
     ahead = CACHE_SLOTS // 2
     for i in range(ahead):
         load(i).start()
     row = lax.broadcasted_iota(jnp.int32, (TILE_ROWS, buf.shape[-1]), 0)
-    for i in range(len(steps)):
+
+    @pl.loop(0, steps)
+    def _(i):
         load(i).wait()
-        l, b = steps[i]
-        slot = i % CACHE_SLOTS
-
-        @pl.loop(0, CACHE_BLOCK)
-        def _(s):
+        l, b, slot = split(i)
+        fresh = new_ref[l, pl.ds(pl.multiple_of(b * CACHE_BLOCK, CACHE_BLOCK), CACHE_BLOCK), :]
+        tiles = []
+        for s in range(CACHE_BLOCK):
             pos = pos_ref[b * CACHE_BLOCK + s]
             base = pl.multiple_of(pos // TILE_ROWS * TILE_ROWS, TILE_ROWS)
             tile = buf[slot, s, pl.ds(base, TILE_ROWS), :].astype(F32)
-            fresh = new_ref[l, pl.ds(b * CACHE_BLOCK + s, 1), :]
-            buf[slot, s, pl.ds(base, TILE_ROWS), :] = jnp.where(row == pos - base, fresh, tile).astype(BF16)
-
+            tiles.append((s, base, jnp.where(row == pos - base, fresh[s:s + 1, :], tile).astype(BF16)))
+        for s, base, tile in tiles:
+            buf[slot, s, pl.ds(base, TILE_ROWS), :] = tile
         store(i).start()
-        nxt = i + ahead
-        if nxt < len(steps):
-            if nxt >= CACHE_SLOTS:
-                store(nxt - CACHE_SLOTS).wait()
-            load(nxt).start()
-    for i in range(max(0, len(steps) - CACHE_SLOTS), len(steps)):
+
+        @pl.when(i + ahead < steps)
+        def _():
+            @pl.when(i + ahead >= CACHE_SLOTS)
+            def _():
+                store(i + ahead - CACHE_SLOTS).wait()
+            load(i + ahead).start()
+
+    @pl.loop(steps - CACHE_SLOTS, steps)
+    def _(i):
         store(i).wait()
 
 

time: 174 us -> 170 us (0.977)
  starting transfers between devices: 6.37 us -> 4.29 us
    ppermute x1, starting transfers between devices: 2.96 us -> 0.57 us  [per_device(): got_l = lax.ppermute(first_l, 'w', back)]
  transfers between devices with their start and end apart: 4 -> 4, of which waited for: 0 -> 0; matrix products, arithmetic and copies ran while one was open for 0% -> 0% of each run, Pallas kernels for 15% -> 16%
where the time goes in v5:
time: 170 us
  Pallas kernels  164 us (96%)
  starting transfers between devices  4.29 us (3%)
    pallas_call x1, Pallas kernels, decode(): pl.pallas_call(functools.partial(decode_kernel, dims), out_shape=(jax.Sha...  137 us
    pallas_call x2, Pallas kernels, write_cache(): pl.pallas_call(cache_kernel, out_shape=jax.ShapeDtypeStruct(cache.shape,...  26.8 us
  transfers between devices with their start and end apart: 4, of which 0 were waited for; matrix products, arithmetic and copies ran while one was open for 0% of the time, Pallas kernels for 16%

profile of v5, /device:TPU:112, one launch (start us, length us, event | category | flops | bytes accessed | tf_op | source)
XLA Modules:
  0.0 170.1 jit_solution(9854115890893118529)
XLA Ops:
  0.6 0.5 multiply_power_fusion.freq_ref
  1.2 136.8 %decode.1 = (bf16[128,1152]{1,0:T(8,128)(2,1)}, f32[2,128,256]{2,1,0:T(8,128)}, f32[2,128,256]{2,1,0:T(8,128)}, f32[128,1152]{1,0:T(8,128)}, f32[128,1152]{1,0:T...) custom-call(bf16[128,1152]{1,0:T(8,128)(2,1)} %hid_ref.1, ...), custom_call_target="tpu_custom_call" | custom-call | tf_op jit(solution)/shard_map/decode/pallas_call | solution.py:644
  138.0 0.6 collective-permute-start
  138.6 1.5 collective-permute-start.1
  140.1 0.0 copy-start.3
  140.1 0.0 copy-start.2
  140.1 13.4 %cache.2 = bf16[2,128,1,128,256]{4,3,2,1,0:T(8,128)(2,1)} custom-call(s32[128]{0:T(128)} %pos_ref.3, bf16[2,128,1,128,256]{4,3,2,1,0:T(8,128)(2,1)} %old_ref.2, f32[2,128,256]{2,1,0:T(8,128)} %get-tuple-element.17.new_ref), custom_call_target="tpu_custom_call" | custom-call | flops 99999997952 | bytes 33554432 | tf_op jit(solution)/shard_map/cache/pallas_call | solution.py:745
  153.5 0.0 collective-permute-done
  153.5 0.0 copy-done.3
  153.5 1.8 %collective-permute-start.3 = (f32[64,1152]{1,0:T(8,128)S(1)}, f32[64,1152]{1,0:T(8,128)S(1)}, u32[]{:S(2)}, u32[]{:S(2)}) collective-permute-start(f32[64,1152]{1,0:T(8,128)S(1)} %slice_add_fusion), channel_id=1, source_target_pairs={{0,6},{1,7},{2,0},{3,1},{4,2},{5,3},{6,4},{7,5},{8,14},{9,15},{10,... | collective-permute-start | bytes 884744 | tf_op jit(solution)/shard_map/ppermute | solution.py:776
  155.3 0.0 collective-permute-done.1
  155.3 0.0 copy-done.2
  155.3 0.4 collective-permute-start.2
  155.8 0.0 copy-start
  155.8 0.0 copy-start.1
  155.8 13.4 %cache.3 = bf16[2,128,1,128,256]{4,3,2,1,0:T(8,128)(2,1)} custom-call(s32[128]{0:T(128)} %pos_ref.3, bf16[2,128,1,128,256]{4,3,2,1,0:T(8,128)(2,1)} %old_ref.3, f32[2,128,256]{2,1,0:T(8,128)} %get-tuple-element.18.new_ref), custom_call_target="tpu_custom_call" | custom-call | flops 99999997952 | bytes 33554432 | tf_op jit(solution)/shard_map/cache/pallas_call | solution.py:745
  169.2 0.0 collective-permute-done.3
  169.2 0.0 collective-permute-done.2
  169.2 0.0 copy-done
  169.2 0.0 copy-done.1
  169.2 0.9 fusion.1
  (3 shorter events, 0.1 us)
Async XLA Ops:
  138.0 15.5 %collective-permute-start = (f32[128,1152]{1,0:T(8,128)}, f32[128,1152]{1,0:T(8,128)S(1)}, u32[]{:S(2)}, u32[]{:S(2)}) collective-permute-start(f32[128,1152]{1,0:T(8,128)} %get-tuple-element.13), channel_id=1, source_target_pairs={{0,6},{1,7},{2,0},{3,1},{4,2},{5,3},{6,4},{7,5},{8,14},{9,15},{10,... | collective-permute-start | bytes 1769480 | tf_op jit(solution)/shard_map/ppermute | solution.py:773
  138.6 16.8 %collective-permute-start.1 = (f32[128,1152]{1,0:T(8,128)}, f32[128,1152]{1,0:T(8,128)S(1)}, u32[]{:S(2)}, u32[]{:S(2)}) collective-permute-start(f32[128,1152]{1,0:T(8,128)} %get-tuple-element.14), channel_id=1, source_target_pairs={{0,2},{1,3},{2,4},{3,5},{4,6},{5,7},{6,0},{7,1},{8,10},{9,11},{10,... | collective-permute-start | bytes 1769480 | tf_op jit(solution)/shard_map/ppermute | solution.py:772
  140.1 13.4 %copy-start.3 = (f32[64,1152]{1,0:T(8,128)S(1)}, f32[64,1152]{1,0:T(8,128)}, u32[]{:S(2)}) copy-start(f32[64,1152]{1,0:T(8,128)} %get-tuple-element.16) | copy-start | bytes 884740
  140.1 15.2 %copy-start.2 = (f32[64,1152]{1,0:T(8,128)S(1)}, f32[64,1152]{1,0:T(8,128)}, u32[]{:S(2)}) copy-start(f32[64,1152]{1,0:T(8,128)} %get-tuple-element.15) | copy-start | bytes 884740
  153.5 15.6 %collective-permute-start.3 = (f32[64,1152]{1,0:T(8,128)S(1)}, f32[64,1152]{1,0:T(8,128)S(1)}, u32[]{:S(2)}, u32[]{:S(2)}) collective-permute-start(f32[64,1152]{1,0:T(8,128)S(1)} %slice_add_fusion), channel_id=1, source_target_pairs={{0,6},{1,7},{2,0},{3,1},{4,2},{5,3},{6,4},{7,5},{8,14},{9,15},{10,... | collective-permute-start | bytes 884744 | tf_op jit(solution)/shard_map/ppermute | solution.py:776
  155.3 13.8 %collective-permute-start.2 = (f32[64,1152]{1,0:T(8,128)S(1)}, f32[64,1152]{1,0:T(8,128)S(1)}, u32[]{:S(2)}, u32[]{:S(2)}) collective-permute-start(f32[64,1152]{1,0:T(8,128)S(1)} %slice_add_fusion.1), channel_id=1, source_target_pairs={{0,2},{1,3},{2,4},{3,5},{4,6},{5,7},{6,0},{7,1},{8,10},{9,11},{10,... | collective-permute-start | bytes 884744 | tf_op jit(solution)/shard_map/ppermute | solution.py:775
  155.8 13.4 %copy-start = (f32[128,1152]{1,0:T(8,128)S(1)}, f32[128,1152]{1,0:T(8,128)}, u32[]{:S(2)}) copy-start(f32[128,1152]{1,0:T(8,128)} %get-tuple-element.12) | copy-start | bytes 1769476
  155.8 13.4 %copy-start.1 = (bf16[128,1152]{1,0:T(8,128)(2,1)S(1)}, bf16[128,1152]{1,0:T(8,128)(2,1)}, u32[]{:S(2)}) copy-start(bf16[128,1152]{1,0:T(8,128)(2,1)} %get-tuple-element.11) | copy-start | bytes 884740

commit v6 on v5

--- a/solution.py
+++ b/solution.py
@@ -2,6 +2,7 @@
 
 import jax
 import jax.numpy as jnp
+import numpy as np
 from jax import lax
 from jax.experimental import pallas as pl
 from jax.experimental.pallas import tpu as pltpu
@@ -43,7 +44,7 @@
     hid_ref, freq_ref, an_ref, mn_ref, pos_ref, kc_ref, vc_ref,
     wq_ref, wk_ref, wv_ref, wo_ref, wg_ref, wu_ref, wd_ref,
     hid_out, knew_ref, vnew_ref, first_r, first_l, next_r, next_l, own_out,
-    cos_buf, sin_buf, act_buf, an_buf, mn_buf, freq_buf, pos_in, know, vnow, gsrc, gbuf, pos_buf, abuf_w, bbuf_w, gu_w, wd_w, tr_w, y_all, m_buf, part, r_t, r_f,
+    cos_buf, sin_buf, act_buf, an_buf, mn_buf, freq_buf, pos_in, know, vnow, gsrc, gbuf, pos_rows, abuf_w, bbuf_w, gu_w, wd_w, tr_w, y_all, m_buf, part, r_t, r_f,
     kbuf, vbuf, qbuf, abuf, hbuf,
     send_sem, recv_sem, loc_sem, kv_sem, out_sem, in_sem,
 ):
@@ -364,14 +365,8 @@
         for l in range(layers):
             start = pl.multiple_of(jnp.where(lax.rem(x, 2) == 0, chip_cols, 0), 64)
             wd_w[l, pl.ds(start, pad), :] = jnp.zeros((pad, width), BF16)
-        lane_block = lax.div(lax.broadcasted_iota(jnp.int32, (1, LANES), 1), SEQ_GROUP)
-        for g in range(groups):
-            line = pos_in[...]
-            for j in range(heads):
-                moved = pltpu.roll(pos_in[...], ((j - g) * SEQ_GROUP) % LANES, 1)
-                line = jnp.where(lane_block == j, moved, line)
-            pos_buf[g] = line
-        angles = jnp.broadcast_to(pos_in[...].astype(F32), (rows, rows)).T * freq_buf[...]
+        pos_rows[...] = jnp.broadcast_to(pos_in[...].astype(F32), (rows, rows)).T
+        angles = pos_rows[...] * freq_buf[...]
         cos_buf[...] = jnp.cos(angles)
         sin_buf[...] = jnp.sin(angles)
         for i in range(1, n_dev):
@@ -399,40 +394,33 @@
     chunk = 4
 
     def attend(l, group):
-        lane_seq = lax.rem(lax.broadcasted_iota(jnp.int32, (cache_len, LANES), 1), SEQ_GROUP)
         row_seq = lax.rem(lax.broadcasted_iota(jnp.int32, (LANES, cache_len), 0), SEQ_GROUP)
-        row_t = lax.broadcasted_iota(jnp.int32, (cache_len, LANES), 0)
-        lane_new = lax.rem(lax.broadcasted_iota(jnp.int32, (SEQ_GROUP, LANES), 1), SEQ_GROUP)
-        row_new = lax.broadcasted_iota(jnp.int32, (SEQ_GROUP, LANES), 0)
+        place = lax.broadcasted_iota(jnp.int32, (LANES, cache_len), 1).astype(F32)
         i = l * groups + group
         slot = lax.rem(i, KV_SLOTS)
         for copy in kv_copies(i, slot):
             copy.wait()
         seqs = pl.ds(pl.multiple_of(group * SEQ_GROUP, SEQ_GROUP), SEQ_GROUP)
         query = jnp.concatenate([qbuf[j, seqs, :] for j in range(heads)], axis=0)
-        scores = jnp.zeros((cache_len, LANES), F32)
+        scores = jnp.zeros((LANES, cache_len), F32)
         for b in range(0, SEQ_GROUP, chunk):
-            block = kbuf[slot, b:b + chunk].reshape(chunk * cache_len, head_dim)
-            prod = dot_t(block, query)
+            prod = dot_t(query, kbuf[slot, b:b + chunk].reshape(chunk * cache_len, head_dim))
             for j in range(chunk):
-                scores = jnp.where(lane_seq == b + j, prod[j * cache_len:(j + 1) * cache_len], scores)
-        k_new = know[l, seqs, :].astype(BF16)
-        v_new = vnow[l, seqs, :]
-        new_score = jnp.sum(jnp.where(row_new == lane_new, dot_t(k_new, query), 0.0), axis=0, keepdims=True)
-        scores = jnp.where(row_t < pos_buf[group], scores, -1e30)
-        top = jnp.maximum(jnp.max(scores, axis=0, keepdims=True), new_score)
+                scores = jnp.where(row_seq == b + j, prod[:, j * cache_len:(j + 1) * cache_len], scores)
+        k_rep = jnp.concatenate([know[l, seqs, :]] * heads, axis=0)
+        v_rep = jnp.concatenate([vnow[l, seqs, :]] * heads, axis=0)
+        new_score = jnp.sum(query.astype(F32) * k_rep, axis=1, keepdims=True)
+        pos = jnp.concatenate([pos_rows[seqs, :]] * heads, axis=0)
+        scores = jnp.where(place < pos, scores, -1e30)
+        top = jnp.maximum(jnp.max(scores, axis=1, keepdims=True), new_score)
         prob = jnp.exp(scores - top)
         prob_new = jnp.exp(new_score - top)
-        total = jnp.sum(prob, axis=0, keepdims=True) + prob_new
-        prob_t = prob.T
-        total_t = jnp.broadcast_to(total, (LANES, LANES)).T
-        new_t = jnp.broadcast_to(prob_new, (LANES, LANES)).T.astype(BF16).astype(F32)
-        v_rep = jnp.concatenate([v_new] * heads, axis=0)
-        acc = jnp.concatenate([new_t] * (head_dim // LANES), axis=1) * v_rep
+        total = jnp.sum(prob, axis=1, keepdims=True) + prob_new
+        acc = prob_new.astype(BF16).astype(F32) * v_rep
         for b in range(0, SEQ_GROUP, chunk):
-            spread = jnp.concatenate([jnp.where(row_seq == b + j, prob_t, 0.0).astype(BF16) for j in range(chunk)], axis=1)
+            spread = jnp.concatenate([jnp.where(row_seq == b + j, prob, 0.0).astype(BF16) for j in range(chunk)], axis=1)
             acc = acc + dot(spread, vbuf[slot, b:b + chunk].reshape(chunk * cache_len, head_dim))
-        attn = (acc / jnp.concatenate([total_t] * (head_dim // LANES), axis=1)).astype(BF16)
+        attn = (acc / total).astype(BF16)
         for j in range(heads):
             abuf[seqs, j * head_dim:(j + 1) * head_dim] = attn[j * SEQ_GROUP:(j + 1) * SEQ_GROUP, :]
 
@@ -543,17 +531,16 @@
     def near(l):
         if l:
             drain([f"{name}{l - 1}" for name in ("eR2", "eL2", "eR3", "eL3")])
-        down(l, xr)
+        both = dot(jnp.concatenate([m_buf[xr], m_buf[xl]], axis=0), wd_w[l])
+        part[xr] = both[:rows]
+        part[xl] = both[rows:]
         if l == last:
             export(part.at[xr, lower], first_r.at[lower])
+            export(part.at[xl, upper], first_l.at[upper])
             export(part.at[xr, upper], next_r)
+            export(part.at[xl, lower], next_l)
         else:
             send(f"eR2{l}", [(part.at[xr, lower], r_f.at[l, 0, lower])], right)
-        down(l, xl)
-        if l == last:
-            export(part.at[xl, upper], first_l.at[upper])
-            export(part.at[xl, lower], next_l)
-        else:
             send(f"eL2{l}", [(part.at[xl, upper], r_f.at[l, 1, upper])], left)
 
     def far(l):
@@ -634,7 +621,7 @@
     groups = rows // SEQ_GROUP
     assert n_dev == CHIPS * CORES and heads * SEQ_GROUP == LANES and cache_len == LANES and rows == LANES
     assert lax.axis_size("dp") % 2 == 0
-    inv_freq = ROPE_BASE ** (-2.0 * jnp.arange(head_dim // 2, dtype=F32) / head_dim)
+    inv_freq = np.float32(ROPE_BASE) ** (np.float32(-2.0) * np.arange(head_dim // 2, dtype=np.float32) / np.float32(head_dim))
     dims = (layers, rows, width, heads, head_dim, cache_len, n_dev, ff)
     anym = pl.BlockSpec(memory_space=pl.ANY)
     new_shape = jax.ShapeDtypeStruct((layers, rows, head_dim), F32)
@@ -658,7 +645,7 @@
             pltpu.VMEM((layers, rows, head_dim), F32),
             pltpu.VMEM((8, 2 * LANES), F32),
             pltpu.VMEM((n_dev, 8, 2 * LANES), F32),
-            pltpu.VMEM((groups, 1, LANES), jnp.int32),
+            pltpu.VMEM((rows, LANES), F32),
             pltpu.VMEM((layers, 2, CHIPS, CORES, piece, w_query.shape[-1] // 2 + head_dim), BF16),
             pltpu.VMEM((layers, CHIPS, CORES, w_out.shape[1], width), BF16),
             pltpu.VMEM((layers, 2, CHIPS, CORES, piece, win), BF16),
@@ -683,64 +670,49 @@
         ],
         compiler_params=pltpu.CompilerParams(collective_id=0, has_side_effects=True, vmem_limit_bytes=67043328),
         name="decode",
-    )(hidden, inv_freq.reshape(1, head_dim // 2), attn_norm, mlp_norm, positions.reshape(1, rows), k_cache, v_cache, w_query, w_key, w_value, w_out, w_gate, w_up, w_down)
+    )(hidden, jnp.asarray(inv_freq).reshape(1, head_dim // 2), attn_norm, mlp_norm, positions.reshape(1, rows), k_cache, v_cache, w_query, w_key, w_value, w_out, w_gate, w_up, w_down)
 
 
 TILE_ROWS = 16
 CACHE_BLOCK = 16
-CACHE_SLOTS = 12
 
 
 def cache_kernel(pos_ref, old_ref, new_ref, out_ref, buf, in_sem, out_sem):
     layers, rows = old_ref.shape[:2]
     blocks = rows // CACHE_BLOCK
-    steps = layers * blocks
-
-    def split(i):
-        return i // blocks, i % blocks, i % CACHE_SLOTS
-
-    def load(i):
-        l, b, slot = split(i)
-        return pltpu.make_async_copy(old_ref.at[l, pl.ds(b * CACHE_BLOCK, CACHE_BLOCK), 0], buf.at[slot], in_sem.at[slot])
-
-    def store(i):
-        l, b, slot = split(i)
-        return pltpu.make_async_copy(buf.at[slot], out_ref.at[l, pl.ds(b * CACHE_BLOCK, CACHE_BLOCK), 0], out_sem.at[slot])
-
-    ahead = CACHE_SLOTS // 2
-    for i in range(ahead):
-        load(i).start()
+    def load(l, b):
+        i = l * blocks + b
+        return pltpu.make_async_copy(old_ref.at[l, pl.ds(b * CACHE_BLOCK, CACHE_BLOCK), 0], buf.at[i], in_sem.at[i])
+
+    def store(l, b):
+        i = l * blocks + b
+        return pltpu.make_async_copy(buf.at[i], out_ref.at[l, pl.ds(b * CACHE_BLOCK, CACHE_BLOCK), 0], out_sem.at[i])
+
+    steps = [(l, b) for l in range(layers) for b in range(blocks)]
+    for l, b in steps:
+        load(l, b).start()
     row = lax.broadcasted_iota(jnp.int32, (TILE_ROWS, buf.shape[-1]), 0)
-
-    @pl.loop(0, steps)
-    def _(i):
-        load(i).wait()
-        l, b, slot = split(i)
-        fresh = new_ref[l, pl.ds(pl.multiple_of(b * CACHE_BLOCK, CACHE_BLOCK), CACHE_BLOCK), :]
-        tiles = []
-        for s in range(CACHE_BLOCK):
-            pos = pos_ref[b * CACHE_BLOCK + s]
-            base = pl.multiple_of(pos // TILE_ROWS * TILE_ROWS, TILE_ROWS)
-            tile = buf[slot, s, pl.ds(base, TILE_ROWS), :].astype(F32)
-            tiles.append((s, base, jnp.where(row == pos - base, fresh[s:s + 1, :], tile).astype(BF16)))
-        for s, base, tile in tiles:
-            buf[slot, s, pl.ds(base, TILE_ROWS), :] = tile
-        store(i).start()
-
-        @pl.when(i + ahead < steps)
-        def _():
-            @pl.when(i + ahead >= CACHE_SLOTS)
-            def _():
-                store(i + ahead - CACHE_SLOTS).wait()
-            load(i + ahead).start()
-
-    @pl.loop(steps - CACHE_SLOTS, steps)
-    def _(i):
-        store(i).wait()
+    for l in range(layers):
+        @pl.loop(0, blocks)
+        def _(b):
+            load(l, b).wait()
+            fresh = new_ref[l, pl.ds(pl.multiple_of(b * CACHE_BLOCK, CACHE_BLOCK), CACHE_BLOCK), :]
+            tiles = []
+            for s in range(CACHE_BLOCK):
+                pos = pos_ref[b * CACHE_BLOCK + s]
+                base = pl.multiple_of(pos // TILE_ROWS * TILE_ROWS, TILE_ROWS)
+                tile = buf[l * blocks + b, s, pl.ds(base, TILE_ROWS), :].astype(F32)
+                tiles.append((s, base, jnp.where(row == pos - base, fresh[s:s + 1, :], tile).astype(BF16)))
+            for s, base, tile in tiles:
+                buf[l * blocks + b, s, pl.ds(base, TILE_ROWS), :] = tile
+            store(l, b).start()
+    for l, b in steps:
+        store(l, b).wait()
 
 
 def write_cache(positions, cache, new_rows):
     cache_len, head_dim = cache.shape[-2:]
+    slots = cache.shape[0] * cache.shape[1] // CACHE_BLOCK
     vmem, anym = pl.BlockSpec(memory_space=pltpu.VMEM), pl.BlockSpec(memory_space=pl.ANY)
     return pl.pallas_call(
         cache_kernel,
@@ -748,9 +720,9 @@
         in_specs=[pl.BlockSpec(memory_space=pltpu.SMEM), anym, vmem],
         out_specs=anym,
         scratch_shapes=[
-            pltpu.VMEM((CACHE_SLOTS, CACHE_BLOCK, cache_len, head_dim), BF16),
-            pltpu.SemaphoreType.DMA((CACHE_SLOTS,)),
-            pltpu.SemaphoreType.DMA((CACHE_SLOTS,)),
+            pltpu.VMEM((slots, CACHE_BLOCK, cache_len, head_dim), BF16),
+            pltpu.SemaphoreType.DMA((slots,)),
+            pltpu.SemaphoreType.DMA((slots,)),
         ],
         cost_estimate=pl.CostEstimate(flops=10**11, bytes_accessed=4 * cache.size, transcendentals=0),
         compiler_params=pltpu.CompilerParams(vmem_limit_bytes=60 * 2**20),

time: 170 us -> 168 us (0.988)
  Pallas kernels: 164 us -> 162 us
where the time goes in v6:
time: 168 us
  Pallas kernels  162 us (96%)
  starting transfers between devices  4.29 us (3%)
    pallas_call x1, Pallas kernels, decode(): pl.pallas_call(functools.partial(decode_kernel, dims), out_shape=(jax.Sha...  135 us
    pallas_call x2, Pallas kernels, write_cache(): pl.pallas_call(cache_kernel, out_shape=jax.ShapeDtypeStruct(cache.shape,...  26.1 us
  transfers between devices with their start and end apart: 4, of which 0 were waited for; matrix products, arithmetic and copies ran while one was open for 0% of the time, Pallas kernels for 16%

profile of v6, /device:TPU:112, one launch (start us, length us, event | category | flops | bytes accessed | tf_op | source)
XLA Modules:
  0.0 167.6 jit_solution(1628311083730683774)
XLA Ops:
  0.6 135.5 %decode.1 = (bf16[128,1152]{1,0:T(8,128)(2,1)}, f32[2,128,256]{2,1,0:T(8,128)}, f32[2,128,256]{2,1,0:T(8,128)}, f32[128,1152]{1,0:T(8,128)}, f32[128,1152]{1,0:T...) custom-call(bf16[128,1152]{1,0:T(8,128)(2,1)} %hid_ref.1, f32[1,128]{1,0:T(1,128)} %constant.5.freq_ref, ...), custom_call_target="tpu_custom_call" | custom-call | tf_op jit(solution)/shard_map/decode/pallas_call | solution.py:631
  136.1 0.5 collective-permute-start
  136.6 1.6 collective-permute-start.1
  138.2 0.0 copy-start.3
  138.2 0.0 copy-start.2
  138.2 13.1 %cache.2 = bf16[2,128,1,128,256]{4,3,2,1,0:T(8,128)(2,1)} custom-call(s32[128]{0:T(128)} %pos_ref.3, bf16[2,128,1,128,256]{4,3,2,1,0:T(8,128)(2,1)} %old_ref.2, f32[2,128,256]{2,1,0:T(8,128)} %get-tuple-element.17.new_ref), custom_call_target="tpu_custom_call" | custom-call | flops 99999997952 | bytes 33554432 | tf_op jit(solution)/shard_map/cache/pallas_call | solution.py:717
  151.3 0.0 collective-permute-done
  151.3 0.0 copy-done.3
  151.3 1.7 %collective-permute-start.3 = (f32[64,1152]{1,0:T(8,128)S(1)}, f32[64,1152]{1,0:T(8,128)S(1)}, u32[]{:S(2)}, u32[]{:S(2)}) collective-permute-start(f32[64,1152]{1,0:T(8,128)S(1)} %slice_add_fusion), channel_id=1, source_target_pairs={{0,6},{1,7},{2,0},{3,1},{4,2},{5,3},{6,4},{7,5},{8,14},{9,15},{10,... | collective-permute-start | bytes 884744 | tf_op jit(solution)/shard_map/ppermute | solution.py:748
  153.1 0.0 collective-permute-done.1
  153.1 0.0 copy-done.2
  153.1 0.5 collective-permute-start.2
  153.6 0.0 copy-start
  153.6 0.0 copy-start.1
  153.6 13.1 %cache.3 = bf16[2,128,1,128,256]{4,3,2,1,0:T(8,128)(2,1)} custom-call(s32[128]{0:T(128)} %pos_ref.3, bf16[2,128,1,128,256]{4,3,2,1,0:T(8,128)(2,1)} %old_ref.3, f32[2,128,256]{2,1,0:T(8,128)} %get-tuple-element.18.new_ref), custom_call_target="tpu_custom_call" | custom-call | flops 99999997952 | bytes 33554432 | tf_op jit(solution)/shard_map/cache/pallas_call | solution.py:717
  166.7 0.0 collective-permute-done.3
  166.7 0.0 collective-permute-done.2
  166.7 0.0 copy-done
  166.7 0.0 copy-done.1
  166.7 0.9 fusion.1
  (3 shorter events, 0.1 us)
Async XLA Ops:
  136.1 15.2 %collective-permute-start = (f32[128,1152]{1,0:T(8,128)}, f32[128,1152]{1,0:T(8,128)S(1)}, u32[]{:S(2)}, u32[]{:S(2)}) collective-permute-start(f32[128,1152]{1,0:T(8,128)} %get-tuple-element.13), channel_id=1, source_target_pairs={{0,6},{1,7},{2,0},{3,1},{4,2},{5,3},{6,4},{7,5},{8,14},{9,15},{10,... | collective-permute-start | bytes 1769480 | tf_op jit(solution)/shard_map/ppermute | solution.py:745
  136.6 16.5 %collective-permute-start.1 = (f32[128,1152]{1,0:T(8,128)}, f32[128,1152]{1,0:T(8,128)S(1)}, u32[]{:S(2)}, u32[]{:S(2)}) collective-permute-start(f32[128,1152]{1,0:T(8,128)} %get-tuple-element.14), channel_id=1, source_target_pairs={{0,2},{1,3},{2,4},{3,5},{4,6},{5,7},{6,0},{7,1},{8,10},{9,11},{10,... | collective-permute-start | bytes 1769480 | tf_op jit(solution)/shard_map/ppermute | solution.py:744
  138.2 13.1 %copy-start.3 = (f32[64,1152]{1,0:T(8,128)S(1)}, f32[64,1152]{1,0:T(8,128)}, u32[]{:S(2)}) copy-start(f32[64,1152]{1,0:T(8,128)} %get-tuple-element.16) | copy-start | bytes 884740
  138.2 14.9 %copy-start.2 = (f32[64,1152]{1,0:T(8,128)S(1)}, f32[64,1152]{1,0:T(8,128)}, u32[]{:S(2)}) copy-start(f32[64,1152]{1,0:T(8,128)} %get-tuple-element.15) | copy-start | bytes 884740
  151.3 15.3 %collective-permute-start.3 = (f32[64,1152]{1,0:T(8,128)S(1)}, f32[64,1152]{1,0:T(8,128)S(1)}, u32[]{:S(2)}, u32[]{:S(2)}) collective-permute-start(f32[64,1152]{1,0:T(8,128)S(1)} %slice_add_fusion), channel_id=1, source_target_pairs={{0,6},{1,7},{2,0},{3,1},{4,2},{5,3},{6,4},{7,5},{8,14},{9,15},{10,... | collective-permute-start | bytes 884744 | tf_op jit(solution)/shard_map/ppermute | solution.py:748
  153.1 13.6 %collective-permute-start.2 = (f32[64,1152]{1,0:T(8,128)S(1)}, f32[64,1152]{1,0:T(8,128)S(1)}, u32[]{:S(2)}, u32[]{:S(2)}) collective-permute-start(f32[64,1152]{1,0:T(8,128)S(1)} %slice_add_fusion.1), channel_id=1, source_target_pairs={{0,2},{1,3},{2,4},{3,5},{4,6},{5,7},{6,0},{7,1},{8,10},{9,11},{10,... | collective-permute-start | bytes 884744 | tf_op jit(solution)/shard_map/ppermute | solution.py:747
  153.6 13.1 %copy-start = (f32[128,1152]{1,0:T(8,128)S(1)}, f32[128,1152]{1,0:T(8,128)}, u32[]{:S(2)}) copy-start(f32[128,1152]{1,0:T(8,128)} %get-tuple-element.12) | copy-start | bytes 1769476
  153.6 13.1 %copy-start.1 = (bf16[128,1152]{1,0:T(8,128)(2,1)S(1)}, bf16[128,1152]{1,0:T(8,128)(2,1)}, u32[]{:S(2)}) copy-start(bf16[128,1152]{1,0:T(8,128)(2,1)} %get-tuple-element.11) | copy-start | bytes 884740

commit v7 on v6

--- a/solution.py
+++ b/solution.py
@@ -29,11 +29,11 @@
 
 
 ORDER = (
-    "bo0", "ao0", "ce0", "in0", "bp0", "af0", "ct0", "bf0", "cd0", "dt1", "ap0", "ao1", "ce1", "cm0", "at0", "ax0",
-    "cf0", "cn0", "bx0", "aw0", "dt0", "af1", "qkv0", "att0", "bo1", "att0", "cx0", "ct1", "att0", "bt0", "bw0", "att0",
-    "mix0", "cm1", "cf1", "yf0", "cw0", "cu0", "ap1", "cd1", "gua0", "dr0", "near0", "ax1", "gub0", "far0", "cn1", "cu1",
-    "aw1", "er0", "bf1", "guo0", "at1", "own0", "cx1", "done0", "qkv1", "att1", "att1", "bx1", "bt1", "att1", "att1", "mix1",
-    "cw1", "yf1", "guo1", "dr1", "own1", "gua1", "near1", "gub1", "far1",
+    "bo0", "ao0", "in0", "bp0", "bq0", "bf0", "ct0", "ap0", "af0", "cd0", "ce0", "cf0", "ax0", "cd1", "bx0", "at0",
+    "ao1", "cn0", "aw0", "ce1", "bw0", "bt0", "qkv0", "att0", "ct1", "cx0", "att0", "att0", "af1", "att0", "cm0", "mix0",
+    "cu0", "ax1", "ap1", "yf0", "bo1", "dt0", "cw0", "cf1", "at1", "cm1", "gua0", "dr0", "near0", "gub0", "dt1", "cx1",
+    "far0", "cn1", "er0", "guo0", "bf1", "own0", "aw1", "cu1", "done0", "qkv1", "att1", "att1", "bx1", "bt1", "att1", "att1",
+    "mix1", "cw1", "yf1", "guo1", "dr1", "own1", "gua1", "near1", "gub1", "far1",
 )
 SHARE_A = (True, True)
 SHARE_B = (True, False)
@@ -74,6 +74,7 @@
     b_mine = pl.multiple_of(h * b_half, b_quarter)
     b_mid = pl.multiple_of(h * b_half + b_quarter, b_quarter)
     b_other = pl.multiple_of(hh * b_half, b_quarter)
+    b_last = pl.multiple_of(hh * b_half + b_quarter, b_quarter)
     q_mine = pl.multiple_of(h * q_half, LANES)
     kv_mine = pl.multiple_of(h * kv_half, LANES)
     starts = [pl.multiple_of(lax.div(chip_cols * xx, LANES) * LANES, LANES) for xx in (x, xr, xo, xl)]
@@ -210,13 +211,30 @@
         return bbuf_w.at[l, xx, c, pl.ds(b_mid, b_quarter)] if SHARE_B[l] else bbuf_w.at[l, xx, c, pl.ds(b_half, b_half)]
 
     def bo(l):
-        src = wo_ref.at[l, pl.ds(b_mine, b_half)] if SHARE_B[l] else wo_ref.at[l]
-        send(f"bR{l}", [(src, b_block(l, x))], right)
-        send(f"bL{l}", [(src, b_block(l, x))], left)
+        if not SHARE_B[l]:
+            send(f"bR{l}", [(wo_ref.at[l], b_block(l, x))], right)
+            send(f"bL{l}", [(wo_ref.at[l], b_block(l, x))], left)
+            return
+        for name, start, view in (("b", b_mine, b_lead(l, x)), ("bb", b_mid, b_tail(l, x))):
+            src = wo_ref.at[l, pl.ds(start, b_quarter)]
+            send(f"{name}R{l}", [(src, view)], right)
+            send(f"{name}L{l}", [(src, view)], left)
+
+    def b_near_lead(l):
+        got(f"bR{l}", b_lead(l, xl))
+        got(f"bL{l}", b_lead(l, xr))
+
+    def b_near_tail(l):
+        got(f"bbR{l}", b_tail(l, xl))
+        got(f"bbL{l}", b_tail(l, xr))
 
     def b_near(l):
-        got(f"bR{l}", b_block(l, xl))
-        got(f"bL{l}", b_block(l, xr))
+        if SHARE_B[l]:
+            b_near_lead(l)
+            b_near_tail(l)
+        else:
+            got(f"bR{l}", b_block(l, xl))
+            got(f"bL{l}", b_block(l, xr))
 
     def b_far(l):
         got(f"bfR{l}", b_lead(l, xo))
@@ -228,9 +246,14 @@
         send(f"bfL{l}", [(b_tail(l, xr), b_tail(l, xr))], left)
 
     def bp(l):
-        b_near(l)
-        to_pair(f"pbR{l}", b_block(l, xl))
-        to_pair(f"pbL{l}", b_block(l, xr))
+        b_near_lead(l)
+        to_pair(f"pbR{l}", b_lead(l, xl))
+        to_pair(f"pbL{l}", b_lead(l, xr))
+
+    def bq(l):
+        b_near_tail(l)
+        to_pair(f"pbbR{l}", b_tail(l, xl))
+        to_pair(f"pbbL{l}", b_tail(l, xr))
 
     def bx(l):
         b_far(l)
@@ -245,8 +268,10 @@
         send(f"bT{l}", [(view, view)], twin)
 
     def bw(l):
-        for name, xx in (("pbR", xl), ("pbL", xr), ("pbF", xo)):
-            got(f"{name}{l}", bbuf_w.at[l, xx, c, pl.ds(b_other, b_half)])
+        for name, xx in (("R", xl), ("L", xr)):
+            got(f"pb{name}{l}", bbuf_w.at[l, xx, c, pl.ds(b_other, b_quarter)])
+            got(f"pbb{name}{l}", bbuf_w.at[l, xx, c, pl.ds(b_last, b_quarter)])
+        got(f"pbF{l}", bbuf_w.at[l, xo, c, pl.ds(b_other, b_half)])
         local_wait(4 * l + 1, bbuf_w.at[l, x, c])
         view = bbuf_w.at[l, :, c, pl.ds(b_other, b_half)]
         send(f"bT1{l}", [(view, view)], twin)
@@ -576,7 +601,7 @@
         hbuf[...] = (hbuf[...].astype(F32) + (part[x] + r_f[l, 0] + r_f[l, 1])).astype(BF16)
 
     table = dict(
-        ao=ao, af=af, ap=ap, ax=ax, at=at, aw=aw, bo=bo, bf=bf, bp=bp, bx=bx, bt=bt, bw=bw, cd=cd, ce=ce, ct=ct, cf=cf,
+        ao=ao, af=af, ap=ap, ax=ax, at=at, aw=aw, bo=bo, bf=bf, bp=bp, bq=bq, bx=bx, bt=bt, bw=bw, cd=cd, ce=ce, ct=ct, cf=cf,
         cn=cn, cm=cm, cx=cx, cu=cu, cw=cw, dt=dt, **{"in": entry},
         qkv=qkv, mix=mix, yf=yf, guo=guo, gua=gua, gub=gub, dr=d_ready, near=near, far=far, er=er, own=own, done=done,
     )

time: 168 us -> 168 us (level)
  transfers between devices with their start and end apart: 4 -> 4, of which waited for: 0 -> 1; matrix products, arithmetic and copies ran while one was open for 0% -> 0% of each run, Pallas kernels for 16% -> 16%
where the time goes in v7:
time: 168 us
  Pallas kernels  161 us (96%)
  starting transfers between devices  4.48 us (3%)
    pallas_call x1, Pallas kernels, decode(): pl.pallas_call(functools.partial(decode_kernel, dims), out_shape=(jax.Sha...  135 us
    pallas_call x2, Pallas kernels, write_cache(): pl.pallas_call(cache_kernel, out_shape=jax.ShapeDtypeStruct(cache.shape,...  26.2 us
  transfers between devices with their start and end apart: 4, of which 1 were waited for; matrix products, arithmetic and copies ran while one was open for 0% of the time, Pallas kernels for 16%

profile of v7, /device:TPU:112, one launch (start us, length us, event | category | flops | bytes accessed | tf_op | source)
XLA Modules:
  0.0 167.8 jit_solution(9114920977575137279)
XLA Ops:
  0.6 135.2 %decode.1 = (bf16[128,1152]{1,0:T(8,128)(2,1)}, f32[2,128,256]{2,1,0:T(8,128)}, f32[2,128,256]{2,1,0:T(8,128)}, f32[128,1152]{1,0:T(8,128)}, f32[128,1152]{1,0:T...) custom-call(bf16[128,1152]{1,0:T(8,128)(2,1)} %hid_ref.1, f32[1,128]{1,0:T(1,128)} %constant.5.freq_ref, ...), custom_call_target="tpu_custom_call" | custom-call | tf_op jit(solution)/shard_map/decode/pallas_call | solution.py:656
  135.8 0.6 collective-permute-start
  136.4 1.5 collective-permute-start.1
  137.9 0.0 copy-start.3
  137.9 0.0 copy-start.2
  137.9 13.1 %cache.2 = bf16[2,128,1,128,256]{4,3,2,1,0:T(8,128)(2,1)} custom-call(s32[128]{0:T(128)} %pos_ref.3, bf16[2,128,1,128,256]{4,3,2,1,0:T(8,128)(2,1)} %old_ref.2, f32[2,128,256]{2,1,0:T(8,128)} %get-tuple-element.17.new_ref), custom_call_target="tpu_custom_call" | custom-call | flops 99999997952 | bytes 33554432 | tf_op jit(solution)/shard_map/cache/pallas_call | solution.py:742
  151.1 0.1 collective-permute-done
  151.2 0.0 copy-done.3
  151.2 2.3 %collective-permute-start.3 = (f32[64,1152]{1,0:T(8,128)S(1)}, f32[64,1152]{1,0:T(8,128)S(1)}, u32[]{:S(2)}, u32[]{:S(2)}) collective-permute-start(f32[64,1152]{1,0:T(8,128)S(1)} %slice_add_fusion), channel_id=1, source_target_pairs={{0,6},{1,7},{2,0},{3,1},{4,2},{5,3},{6,4},{7,5},{8,14},{9,15},{10,... | collective-permute-start | bytes 884744 | tf_op jit(solution)/shard_map/ppermute | solution.py:773
  153.5 0.0 collective-permute-done.1
  153.5 0.0 copy-done.2
  153.6 0.1 collective-permute-start.2
  153.7 0.0 copy-start
  153.7 0.0 copy-start.1
  153.7 13.1 %cache.3 = bf16[2,128,1,128,256]{4,3,2,1,0:T(8,128)(2,1)} custom-call(s32[128]{0:T(128)} %pos_ref.3, bf16[2,128,1,128,256]{4,3,2,1,0:T(8,128)(2,1)} %old_ref.3, f32[2,128,256]{2,1,0:T(8,128)} %get-tuple-element.18.new_ref), custom_call_target="tpu_custom_call" | custom-call | flops 99999997952 | bytes 33554432 | tf_op jit(solution)/shard_map/cache/pallas_call | solution.py:742
  166.8 0.0 collective-permute-done.3
  166.9 0.0 collective-permute-done.2
  166.9 0.0 copy-done
  166.9 0.0 copy-done.1
  166.9 0.9 fusion.1
  (3 shorter events, 0.1 us)
Async XLA Ops:
  135.8 15.4 %collective-permute-start = (f32[128,1152]{1,0:T(8,128)}, f32[128,1152]{1,0:T(8,128)S(1)}, u32[]{:S(2)}, u32[]{:S(2)}) collective-permute-start(f32[128,1152]{1,0:T(8,128)} %get-tuple-element.13), channel_id=1, source_target_pairs={{0,6},{1,7},{2,0},{3,1},{4,2},{5,3},{6,4},{7,5},{8,14},{9,15},{10,... | collective-permute-start | bytes 1769480 | tf_op jit(solution)/shard_map/ppermute | solution.py:770
  136.4 17.1 %collective-permute-start.1 = (f32[128,1152]{1,0:T(8,128)}, f32[128,1152]{1,0:T(8,128)S(1)}, u32[]{:S(2)}, u32[]{:S(2)}) collective-permute-start(f32[128,1152]{1,0:T(8,128)} %get-tuple-element.14), channel_id=1, source_target_pairs={{0,2},{1,3},{2,4},{3,5},{4,6},{5,7},{6,0},{7,1},{8,10},{9,11},{10,... | collective-permute-start | bytes 1769480 | tf_op jit(solution)/shard_map/ppermute | solution.py:769
  137.9 13.3 %copy-start.3 = (f32[64,1152]{1,0:T(8,128)S(1)}, f32[64,1152]{1,0:T(8,128)}, u32[]{:S(2)}) copy-start(f32[64,1152]{1,0:T(8,128)} %get-tuple-element.16) | copy-start | bytes 884740
  137.9 15.6 %copy-start.2 = (f32[64,1152]{1,0:T(8,128)S(1)}, f32[64,1152]{1,0:T(8,128)}, u32[]{:S(2)}) copy-start(f32[64,1152]{1,0:T(8,128)} %get-tuple-element.15) | copy-start | bytes 884740
  151.2 15.6 %collective-permute-start.3 = (f32[64,1152]{1,0:T(8,128)S(1)}, f32[64,1152]{1,0:T(8,128)S(1)}, u32[]{:S(2)}, u32[]{:S(2)}) collective-permute-start(f32[64,1152]{1,0:T(8,128)S(1)} %slice_add_fusion), channel_id=1, source_target_pairs={{0,6},{1,7},{2,0},{3,1},{4,2},{5,3},{6,4},{7,5},{8,14},{9,15},{10,... | collective-permute-start | bytes 884744 | tf_op jit(solution)/shard_map/ppermute | solution.py:773
  153.6 13.3 %collective-permute-start.2 = (f32[64,1152]{1,0:T(8,128)S(1)}, f32[64,1152]{1,0:T(8,128)S(1)}, u32[]{:S(2)}, u32[]{:S(2)}) collective-permute-start(f32[64,1152]{1,0:T(8,128)S(1)} %slice_add_fusion.1), channel_id=1, source_target_pairs={{0,2},{1,3},{2,4},{3,5},{4,6},{5,7},{6,0},{7,1},{8,10},{9,11},{10,... | collective-permute-start | bytes 884744 | tf_op jit(solution)/shard_map/ppermute | solution.py:772
  153.7 13.2 %copy-start = (f32[128,1152]{1,0:T(8,128)S(1)}, f32[128,1152]{1,0:T(8,128)}, u32[]{:S(2)}) copy-start(f32[128,1152]{1,0:T(8,128)} %get-tuple-element.12) | copy-start | bytes 1769476
  153.7 13.2 %copy-start.1 = (bf16[128,1152]{1,0:T(8,128)(2,1)S(1)}, bf16[128,1152]{1,0:T(8,128)(2,1)}, u32[]{:S(2)}) copy-start(bf16[128,1152]{1,0:T(8,128)(2,1)} %get-tuple-element.11) | copy-start | bytes 884740

commit v8 on v7

--- a/solution.py
+++ b/solution.py
@@ -730,7 +730,8 @@
                 tiles.append((s, base, jnp.where(row == pos - base, fresh[s:s + 1, :], tile).astype(BF16)))
             for s, base, tile in tiles:
                 buf[l * blocks + b, s, pl.ds(base, TILE_ROWS), :] = tile
-            store(l, b).start()
+    for l, b in steps:
+        store(l, b).start()
     for l, b in steps:
         store(l, b).wait()
 

time: 168 us -> 168 us (level)
  transfers between devices with their start and end apart: 4 -> 4, of which waited for: 1 -> 1; matrix products, arithmetic and copies ran while one was open for 0% -> 0% of each run, Pallas kernels for 16% -> 15%
where the time goes in v8:
time: 168 us
  Pallas kernels  161 us (96%)
  starting transfers between devices  4.48 us (3%)
    pallas_call x1, Pallas kernels, decode(): pl.pallas_call(functools.partial(decode_kernel, dims), out_shape=(jax.Sha...  135 us
    pallas_call x2, Pallas kernels, write_cache(): pl.pallas_call(cache_kernel, out_shape=jax.ShapeDtypeStruct(cache.shape,...  25.9 us
  transfers between devices with their start and end apart: 4, of which 1 were waited for; matrix products, arithmetic and copies ran while one was open for 0% of the time, Pallas kernels for 15%

profile of v8, /device:TPU:112, one launch (start us, length us, event | category | flops | bytes accessed | tf_op | source)
XLA Modules:
  0.0 167.6 jit_solution(2651486880650214706)
XLA Ops:
  0.6 135.2 %decode.1 = (bf16[128,1152]{1,0:T(8,128)(2,1)}, f32[2,128,256]{2,1,0:T(8,128)}, f32[2,128,256]{2,1,0:T(8,128)}, f32[128,1152]{1,0:T(8,128)}, f32[128,1152]{1,0:T...) custom-call(bf16[128,1152]{1,0:T(8,128)(2,1)} %hid_ref.1, f32[1,128]{1,0:T(1,128)} %constant.5.freq_ref, ...), custom_call_target="tpu_custom_call" | custom-call | tf_op jit(solution)/shard_map/decode/pallas_call | solution.py:656
  135.8 0.6 collective-permute-start
  136.4 1.5 collective-permute-start.1
  137.9 0.0 copy-start.3
  137.9 0.0 copy-start.2
  137.9 13.0 %cache.2 = bf16[2,128,1,128,256]{4,3,2,1,0:T(8,128)(2,1)} custom-call(s32[128]{0:T(128)} %pos_ref.3, bf16[2,128,1,128,256]{4,3,2,1,0:T(8,128)(2,1)} %old_ref.2, f32[2,128,256]{2,1,0:T(8,128)} %get-tuple-element.17.new_ref), custom_call_target="tpu_custom_call" | custom-call | flops 99999997952 | bytes 33554432 | tf_op jit(solution)/shard_map/cache/pallas_call | solution.py:743
  150.9 0.3 collective-permute-done
  151.2 0.0 copy-done.3
  151.2 2.3 %collective-permute-start.3 = (f32[64,1152]{1,0:T(8,128)S(1)}, f32[64,1152]{1,0:T(8,128)S(1)}, u32[]{:S(2)}, u32[]{:S(2)}) collective-permute-start(f32[64,1152]{1,0:T(8,128)S(1)} %slice_add_fusion), channel_id=1, source_target_pairs={{0,6},{1,7},{2,0},{3,1},{4,2},{5,3},{6,4},{7,5},{8,14},{9,15},{10,... | collective-permute-start | bytes 884744 | tf_op jit(solution)/shard_map/ppermute | solution.py:774
  153.5 0.0 collective-permute-done.1
  153.5 0.0 copy-done.2
  153.6 0.1 collective-permute-start.2
  153.7 0.0 copy-start
  153.7 0.0 copy-start.1
  153.7 13.0 %cache.3 = bf16[2,128,1,128,256]{4,3,2,1,0:T(8,128)(2,1)} custom-call(s32[128]{0:T(128)} %pos_ref.3, bf16[2,128,1,128,256]{4,3,2,1,0:T(8,128)(2,1)} %old_ref.3, f32[2,128,256]{2,1,0:T(8,128)} %get-tuple-element.18.new_ref), custom_call_target="tpu_custom_call" | custom-call | flops 99999997952 | bytes 33554432 | tf_op jit(solution)/shard_map/cache/pallas_call | solution.py:743
  166.7 0.0 collective-permute-done.3
  166.7 0.0 collective-permute-done.2
  166.7 0.0 copy-done
  166.7 0.0 copy-done.1
  166.7 0.9 fusion.1
  (3 shorter events, 0.1 us)
Async XLA Ops:
  135.8 15.4 %collective-permute-start = (f32[128,1152]{1,0:T(8,128)}, f32[128,1152]{1,0:T(8,128)S(1)}, u32[]{:S(2)}, u32[]{:S(2)}) collective-permute-start(f32[128,1152]{1,0:T(8,128)} %get-tuple-element.13), channel_id=1, source_target_pairs={{0,6},{1,7},{2,0},{3,1},{4,2},{5,3},{6,4},{7,5},{8,14},{9,15},{10,... | collective-permute-start | bytes 1769480 | tf_op jit(solution)/shard_map/ppermute | solution.py:771
  136.4 17.1 %collective-permute-start.1 = (f32[128,1152]{1,0:T(8,128)}, f32[128,1152]{1,0:T(8,128)S(1)}, u32[]{:S(2)}, u32[]{:S(2)}) collective-permute-start(f32[128,1152]{1,0:T(8,128)} %get-tuple-element.14), channel_id=1, source_target_pairs={{0,2},{1,3},{2,4},{3,5},{4,6},{5,7},{6,0},{7,1},{8,10},{9,11},{10,... | collective-permute-start | bytes 1769480 | tf_op jit(solution)/shard_map/ppermute | solution.py:770
  137.9 13.3 %copy-start.3 = (f32[64,1152]{1,0:T(8,128)S(1)}, f32[64,1152]{1,0:T(8,128)}, u32[]{:S(2)}) copy-start(f32[64,1152]{1,0:T(8,128)} %get-tuple-element.16) | copy-start | bytes 884740
  137.9 15.6 %copy-start.2 = (f32[64,1152]{1,0:T(8,128)S(1)}, f32[64,1152]{1,0:T(8,128)}, u32[]{:S(2)}) copy-start(f32[64,1152]{1,0:T(8,128)} %get-tuple-element.15) | copy-start | bytes 884740
  151.2 15.4 %collective-permute-start.3 = (f32[64,1152]{1,0:T(8,128)S(1)}, f32[64,1152]{1,0:T(8,128)S(1)}, u32[]{:S(2)}, u32[]{:S(2)}) collective-permute-start(f32[64,1152]{1,0:T(8,128)S(1)} %slice_add_fusion), channel_id=1, source_target_pairs={{0,6},{1,7},{2,0},{3,1},{4,2},{5,3},{6,4},{7,5},{8,14},{9,15},{10,... | collective-permute-start | bytes 884744 | tf_op jit(solution)/shard_map/ppermute | solution.py:774
  153.6 13.1 %collective-permute-start.2 = (f32[64,1152]{1,0:T(8,128)S(1)}, f32[64,1152]{1,0:T(8,128)S(1)}, u32[]{:S(2)}, u32[]{:S(2)}) collective-permute-start(f32[64,1152]{1,0:T(8,128)S(1)} %slice_add_fusion.1), channel_id=1, source_target_pairs={{0,2},{1,3},{2,4},{3,5},{4,6},{5,7},{6,0},{7,1},{8,10},{9,11},{10,... | collective-permute-start | bytes 884744 | tf_op jit(solution)/shard_map/ppermute | solution.py:773
  153.7 13.0 %copy-start = (f32[128,1152]{1,0:T(8,128)S(1)}, f32[128,1152]{1,0:T(8,128)}, u32[]{:S(2)}) copy-start(f32[128,1152]{1,0:T(8,128)} %get-tuple-element.12) | copy-start | bytes 1769476
  153.7 13.0 %copy-start.1 = (bf16[128,1152]{1,0:T(8,128)(2,1)S(1)}, bf16[128,1152]{1,0:T(8,128)(2,1)}, u32[]{:S(2)}) copy-start(bf16[128,1152]{1,0:T(8,128)(2,1)} %get-tuple-element.11) | copy-start | bytes 884740

commit v9 on v8

--- a/solution.py
+++ b/solution.py
@@ -31,9 +31,9 @@
 ORDER = (
     "bo0", "ao0", "in0", "bp0", "bq0", "bf0", "ct0", "ap0", "af0", "cd0", "ce0", "cf0", "ax0", "cd1", "bx0", "at0",
     "ao1", "cn0", "aw0", "ce1", "bw0", "bt0", "qkv0", "att0", "ct1", "cx0", "att0", "att0", "af1", "att0", "cm0", "mix0",
-    "cu0", "ax1", "ap1", "yf0", "bo1", "dt0", "cw0", "cf1", "at1", "cm1", "gua0", "dr0", "near0", "gub0", "dt1", "cx1",
-    "far0", "cn1", "er0", "guo0", "bf1", "own0", "aw1", "cu1", "done0", "qkv1", "att1", "att1", "bx1", "bt1", "att1", "att1",
-    "mix1", "cw1", "yf1", "guo1", "dr1", "own1", "gua1", "near1", "gub1", "far1",
+    "cu0", "cv0", "ax1", "ap1", "yf0", "bo1", "dt0", "cw0", "cf1", "at1", "cm1", "gua0", "dr0", "near0", "gub0", "dt1",
+    "cx1", "far0", "cn1", "er0", "guo0", "bf1", "own0", "aw1", "cu1", "done0", "qkv1", "att1", "att1", "bx1", "bt1", "cv1",
+    "att1", "att1", "mix1", "cw1", "yf1", "guo1", "dr1", "own1", "gua1", "near1", "gub1", "far1",
 )
 SHARE_A = (True, True)
 SHARE_B = (True, False)
@@ -340,17 +340,32 @@
         view = gu_w.at[l, h, :, c]
         send(f"cT{l}", [(view, view)], twin)
 
-    def cw(l):
-        for name, xx, cols in (("pcR", xl, fore), ("pcL", xr, fore), ("pdR", xl, aft), ("pdL", xr, aft)):
-            got(f"{name}{l}", gu_w.at[l, hh, xx, c, :, cols])
+    def late_half(l):
+        return ("pd", aft) if l == 0 else ("pc", fore)
+
+    def early_half(l):
+        return ("pc", fore) if l == 0 else ("pd", aft)
+
+    def cv(l):
+        name, cols = early_half(l)
+        got(f"{name}R{l}", gu_w.at[l, hh, xl, c, :, cols])
+        got(f"{name}L{l}", gu_w.at[l, hh, xr, c, :, cols])
         got(f"pcF{l}", gu_w.at[l, hh, xo, c])
         local_wait(4 * l + 2, gu_w.at[l, :, x, c])
-        view = gu_w.at[l, hh, :, c]
-        send(f"cT1{l}", [(view, view)], twin)
+        views = [gu_w.at[l, hh, xx, c] for xx in (x, xo)] + [gu_w.at[l, hh, xx, c, :, cols] for xx in (xl, xr)]
+        send(f"cT1{l}", [(view, view) for view in views], twin, gu_w.at[l, hh, pl.ds(0, 3), c])
+
+    def cw(l):
+        name, cols = late_half(l)
+        got(f"{name}R{l}", gu_w.at[l, hh, xl, c, :, cols])
+        got(f"{name}L{l}", gu_w.at[l, hh, xr, c, :, cols])
+        views = [gu_w.at[l, hh, xx, c, :, cols] for xx in (xl, xr)]
+        send(f"cT2{l}", [(view, view) for view in views], twin, gu_w.at[l, hh, xo, c])
 
     def c_ready(l):
         got(f"cT{l}", gu_w.at[l, h, :, cc])
-        got(f"cT1{l}", gu_w.at[l, hh, :, cc])
+        got(f"cT1{l}", gu_w.at[l, hh, pl.ds(0, 3), cc])
+        got(f"cT2{l}", gu_w.at[l, hh, xo, cc])
 
     def dt(l):
         send(f"dT{l}", [(wd_ref.at[l], wd_w.at[l, wd_mine])], twin)
@@ -602,7 +617,7 @@
 
     table = dict(
         ao=ao, af=af, ap=ap, ax=ax, at=at, aw=aw, bo=bo, bf=bf, bp=bp, bq=bq, bx=bx, bt=bt, bw=bw, cd=cd, ce=ce, ct=ct, cf=cf,
-        cn=cn, cm=cm, cx=cx, cu=cu, cw=cw, dt=dt, **{"in": entry},
+        cn=cn, cm=cm, cx=cx, cu=cu, cv=cv, cw=cw, dt=dt, **{"in": entry},
         qkv=qkv, mix=mix, yf=yf, guo=guo, gua=gua, gub=gub, dr=d_ready, near=near, far=far, er=er, own=own, done=done,
     )
 

time: 168 us -> 167 us (level)
  transfers between devices with their start and end apart: 4 -> 4, of which waited for: 1 -> 0; matrix products, arithmetic and copies ran while one was open for 0% -> 0% of each run, Pallas kernels for 15% -> 16%
where the time goes in v9:
time: 167 us
  Pallas kernels  161 us (96%)
  starting transfers between devices  4.29 us (3%)
    pallas_call x1, Pallas kernels, decode(): pl.pallas_call(functools.partial(decode_kernel, dims), out_shape=(jax.Sha...  135 us
    pallas_call x2, Pallas kernels, write_cache(): pl.pallas_call(cache_kernel, out_shape=jax.ShapeDtypeStruct(cache.shape,...  25.9 us
  transfers between devices with their start and end apart: 4, of which 0 were waited for; matrix products, arithmetic and copies ran while one was open for 0% of the time, Pallas kernels for 16%

profile of v9, /device:TPU:112, one launch (start us, length us, event | category | flops | bytes accessed | tf_op | source)
XLA Modules:
  0.0 167.2 jit_solution(6149087963076503712)
XLA Ops:
  0.6 135.3 %decode.1 = (bf16[128,1152]{1,0:T(8,128)(2,1)}, f32[2,128,256]{2,1,0:T(8,128)}, f32[2,128,256]{2,1,0:T(8,128)}, f32[128,1152]{1,0:T(8,128)}, f32[128,1152]{1,0:T...) custom-call(bf16[128,1152]{1,0:T(8,128)(2,1)} %hid_ref.1, f32[1,128]{1,0:T(1,128)} %constant.5.freq_ref, ...), custom_call_target="tpu_custom_call" | custom-call | tf_op jit(solution)/shard_map/decode/pallas_call | solution.py:671
  135.9 0.6 collective-permute-start
  136.5 1.5 collective-permute-start.1
  138.0 0.0 copy-start.3
  138.0 0.0 copy-start.2
  138.0 13.0 %cache.2 = bf16[2,128,1,128,256]{4,3,2,1,0:T(8,128)(2,1)} custom-call(s32[128]{0:T(128)} %pos_ref.3, bf16[2,128,1,128,256]{4,3,2,1,0:T(8,128)(2,1)} %old_ref.2, f32[2,128,256]{2,1,0:T(8,128)} %get-tuple-element.17.new_ref), custom_call_target="tpu_custom_call" | custom-call | flops 99999997952 | bytes 33554432 | tf_op jit(solution)/shard_map/cache/pallas_call | solution.py:758
  151.0 0.0 collective-permute-done
  151.0 0.0 copy-done.3
  151.0 1.8 %collective-permute-start.3 = (f32[64,1152]{1,0:T(8,128)S(1)}, f32[64,1152]{1,0:T(8,128)S(1)}, u32[]{:S(2)}, u32[]{:S(2)}) collective-permute-start(f32[64,1152]{1,0:T(8,128)S(1)} %slice_add_fusion), channel_id=1, source_target_pairs={{0,6},{1,7},{2,0},{3,1},{4,2},{5,3},{6,4},{7,5},{8,14},{9,15},{10,... | collective-permute-start | bytes 884744 | tf_op jit(solution)/shard_map/ppermute | solution.py:789
  152.8 0.0 collective-permute-done.1
  152.8 0.0 copy-done.2
  152.9 0.4 collective-permute-start.2
  153.3 0.0 copy-start
  153.3 0.0 copy-start.1
  153.3 13.0 %cache.3 = bf16[2,128,1,128,256]{4,3,2,1,0:T(8,128)(2,1)} custom-call(s32[128]{0:T(128)} %pos_ref.3, bf16[2,128,1,128,256]{4,3,2,1,0:T(8,128)(2,1)} %old_ref.3, f32[2,128,256]{2,1,0:T(8,128)} %get-tuple-element.18.new_ref), custom_call_target="tpu_custom_call" | custom-call | flops 99999997952 | bytes 33554432 | tf_op jit(solution)/shard_map/cache/pallas_call | solution.py:758
  166.3 0.0 collective-permute-done.3
  166.3 0.0 collective-permute-done.2
  166.3 0.0 copy-done
  166.3 0.0 copy-done.1
  166.3 0.9 fusion.1
  (3 shorter events, 0.1 us)
Async XLA Ops:
  135.9 15.1 %collective-permute-start = (f32[128,1152]{1,0:T(8,128)}, f32[128,1152]{1,0:T(8,128)S(1)}, u32[]{:S(2)}, u32[]{:S(2)}) collective-permute-start(f32[128,1152]{1,0:T(8,128)} %get-tuple-element.13), channel_id=1, source_target_pairs={{0,6},{1,7},{2,0},{3,1},{4,2},{5,3},{6,4},{7,5},{8,14},{9,15},{10,... | collective-permute-start | bytes 1769480 | tf_op jit(solution)/shard_map/ppermute | solution.py:786
  136.5 16.3 %collective-permute-start.1 = (f32[128,1152]{1,0:T(8,128)}, f32[128,1152]{1,0:T(8,128)S(1)}, u32[]{:S(2)}, u32[]{:S(2)}) collective-permute-start(f32[128,1152]{1,0:T(8,128)} %get-tuple-element.14), channel_id=1, source_target_pairs={{0,2},{1,3},{2,4},{3,5},{4,6},{5,7},{6,0},{7,1},{8,10},{9,11},{10,... | collective-permute-start | bytes 1769480 | tf_op jit(solution)/shard_map/ppermute | solution.py:785
  138.0 13.0 %copy-start.3 = (f32[64,1152]{1,0:T(8,128)S(1)}, f32[64,1152]{1,0:T(8,128)}, u32[]{:S(2)}) copy-start(f32[64,1152]{1,0:T(8,128)} %get-tuple-element.16) | copy-start | bytes 884740
  138.0 14.8 %copy-start.2 = (f32[64,1152]{1,0:T(8,128)S(1)}, f32[64,1152]{1,0:T(8,128)}, u32[]{:S(2)}) copy-start(f32[64,1152]{1,0:T(8,128)} %get-tuple-element.15) | copy-start | bytes 884740
  151.0 15.2 %collective-permute-start.3 = (f32[64,1152]{1,0:T(8,128)S(1)}, f32[64,1152]{1,0:T(8,128)S(1)}, u32[]{:S(2)}, u32[]{:S(2)}) collective-permute-start(f32[64,1152]{1,0:T(8,128)S(1)} %slice_add_fusion), channel_id=1, source_target_pairs={{0,6},{1,7},{2,0},{3,1},{4,2},{5,3},{6,4},{7,5},{8,14},{9,15},{10,... | collective-permute-start | bytes 884744 | tf_op jit(solution)/shard_map/ppermute | solution.py:789
  152.9 13.4 %collective-permute-start.2 = (f32[64,1152]{1,0:T(8,128)S(1)}, f32[64,1152]{1,0:T(8,128)S(1)}, u32[]{:S(2)}, u32[]{:S(2)}) collective-permute-start(f32[64,1152]{1,0:T(8,128)S(1)} %slice_add_fusion.1), channel_id=1, source_target_pairs={{0,2},{1,3},{2,4},{3,5},{4,6},{5,7},{6,0},{7,1},{8,10},{9,11},{10,... | collective-permute-start | bytes 884744 | tf_op jit(solution)/shard_map/ppermute | solution.py:788
  153.3 13.0 %copy-start = (f32[128,1152]{1,0:T(8,128)S(1)}, f32[128,1152]{1,0:T(8,128)}, u32[]{:S(2)}) copy-start(f32[128,1152]{1,0:T(8,128)} %get-tuple-element.12) | copy-start | bytes 1769476
  153.3 13.0 %copy-start.1 = (bf16[128,1152]{1,0:T(8,128)(2,1)S(1)}, bf16[128,1152]{1,0:T(8,128)(2,1)}, u32[]{:S(2)}) copy-start(bf16[128,1152]{1,0:T(8,128)(2,1)} %get-tuple-element.11) | copy-start | bytes 884740
